TPU v7x, 32 devices: a whole 2x2x4 slice. The times are simulated.
32 devices in a mesh: seq: 16 (over z, x, core), head: 2 (over y).
Axes of the slice: x: 2, y: 2, z: 4, core: 2. Of those that a mesh axis runs over, the one named last changes fastest.
Arguments:
- hidden: bfloat16 [4608, 8192], P('seq'), may hold values from -6 to 6
- norm_gain: bfloat16 [8192], replicated, may hold values from 0.099609375 to 1.8984375
- w_query: bfloat16 [8192, 1024], P('seq', 'head'), may hold values from -0.125 to 0.125
- w_key: bfloat16 [8192, 256], P('seq', 'head'), may hold values from -0.125 to 0.125
- w_value: bfloat16 [8192, 256], P('seq', 'head'), may hold values from -0.0625 to 0.0625
- bias_query: bfloat16 [1024], P('head'), may hold values from -3 to 3
- bias_key: bfloat16 [256], P('head'), may hold values from -200 to 200
- bias_value: bfloat16 [256], P('head'), may hold values from -3 to 3
- w_out: bfloat16 [1024, 8192], P('head', 'seq'), may hold values from -0.1875 to 0.1875
Outputs:
- attn_out: bfloat16 [4608, 8192], P(('seq', 'head'))
All inputs are finite; a program needn't handle non-finite values.
Results may differ from a plain program's by a relative error of at most 0.014.
The roundings to bfloat16 on the way count: a program that leaves them out, or rounds other values in their place, can miss the bound.
Values may be sent and summed in bfloat16 or wider, within the bound.
No kernel may reach another device: no remote copies, remote signals or barrier semaphores. Data moves between devices by JAX's collectives and lax.ppermute only.
A program may use at most 192 MiB of HBM per device.

v0:
```python
import functools

import jax
import jax.numpy as jnp
from jax import lax
from jax.experimental import pallas as pl
from jax.experimental.pallas import tpu as pltpu
from jax.sharding import PartitionSpec as P

HEAD_DIM = 128
ROPE_BASE = 1000000.0
EPSILON = 1e-06
LOG2E = 1.4426950408889634


VMEM = pl.BlockSpec(memory_space=pltpu.VMEM)
SMEM = pl.BlockSpec(memory_space=pltpu.SMEM)
HBM = pl.BlockSpec(memory_space=pltpu.HBM)


GRANT = pltpu.CompilerParams(vmem_limit_bytes=28 << 20)


def estimate(microseconds):
    return pl.CostEstimate(
        flops=microseconds * 10**9, bytes_accessed=10**6, transcendentals=0
    )


def dot(a, b, dims=((1,), (0,))):
    return lax.dot_general(a, b, (dims, ((), ())), preferred_element_type=jnp.float32)


def ring_place(seq_size, shard):
    rows = seq_size // 4
    chip = shard // 2
    return jnp.where(chip % 2 == 0, chip // 2, 2 * rows - 1 - chip // 2)


def ring_chip(seq_size, place):
    rows = seq_size // 4
    if place < rows:
        return 2 * place
    return 2 * (2 * rows - 1 - place) + 1


def ring_perm(seq_size, turn):
    chips = seq_size // 2
    pairs = []
    for place in range(chips):
        here = ring_chip(seq_size, place) * 2
        pairs.append((here, ring_chip(seq_size, (place + turn) % chips) * 2))
        pairs.append((here + 1, ring_chip(seq_size, (place - turn) % chips) * 2 + 1))
    return pairs


def slot_shards(seq_size, shard, turn=1):
    chips = seq_size // 2
    rows = seq_size // 4
    place = ring_place(seq_size, shard)
    core = shard % 2
    out = []
    for which in (core, 1 - core):
        way = jnp.where(which == 0, -turn, turn)
        for step in range(chips // 2 + 1):
            at = (place + way * step) % chips
            chip = jnp.where(at < rows, 2 * at, 2 * (2 * rows - 1 - at) + 1)
            out.append(chip * 2 + which)
            if 0 < step < chips // 2:
                out.append(chip * 2 + 1 - which)
    return out


def swap_core(value, seq_size):
    return lax.ppermute(value, "seq", [(s, s ^ 1) for s in range(seq_size)])


def swap_head(value):
    return lax.ppermute(value, "head", [(0, 1), (1, 0)])


def swap_both(value, seq_size):
    pairs = [(i, (((i // 2) ^ 1) * 2) + (1 - i % 2)) for i in range(2 * seq_size)]
    return lax.ppermute(value, ("seq", "head"), pairs)


def pass_on(value, seq_size, turn):
    return lax.ppermute(value, "seq", ring_perm(seq_size, turn))


def ring_gather(own, other, seq_size, turn=1):
    half = seq_size // 4
    held = [own]
    first, second = own, other
    for step in range(1, half + 1):
        first = pass_on(first, seq_size, turn)
        held.append(first)
        if step < half:
            second = pass_on(second, seq_size, turn)
            held.append(second)
    return held


def norm_kernel(table, hidden, gain, mine, other):
    slots, rows, depth = mine.shape
    width = hidden.shape[1]

    def columns_of(index):
        return pl.ds(pl.multiple_of(index * depth, depth), depth)

    def square(index, squares):
        part = hidden[:, columns_of(index)].astype(jnp.float32)
        part = part * part
        for lane in range(0, depth, 128):
            squares = squares + part[:, lane : lane + 128]
        return squares

    squares = jnp.zeros((rows, 128), jnp.float32)
    squares = lax.fori_loop(0, width // depth, square, squares)
    mean = jnp.sum(squares, axis=1, keepdims=True) * (1.0 / width)
    inverse = lax.rsqrt(mean + EPSILON)
    for start, target in ((0, mine), (slots, other)):

        @pl.loop(0, slots)
        def _(slot, start=start, target=target):
            columns = columns_of(table[start + slot])
            value = hidden[:, columns].astype(jnp.float32) * inverse
            value = value * gain[:, columns].astype(jnp.float32)
            target[slot] = value.astype(jnp.bfloat16)


def norm(table, hidden, gain, slots, depth):
    rows = hidden.shape[0]
    shape = jax.ShapeDtypeStruct((slots, rows, depth), jnp.bfloat16)
    return pl.pallas_call(
        norm_kernel,
        out_shape=(shape, shape),
        in_specs=[SMEM, VMEM, VMEM],
        out_specs=(VMEM, VMEM),
        compiler_params=GRANT,
        cost_estimate=estimate(4),
        name="norm",
    )(table, hidden, gain)


def project_kernel(start, count, mine, other, *refs):
    weights = refs[:count]
    keep, send = refs[-2:]
    carried = refs[count:-2]
    for source, target, old in zip(
        (other, mine), (send, keep), carried[::-1] or (None, None)
    ):
        total = None if old is None else old[...]
        for slot in range(count):
            term = dot(source[start + slot], weights[slot][...])
            total = term if total is None else total + term
        target[...] = total


def project(mine, other, weights, start, carried):
    count = len(weights)
    shape = (mine.shape[1], weights[0].shape[1])
    shape = jax.ShapeDtypeStruct(shape, jnp.float32)
    return pl.pallas_call(
        functools.partial(project_kernel, start, count),
        out_shape=(shape, shape),
        in_specs=[VMEM] * (2 + count + len(carried)),
        out_specs=(VMEM, VMEM),
        compiler_params=GRANT,
        cost_estimate=estimate(4),
    )(mine, other, *weights, *carried)


def rotated(value, cosine, sine):
    return value * cosine + pltpu.roll(value, HEAD_DIM // 2, 1) * sine


def keys_values_kernel(keep, got, bias, cosine, sine, out):
    total = keep[...] + got[...] + bias[...]
    out[:, :HEAD_DIM] = rotated(total[:, :HEAD_DIM], cosine[...], sine[...]).astype(
        jnp.bfloat16
    )
    out[:, HEAD_DIM:] = total[:, HEAD_DIM:].astype(jnp.bfloat16)


def keys_values(keep, got, bias, cosine, sine):
    return pl.pallas_call(
        keys_values_kernel,
        out_shape=jax.ShapeDtypeStruct(keep.shape, jnp.bfloat16),
        in_specs=[VMEM] * 5,
        out_specs=VMEM,
        compiler_params=GRANT,
        cost_estimate=estimate(1),
        name="kv",
    )(keep, got, bias, cosine, sine)


def query_kernel(keep, got, bias, cosine, sine, out):
    parts = []
    for column in range(0, keep.shape[1], HEAD_DIM):
        span = slice(column, column + HEAD_DIM)
        value = keep[:, span] + got[:, span] + bias[:, span]
        parts.append(rotated(value, cosine[...], sine[...]))
    out[...] = jnp.concatenate(parts, axis=0).T.astype(jnp.bfloat16)


def queries(keep, got, bias, cosine, sine):
    rows, columns = keep.shape
    shape = (HEAD_DIM, rows * columns // HEAD_DIM)
    return pl.pallas_call(
        query_kernel,
        out_shape=jax.ShapeDtypeStruct(shape, jnp.bfloat16),
        in_specs=[VMEM] * 5,
        out_specs=VMEM,
        compiler_params=GRANT,
        cost_estimate=estimate(2),
        name="qs",
    )(keep, got, bias, cosine, sine)


def attend_kernel(first, count, offset, table, query, *refs):
    inputs = len(refs) - (7 if first else 8)
    carried = () if first else refs[inputs - 3 : inputs]
    sources = refs[: inputs - (0 if first else 3)]
    if first:
        high, weight, mixture = refs[inputs : inputs + 3]
        pairs, sems, even, odd = refs[inputs + 3 :]
    else:
        out = refs[inputs]
        pairs, sems, even, odd, high, weight, mixture = refs[inputs + 1 :]
    rows, _ = sources[0].shape[-2:]
    lanes = query.shape[1]
    shard = table[0]
    factor = HEAD_DIM ** (-0.5) * LOG2E

    def copy(slot, at):
        pltpu.make_async_copy(sources[slot], pairs.at[at], sems.at[at]).start()

    def wait(at):
        pltpu.make_async_copy(pairs.at[at], pairs.at[at], sems.at[at]).wait()

    start = 1 if first else 0
    if first:
        copy(0, 0)
    needed = jnp.int32(0)
    for slot in range(start, count):
        seen = table[offset + slot] < shard

        @pl.when(seen)
        def _(slot=slot, needed=needed):
            copy(slot, needed + start)

        needed = needed + seen.astype(jnp.int32)
    for new, old in zip((high, weight, mixture), carried):
        new[...] = old[...]

    def keys_of(at, size):
        return pairs[pl.ds(at, size), :, :HEAD_DIM].reshape(size * rows, HEAD_DIM)

    def values_of(at, size):
        return pairs[pl.ds(at, size), :, HEAD_DIM:].reshape(size * rows, HEAD_DIM).T

    def update(scores, values, fresh):
        top = jnp.max(scores, axis=0, keepdims=True)
        if not fresh:
            top = jnp.maximum(top, high[...])
        probs = jnp.exp2((scores - top) * factor)
        added = jnp.sum(probs, axis=0, keepdims=True)
        mixed = dot(values, probs.astype(jnp.bfloat16))
        if not fresh:
            scale = jnp.exp2((high[...] - top) * factor)
            added = added + weight[...] * scale
            mixed = mixed + mixture[...] * scale
        high[...] = top
        weight[...] = added
        mixture[...] = mixed

    if first:
        wait(0)
        scores = dot(keys_of(0, 1), query[...])
        row = lax.broadcasted_iota(jnp.int32, scores.shape, 0)
        lane = lax.rem(lax.broadcasted_iota(jnp.int32, (1, lanes), 1), rows)
        update(jnp.where(row <= lane, scores, -jnp.inf), values_of(0, 1), True)

    single = lax.rem(needed, 2)

    @pl.when(single == 1)
    def _():
        wait(start)
        update(dot(keys_of(start, 1), query[...]), values_of(start, 1), False)

    begin = start + single
    turns = needed // 2

    def arrive(turn):
        wait(begin + 2 * turn)
        wait(begin + 2 * turn + 1)

    def step(turn, here, there):
        @pl.when(turn + 1 < turns)
        def _():
            arrive(turn + 1)

        at = begin + 2 * jnp.minimum(turn + 1, turns - 1)
        there[...] = dot(keys_of(at, 2), query[...])
        update(here[...], values_of(begin + 2 * turn, 2), False)

    @pl.when(turns > 0)
    def _():
        arrive(0)
        even[...] = dot(keys_of(begin, 2), query[...])

        @pl.loop(0, (turns + 1) // 2)
        def _(index):
            step(2 * index, even, odd)

            @pl.when(2 * index + 1 < turns)
            def _():
                step(2 * index + 1, odd, even)

    if not first:
        value = (mixture[...] / weight[...]).T
        for head in range(lanes // rows):
            out[:, head * HEAD_DIM : (head + 1) * HEAD_DIM] = value[
                head * rows : (head + 1) * rows
            ].astype(jnp.bfloat16)


def attend(table, query, sources, offset, carried):
    count = len(sources)
    lanes = query.shape[1]
    rows = sources[0].shape[-2]
    first = not carried
    state = [
        ((1, lanes), jnp.float32),
        ((1, lanes), jnp.float32),
        ((HEAD_DIM, lanes), jnp.float32),
    ]
    if first:
        out_shape = tuple(jax.ShapeDtypeStruct(*one) for one in state)
        out_specs = (VMEM,) * 3
    else:
        out_shape = jax.ShapeDtypeStruct((rows, lanes // rows * HEAD_DIM), jnp.bfloat16)
        out_specs = VMEM
    scratch = [
        pltpu.VMEM((count, rows, 2 * HEAD_DIM), jnp.bfloat16),
        pltpu.SemaphoreType.DMA((count,)),
        pltpu.VMEM((2 * rows, lanes), jnp.float32),
        pltpu.VMEM((2 * rows, lanes), jnp.float32),
    ]
    if not first:
        scratch += [pltpu.VMEM(*one) for one in state]
    return pl.pallas_call(
        functools.partial(attend_kernel, first, count, offset),
        out_shape=out_shape,
        in_specs=[SMEM, VMEM] + [HBM] * len(sources) + [VMEM] * len(carried),
        out_specs=out_specs,
        scratch_shapes=scratch,
        compiler_params=GRANT,
        cost_estimate=estimate(8),
    )(table, query, *sources, *carried)


def out_kernel(pieces, place, mine, across, mine_other, across_other, *refs):
    weights = refs[:pieces]
    keep, keep_other, send, send_other, source, block, sems, weight_sems = refs[pieces:]
    rows = mine.shape[0] // 2
    depth = mine.shape[1]
    half = place[0]
    near = pl.ds(pl.multiple_of(half * rows, 16), rows)
    far = pl.ds(pl.multiple_of((1 - half) * rows, 16), rows)
    copies = []
    for group, (own, other) in enumerate(((mine, mine_other), (across, across_other))):
        for part, (ref, span) in enumerate(
            ((own, near), (other, near), (own, far), (other, far))
        ):
            copies.append(
                pltpu.make_async_copy(
                    ref.at[span],
                    source.at[group, pl.ds(part * rows, rows)],
                    sems.at[group, part],
                )
            )
    for copy in copies:
        copy.start()
    for piece in range(pieces):
        pltpu.make_async_copy(
            weights[piece], block.at[piece], weight_sems.at[piece]
        ).start()
    for copy in copies:
        copy.wait()

    @pl.loop(0, pieces)
    def _(piece):
        pltpu.make_async_copy(
            block.at[piece], block.at[piece], weight_sems.at[piece]
        ).wait()
        one = dot(source[0], block[piece, :depth]).astype(jnp.bfloat16)
        two = dot(source[1], block[piece, depth:]).astype(jnp.bfloat16)
        value = (one.astype(jnp.float32) + two.astype(jnp.float32)).astype(jnp.bfloat16)
        for part, target in enumerate((keep, keep_other, send, send_other)):
            target[piece] = value[part * rows : (part + 1) * rows]


def project_out(place, attended, weights):
    pieces = len(weights)
    rows, depth = attended[0].shape
    columns = weights[0].shape[1]
    shape = jax.ShapeDtypeStruct((pieces, rows // 2, columns), jnp.bfloat16)
    return pl.pallas_call(
        functools.partial(out_kernel, pieces),
        out_shape=(shape,) * 4,
        in_specs=[SMEM] + [HBM] * (4 + pieces),
        out_specs=(VMEM,) * 4,
        scratch_shapes=[
            pltpu.VMEM((2, 2 * rows, depth), jnp.bfloat16),
            pltpu.VMEM((pieces, 2 * depth, columns), jnp.bfloat16),
            pltpu.SemaphoreType.DMA((2, 4)),
            pltpu.SemaphoreType.DMA((pieces,)),
        ],
        compiler_params=GRANT,
        cost_estimate=estimate(3),
    )(place, *attended, *weights)


def place_kernel(start, slots, width, table, place, *refs):
    keep, got, other, across = refs[:4]
    out, sems = refs[-2:]
    pieces, _, columns = keep.shape
    half = place[0]
    copies = []
    for piece in range(pieces):
        here = table[start + piece] * width
        there = table[slots + start + piece] * width
        for index, (value, base, side) in enumerate(
            (
                (keep, here, half),
                (got, here, 1 - half),
                (other, there, half),
                (across, there, 1 - half),
            )
        ):
            at = pl.multiple_of(base + side * columns, columns)
            copies.append(
                pltpu.make_async_copy(
                    value.at[piece], out.at[:, pl.ds(at, columns)], sems.at[index, piece]
                )
            )
    for copy in copies:
        copy.start()
    for copy in copies:
        copy.wait()


def place_part(table, place, parts, start, slots, width, whole):
    pieces, rows, columns = parts[0].shape
    extra = [] if whole is None else [whole]
    return pl.pallas_call(
        functools.partial(place_kernel, start, slots, width),
        out_shape=jax.ShapeDtypeStruct((rows, 4 * slots * columns), jnp.bfloat16),
        in_specs=[SMEM, SMEM] + [VMEM] * 4 + [HBM] * len(extra),
        out_specs=HBM,
        scratch_shapes=[pltpu.SemaphoreType.DMA((4, pieces))],
        input_output_aliases={6: 0} if extra else {},
        compiler_params=GRANT,
        cost_estimate=estimate(1),
    )(table, place, *parts, *extra)


def fast(
    seq_size, hidden, norm_gain, w_query, w_key, w_value, bias_query, bias_key,
    bias_value, w_out,
):
    rows, width = hidden.shape
    depth = w_query.shape[0]
    slots = seq_size // 2
    shard = lax.axis_index("seq")
    side = lax.axis_index("head")
    table = jnp.stack(slot_shards(seq_size, shard) + slot_shards(seq_size, shard, -1))
    place = jnp.reshape(side, (1,)).astype(jnp.int32)

    w_kv = jnp.concatenate([w_key, w_value], axis=1)
    w_kv_other = swap_core(w_kv, seq_size)
    kv_weights = ring_gather(w_kv, w_kv_other, seq_size)
    mine, for_other = norm(table, hidden, norm_gain.reshape(1, width), slots, depth)
    positions = shard * rows + jnp.arange(rows, dtype=jnp.int32)
    half_dim = HEAD_DIM // 2
    freq = ROPE_BASE ** (-2.0 * jnp.arange(half_dim, dtype=jnp.float32) / HEAD_DIM)
    angles = positions.astype(jnp.float32)[:, None] * freq[None, :]
    cosine = jnp.cos(angles)
    sine = jnp.sin(angles)
    cosine = jnp.concatenate([cosine, cosine], axis=1)
    sine = jnp.concatenate([-sine, sine], axis=1)

    bias_kv = jnp.concatenate([bias_key, bias_value]).astype(jnp.float32)[None]
    bias_query = bias_query.astype(jnp.float32)[None]
    for_other, cosine, sine, bias_kv, bias_query = lax.optimization_barrier(
        (for_other, cosine, sine, bias_kv, bias_query)
    )
    other = swap_core(for_other, seq_size)

    keep, send = project(mine, other, kv_weights, 0, ())
    got = swap_core(send, seq_size)
    own_kv = keys_values(keep, got, bias_kv, cosine, sine)
    other_kv = swap_core(own_kv, seq_size)
    held = ring_gather(own_kv, other_kv, seq_size, -1)
    swapped = [other_kv]
    for one in held[1:]:
        swapped.append(swap_core(one, seq_size))

    w_query_other = swap_core(w_query, seq_size)
    q_weights = ring_gather(w_query, w_query_other, seq_size)
    early = slots - 3
    sums = project(mine, other, q_weights[:early], 0, ())
    keep, send = project(mine, other, q_weights[early:], early, sums)
    got = swap_core(send, seq_size)
    query = queries(keep, got, bias_query, cosine, sine)
    state = attend(table, query, held, 2 * slots, ())
    attended = attend(table, query, swapped, 3 * slots, state)

    columns = w_out.shape[1] // 2
    near = lax.dynamic_slice_in_dim(w_out, side * columns, columns, 1)
    far = lax.dynamic_slice_in_dim(w_out, (1 - side) * columns, columns, 1)
    far = swap_head(far)
    piece = jnp.concatenate([near, far])
    piece_other = swap_core(piece, seq_size)
    out_weights = ring_gather(piece, piece_other, seq_size)

    across = swap_head(attended)
    attended_other = swap_core(attended, seq_size)
    across_other = swap_core(across, seq_size)
    operands = (attended, across, attended_other, across_other)
    whole = None
    start = 0
    for count in (slots - 3, 3):
        keep, keep_other, send, send_other = project_out(
            place, operands, out_weights[start : start + count]
        )
        got = swap_head(send)
        got_other = swap_both(send_other, seq_size)
        kept_other = swap_core(keep_other, seq_size)
        whole = place_part(
            table, place, (keep, got, kept_other, got_other), start, slots,
            w_out.shape[1], whole,
        )
        start += count
    return whole


def rotary(values, positions):
    half_dim = values.shape[-1] // 2
    freq = ROPE_BASE ** (-2.0 * jnp.arange(half_dim, dtype=jnp.float32) / values.shape[-1])
    angles = positions.astype(jnp.float32)[:, None, None] * freq[None, None, :]
    cosine = jnp.cos(angles)
    sine = jnp.sin(angles)
    first = values[..., :half_dim]
    second = values[..., half_dim:]
    return jnp.concatenate(
        [first * cosine - second * sine, second * cosine + first * sine], axis=-1
    )


def plain(hidden, norm_gain, w_query, w_key, w_value, bias_query, bias_key, bias_value, w_out):
    rows = hidden.shape[0]
    heads = w_query.shape[1] // HEAD_DIM
    positions = lax.axis_index("seq") * rows + jnp.arange(rows, dtype=jnp.int32)
    widened = hidden.astype(jnp.float32)
    inverse = lax.rsqrt(jnp.mean(widened * widened, axis=-1, keepdims=True) + EPSILON)
    normed = (widened * inverse * norm_gain.astype(jnp.float32)).astype(jnp.bfloat16)
    weights = jnp.concatenate([w_query, w_key, w_value], axis=1)
    biases = jnp.concatenate([bias_query, bias_key, bias_value]).astype(jnp.float32)
    weights = lax.all_gather(weights, "seq", axis=0, tiled=True)
    qkv = jnp.dot(normed, weights, preferred_element_type=jnp.float32) + biases
    query, keys, values = jnp.split(
        qkv, [heads * HEAD_DIM, (heads + 1) * HEAD_DIM], axis=1
    )
    query = rotary(query.reshape(rows, heads, HEAD_DIM), positions).astype(jnp.bfloat16)
    keys = rotary(keys.reshape(rows, 1, HEAD_DIM), positions).reshape(rows, HEAD_DIM)
    pair = jnp.concatenate([keys, values], axis=1).astype(jnp.bfloat16)
    pair = lax.all_gather(pair, "seq", axis=0, tiled=True)
    scores = jnp.einsum(
        "qhd,kd->hqk", query, pair[:, :HEAD_DIM], preferred_element_type=jnp.float32
    )
    allowed = positions[:, None] >= jnp.arange(pair.shape[0], dtype=jnp.int32)[None, :]
    scores = jnp.where(allowed[None], scores * HEAD_DIM ** (-0.5), -jnp.inf)
    probs = jnp.exp(scores - jnp.max(scores, axis=-1, keepdims=True))
    total = jnp.sum(probs, axis=-1, keepdims=True)
    mixed = jnp.einsum(
        "hqk,kd->hqd",
        probs.astype(jnp.bfloat16),
        pair[:, HEAD_DIM:],
        preferred_element_type=jnp.float32,
    )
    attended = (mixed / total).astype(jnp.bfloat16)
    attended = attended.transpose(1, 0, 2).reshape(rows, heads * HEAD_DIM)
    partial_out = jnp.dot(
        attended,
        lax.all_gather(w_out, "seq", axis=1, tiled=True),
        preferred_element_type=jnp.float32,
    )
    return lax.psum_scatter(
        partial_out.astype(jnp.bfloat16), "head", scatter_dimension=0, tiled=True
    )


def local(seq_size, head_size, *args):
    hidden, w_query, w_out = args[0], args[2], args[8]
    fits = (
        head_size == 2
        and seq_size % 4 == 0
        and seq_size >= 8
        and hidden.shape[0] % 32 == 0
        and w_query.shape[0] % 128 == 0
        and w_out.shape[1] % 256 == 0
    )
    if fits:
        return fast(seq_size, *args)
    return plain(*args)


def solution(mesh):
    in_specs = (
        P("seq", None),
        P(),
        P("seq", "head"),
        P("seq", "head"),
        P("seq", "head"),
        P("head"),
        P("head"),
        P("head"),
        P("head", "seq"),
    )
    out_specs = P(("seq", "head"), None)
    body = functools.partial(local, mesh.shape["seq"], mesh.shape["head"])
    return jax.shard_map(
        body, mesh=mesh, in_specs=in_specs, out_specs=out_specs, check_vma=False
    )
```

profile of v0, /device:TPU:0, one launch (start us, length us, event | category | flops | bytes accessed | tf_op | source)
XLA Modules:
  0.0 174.4 jit_solution(7266009748768165814)
XLA Ops:
  3.6 2.3 %copy-done = bf16[288,8192]{1,0:T(8,128)(2,1)S(1)} copy-done((bf16[288,8192]{1,0:T(8,128)(2,1)S(1)}, bf16[288,8192]{1,0:T(8,128)(2,1)}, u32[]{:S(2)}) %copy-start) | copy-done | bytes 4718616
  5.9 4.8 %norm.1 = (bf16[8,288,512]{2,1,0:T(8,128)(2,1)S(1)}, bf16[8,288,512]{2,1,0:T(8,128)(2,1)}) custom-call(s32[32]{0:T(128)S(1)} %stack.125.table, bf16[288,8192]{1,0:T(8,128)(2,1)S(1)} %copy-done, bf16[1,8192]{1,0:T(2,128)(2,1)S(1)} %reshape.46.gain), custom_call_target="tpu_custom_call" | custom-call | flops 4000000000 | bytes 1000000 | tf_op jit(solution)/shard_map/norm/pallas_call | solution.py:135
  12.9 3.0 %collective-permute-start.1 = (bf16[512,512]{1,0:T(8,128)(2,1)S(1)}, bf16[512,512]{1,0:T(8,128)(2,1)}, u32[]{:S(2)}, u32[]{:S(2)}) collective-permute-start(bf16[512,512]{1,0:T(8,128)(2,1)S(1)} %copy-done.1), channel_id=1, source_target_pairs={{0,8},{2,6},{8,16},{10,2},{16,24},{18,10},{24,28},{26,18},{28,20},... | collective-permute-start | bytes 1572872 | tf_op jit(solution)/shard_map/ppermute | solution.py:88
  16.0 1.6 collective-permute-start.10
  18.7 7.2 %collective-permute-done.10.refs_1_ = bf16[512,256]{1,0:T(8,128)(2,1)} collective-permute-done((bf16[512,256]{1,0:T(8,128)(2,1)S(1)}, bf16[512,256]{1,0:T(8,128)(2,1)}, u32[]{:S(2)}, u32[]{:S(2)}) %collective-permute-start.10) | collective-permute-done | bytes 262176 | tf_op jit(solution)/shard_map/ppermute | solution.py:88
  25.9 2.1 %collective-permute-start.37 = (bf16[512,256]{1,0:T(8,128)(2,1)S(1)}, bf16[512,256]{1,0:T(8,128)(2,1)S(1)}, u32[]{:S(2)}, u32[]{:S(2)}) collective-permute-start(bf16[512,256]{1,0:T(8,128)(2,1)S(1)} %get-tuple-element.54), channel_id=1, source_target_pairs={{0,1},{1,0},{2,3},{3,2},{4,5},{5,4},{6,7},{7,6},{8,9},{9,8},{10,11... | collective-permute-start | bytes 786440 | tf_op jit(solution)/shard_map/ppermute | solution.py:79
  28.0 1.6 collective-permute-start.5
  29.6 1.6 collective-permute-start.2
  31.1 1.6 collective-permute-start.12
  33.7 1.7 collective-permute-start.13
  35.5 10.3 %collective-permute-done.12.refs_2_ = bf16[512,256]{1,0:T(8,128)(2,1)S(1)} collective-permute-done((bf16[512,256]{1,0:T(8,128)(2,1)}, bf16[512,256]{1,0:T(8,128)(2,1)S(1)}, u32[]{:S(2)}, u32[]{:S(2)}) %collective-permute-start.12) | collective-permute-done | bytes 262176 | tf_op jit(solution)/shard_map/ppermute | solution.py:88
  45.8 1.6 collective-permute-start.14
  48.6 1.6 collective-permute-start.15
  50.2 1.6 collective-permute-start.6
  51.8 1.6 collective-permute-start.3
  55.0 1.6 collective-permute-start.17
  56.6 12.4 %collective-permute-done.16.refs_6_ = bf16[512,256]{1,0:T(8,128)(2,1)S(1)} collective-permute-done((bf16[512,256]{1,0:T(8,128)(2,1)S(1)}, bf16[512,256]{1,0:T(8,128)(2,1)S(1)}, u32[]{:S(2)}, u32[]{:S(2)}) %collective-permute-start.16) | collective-permute-done | bytes 262176 | tf_op jit(solution)/shard_map/ppermute | solution.py:88
  69.0 1.6 collective-permute-start.38
  71.8 1.6 collective-permute-start.7
  73.4 1.6 collective-permute-start.8
  75.0 1.7 copy-done.3
  76.7 2.3 %shard_map.93 = (f32[288,256]{1,0:T(8,128)S(1)}, f32[288,256]{1,0:T(8,128)S(1)}) custom-call(bf16[8,288,512]{2,1,0:T(8,128)(2,1)S(1)} %copy-done.3, bf16[8,288,512]{2,1,0:T(8,128)(2,1)S(1)} %collective-permute-done.other, bf16[512,256]{1,0:T(8,128)(2,1)S(1)} %constant_dynamic-update-slice_fusion.refs_0_, bf16[512,256]{1,0:T(8,128)(2,1)} %collective-permute-done.10.refs_1_, ...), custom_call_target="tpu_custom_call" | custom-call | flops 4000000000 | bytes 1000000 | tf_op jit(solution)/shard_map/pallas_call | solution.py:164
  79.1 2.7 %shard_map.91 = (f32[288,512]{1,0:T(8,128)S(1)}, f32[288,512]{1,0:T(8,128)S(1)}) custom-call(bf16[8,288,512]{2,1,0:T(8,128)(2,1)S(1)} %copy-done.3, bf16[8,288,512]{2,1,0:T(8,128)(2,1)S(1)} %collective-permute-done.other, bf16[512,512]{1,0:T(8,128)(2,1)S(1)} %copy-done.1, bf16[512,512]{1,0:T(8,128)(2,1)} %collective-permute-done.1.refs_1_, ...), custom_call_target="tpu_custom_call" | custom-call | flops 4000000000 | bytes 1000000 | tf_op jit(solution)/shard_map/pallas_call | solution.py:164
  81.8 2.0 %collective-permute-done.7.refs_1_ = bf16[512,512]{1,0:T(8,128)(2,1)S(1)} collective-permute-done((bf16[512,512]{1,0:T(8,128)(2,1)S(1)}, bf16[512,512]{1,0:T(8,128)(2,1)S(1)}, u32[]{:S(2)}, u32[]{:S(2)}) %collective-permute-start.7) | collective-permute-done | bytes 524320 | tf_op jit(solution)/shard_map/ppermute | solution.py:88
  83.8 5.6 %collective-permute-done.8.refs_2_ = bf16[512,512]{1,0:T(8,128)(2,1)S(1)} collective-permute-done((bf16[512,512]{1,0:T(8,128)(2,1)S(1)}, bf16[512,512]{1,0:T(8,128)(2,1)S(1)}, u32[]{:S(2)}, u32[]{:S(2)}) %collective-permute-start.8) | collective-permute-done | bytes 524320 | tf_op jit(solution)/shard_map/ppermute | solution.py:88
  90.6 1.6 collective-permute-start.39
  92.5 1.6 collective-permute-start.20
  94.6 1.6 collective-permute-start.22
  96.1 3.1 %collective-permute-done.20.refs_1_ = bf16[288,256]{1,0:T(8,128)(2,1)S(1)} collective-permute-done((bf16[288,256]{1,0:T(8,128)(2,1)S(1)}, bf16[288,256]{1,0:T(8,128)(2,1)S(1)}, u32[]{:S(2)}, u32[]{:S(2)}) %collective-permute-start.20) | collective-permute-done | bytes 147488 | tf_op jit(solution)/shard_map/ppermute | solution.py:88
  99.2 1.6 collective-permute-start.24
  100.8 1.6 collective-permute-done.22.refs_2_
  104.0 2.0 %collective-permute-done.24.refs_3_ = bf16[288,256]{1,0:T(8,128)(2,1)S(1)} collective-permute-done((bf16[288,256]{1,0:T(8,128)(2,1)S(1)}, bf16[288,256]{1,0:T(8,128)(2,1)S(1)}, u32[]{:S(2)}, u32[]{:S(2)}) %collective-permute-start.24) | collective-permute-done | bytes 147488 | tf_op jit(solution)/shard_map/ppermute | solution.py:88
  110.7 2.0 %collective-permute-done.28.refs_5_ = bf16[288,256]{1,0:T(8,128)(2,1)S(1)} collective-permute-done((bf16[288,256]{1,0:T(8,128)(2,1)S(1)}, bf16[288,256]{1,0:T(8,128)(2,1)S(1)}, u32[]{:S(2)}, u32[]{:S(2)}) %collective-permute-start.28) | collective-permute-done | bytes 147488 | tf_op jit(solution)/shard_map/ppermute | solution.py:88
  117.8 1.7 shard_map.94
  119.6 1.6 collective-permute-start.40
  121.2 2.5 %collective-permute-start.43 = (bf16[1024,256]{1,0:T(8,128)(2,1)S(1)}, bf16[1024,256]{1,0:T(8,128)(2,1)S(1)}, u32[]{:S(2)}, u32[]{:S(2)}) collective-permute-start(bf16[1024,256]{1,0:T(8,128)(2,1)S(1)} %collective-permute-done.42.refs_2_), channel_id=1, source_target_pairs={{0,8},{2,6},{8,16},{10,2},{16,24},{18,10},{24,28},{26,18},{28,20},... | collective-permute-start | bytes 1572872 | tf_op jit(solution)/shard_map/ppermute | solution.py:88
  125.4 8.4 %collective-permute-done.34.across = bf16[288,512]{1,0:T(8,128)(2,1)S(1)} collective-permute-done((bf16[288,512]{1,0:T(8,128)(2,1)S(1)}, bf16[288,512]{1,0:T(8,128)(2,1)S(1)}, u32[]{:S(2)}, u32[]{:S(2)}) %collective-permute-start.34) | collective-permute-done | bytes 294944 | tf_op jit(solution)/shard_map/ppermute | solution.py:79
  133.8 2.0 %collective-permute-done.43.refs_4_ = bf16[1024,256]{1,0:T(8,128)(2,1)S(1)} collective-permute-done((bf16[1024,256]{1,0:T(8,128)(2,1)S(1)}, bf16[1024,256]{1,0:T(8,128)(2,1)S(1)}, u32[]{:S(2)}, u32[]{:S(2)}) %collective-permute-start.43) | collective-permute-done | bytes 524320 | tf_op jit(solution)/shard_map/ppermute | solution.py:88
  135.8 3.6 %collective-permute-start.44 = (bf16[1024,256]{1,0:T(8,128)(2,1)S(1)}, bf16[1024,256]{1,0:T(8,128)(2,1)S(1)}, u32[]{:S(2)}, u32[]{:S(2)}) collective-permute-start(bf16[1024,256]{1,0:T(8,128)(2,1)S(1)} %collective-permute-done.43.refs_4_), channel_id=1, source_target_pairs={{0,8},{2,6},{8,16},{10,2},{16,24},{18,10},{24,28},{26,18},{28,20},... | collective-permute-start | bytes 1572872 | tf_op jit(solution)/shard_map/ppermute | solution.py:88
  139.4 5.0 %collective-permute-start.45 = (bf16[1024,256]{1,0:T(8,128)(2,1)S(1)}, bf16[1024,256]{1,0:T(8,128)(2,1)S(1)}, u32[]{:S(2)}, u32[]{:S(2)}) collective-permute-start(bf16[1024,256]{1,0:T(8,128)(2,1)S(1)} %collective-permute-done.40.refs_0_), channel_id=1, source_target_pairs={{0,8},{2,6},{8,16},{10,2},{16,24},{18,10},{24,28},{26,18},{28,20},... | collective-permute-start | bytes 1572872 | tf_op jit(solution)/shard_map/ppermute | solution.py:88
  144.4 4.2 %shard_map.97 = (bf16[5,144,256]{2,1,0:T(8,128)(2,1)S(1)}, bf16[5,144,256]{2,1,0:T(8,128)(2,1)S(1)}, bf16[5,144,256]{2,1,0:T(8,128)(2,1)S(1)}, bf16[5,144,256]{2,1,0:T(8,128)(2,1)S(1)}) custom-call(s32[1]{0:T(128)} %bitcast.30.place, bf16[288,512]{1,0:T(8,128)(2,1)S(1)} %shard_map.95.mine, bf16[288,512]{1,0:T(8,128)(2,1)S(1)} %collective-permute-done.34.across, ...), custom_call_target="tpu_custom_call" | custom-call | flops 3000000000 | bytes 1000000 | tf_op jit(solution)/shard_map/pallas_call | solution.py:410
  149.1 1.6 collective-permute-start.51
  150.8 2.0 %collective-permute-done.45.refs_2_ = bf16[1024,256]{1,0:T(8,128)(2,1)S(1)} collective-permute-done((bf16[1024,256]{1,0:T(8,128)(2,1)S(1)}, bf16[1024,256]{1,0:T(8,128)(2,1)S(1)}, u32[]{:S(2)}, u32[]{:S(2)}) %collective-permute-start.45) | collective-permute-done | bytes 524320 | tf_op jit(solution)/shard_map/ppermute | solution.py:88
  152.8 3.1 %shard_map.96 = (bf16[3,144,256]{2,1,0:T(8,128)(2,1)S(1)}, bf16[3,144,256]{2,1,0:T(8,128)(2,1)S(1)}, bf16[3,144,256]{2,1,0:T(8,128)(2,1)S(1)}, bf16[3,144,256]{2,1,0:T(8,128)(2,1)S(1)}) custom-call(s32[1]{0:T(128)} %bitcast.30.place, bf16[288,512]{1,0:T(8,128)(2,1)S(1)} %shard_map.95.mine, bf16[288,512]{1,0:T(8,128)(2,1)S(1)} %collective-permute-done.34.across, ...), custom_call_target="tpu_custom_call" | custom-call | flops 3000000000 | bytes 1000000 | tf_op jit(solution)/shard_map/pallas_call | solution.py:410
  156.5 3.6 %collective-permute-done.49.refs_1_ = bf16[5,144,256]{2,1,0:T(8,128)(2,1)S(1)} collective-permute-done((bf16[5,144,256]{2,1,0:T(8,128)(2,1)S(1)}, bf16[5,144,256]{2,1,0:T(8,128)(2,1)S(1)}, u32[]{:S(2)}, u32[]{:S(2)}) %collective-permute-start.49) | collective-permute-done | bytes 368672 | tf_op jit(solution)/shard_map/ppermute | solution.py:79
  160.1 5.9 %collective-permute-done.51.refs_3_ = bf16[5,144,256]{2,1,0:T(8,128)(2,1)S(1)} collective-permute-done((bf16[5,144,256]{2,1,0:T(8,128)(2,1)S(1)}, bf16[5,144,256]{2,1,0:T(8,128)(2,1)S(1)}, u32[]{:S(2)}, u32[]{:S(2)}) %collective-permute-start.51) | collective-permute-done | bytes 368672 | tf_op jit(solution)/shard_map/ppermute | solution.py:84
  166.0 1.8 %shard_map.98.refs_4_ = bf16[144,8192]{1,0:T(8,128)(2,1)} custom-call(s32[32]{0:T(128)S(1)} %stack.125.table, s32[1]{0:T(128)} %bitcast.30.place, bf16[5,144,256]{2,1,0:T(8,128)(2,1)S(1)} %get-tuple-element.49.refs_0_, bf16[5,144,256]{2,1,0:T(8,128)(2,1)S(1)} %collective-permute-done.49.refs_1_, bf16[5,144,256]{2,1,0:T(8,128)(2,1)S(1)} %collective-permute-done.50.refs_2_, ...), custom_call_target="tpu_custom_call" | custom-call | flops 1000000000 | bytes 1000000 | tf_op jit(solution)/shard_map/pallas_call | solution.py:458
  167.8 4.5 %collective-permute-done.46.refs_1_ = bf16[3,144,256]{2,1,0:T(8,128)(2,1)S(1)} collective-permute-done((bf16[3,144,256]{2,1,0:T(8,128)(2,1)S(1)}, bf16[3,144,256]{2,1,0:T(8,128)(2,1)S(1)}, u32[]{:S(2)}, u32[]{:S(2)}) %collective-permute-start.46) | collective-permute-done | bytes 221216 | tf_op jit(solution)/shard_map/ppermute | solution.py:79
  (96 shorter events, 30.3 us)
Async XLA Ops:
  12.2 62.8 %collective-permute-start = (bf16[8,288,512]{2,1,0:T(8,128)(2,1)}, bf16[8,288,512]{2,1,0:T(8,128)(2,1)S(1)}, u32[]{:S(2)}, u32[]{:S(2)}) collective-permute-start(bf16[8,288,512]{2,1,0:T(8,128)(2,1)} %get-tuple-element.31), channel_id=1, source_target_pairs={{0,2},{2,0},{4,6},{6,4},{8,10},{10,8},{12,14},{14,12},{16,18},{18,... | collective-permute-start | bytes 7077896 | tf_op jit(solution)/shard_map/ppermute | solution.py:75
  12.9 15.1 %collective-permute-start.4 = (bf16[512,512]{1,0:T(8,128)(2,1)S(1)}, bf16[512,512]{1,0:T(8,128)(2,1)}, u32[]{:S(2)}, u32[]{:S(2)}) collective-permute-start(bf16[512,512]{1,0:T(8,128)(2,1)S(1)} %copy-done.1), channel_id=1, source_target_pairs={{0,2},{2,0},{4,6},{6,4},{8,10},{10,8},{12,14},{14,12},{16,18},{18,... | collective-permute-start | bytes 1572872 | tf_op jit(solution)/shard_map/ppermute | solution.py:75
  12.9 16.6 %collective-permute-start.1 = (bf16[512,512]{1,0:T(8,128)(2,1)S(1)}, bf16[512,512]{1,0:T(8,128)(2,1)}, u32[]{:S(2)}, u32[]{:S(2)}) collective-permute-start(bf16[512,512]{1,0:T(8,128)(2,1)S(1)} %copy-done.1), channel_id=1, source_target_pairs={{0,8},{2,6},{8,16},{10,2},{16,24},{18,10},{24,28},{26,18},{28,20},... | collective-permute-start | bytes 1572872 | tf_op jit(solution)/shard_map/ppermute | solution.py:88
  16.0 9.9 %collective-permute-start.10 = (bf16[512,256]{1,0:T(8,128)(2,1)S(1)}, bf16[512,256]{1,0:T(8,128)(2,1)}, u32[]{:S(2)}, u32[]{:S(2)}) collective-permute-start(bf16[512,256]{1,0:T(8,128)(2,1)S(1)} %constant_dynamic-update-slice_fusion.refs_0_), channel_id=1, source_target_pairs={{0,8},{2,6},{8,16},{10,2},{16,24},{18,10},{24,28},{26,18},{28,20},... | collective-permute-start | bytes 786440 | tf_op jit(solution)/shard_map/ppermute | solution.py:88
  17.6 13.5 %collective-permute-start.11 = (bf16[512,256]{1,0:T(8,128)(2,1)S(1)}, bf16[512,256]{1,0:T(8,128)(2,1)}, u32[]{:S(2)}, u32[]{:S(2)}) collective-permute-start(bf16[512,256]{1,0:T(8,128)(2,1)S(1)} %constant_dynamic-update-slice_fusion.refs_0_), channel_id=1, source_target_pairs={{0,2},{2,0},{4,6},{6,4},{8,10},{10,8},{12,14},{14,12},{16,18},{18,... | collective-permute-start | bytes 786440 | tf_op jit(solution)/shard_map/ppermute | solution.py:75
  25.9 7.8 %collective-permute-start.37 = (bf16[512,256]{1,0:T(8,128)(2,1)S(1)}, bf16[512,256]{1,0:T(8,128)(2,1)S(1)}, u32[]{:S(2)}, u32[]{:S(2)}) collective-permute-start(bf16[512,256]{1,0:T(8,128)(2,1)S(1)} %get-tuple-element.54), channel_id=1, source_target_pairs={{0,1},{1,0},{2,3},{3,2},{4,5},{5,4},{6,7},{7,6},{8,9},{9,8},{10,11... | collective-permute-start | bytes 786440 | tf_op jit(solution)/shard_map/ppermute | solution.py:79
  28.0 22.2 %collective-permute-start.5 = (bf16[512,512]{1,0:T(8,128)(2,1)}, bf16[512,512]{1,0:T(8,128)(2,1)S(1)}, u32[]{:S(2)}, u32[]{:S(2)}) collective-permute-start(bf16[512,512]{1,0:T(8,128)(2,1)} %collective-permute-done.4), channel_id=1, source_target_pairs={{0,8},{2,6},{8,16},{10,2},{16,24},{18,10},{24,28},{26,18},{28,20},... | collective-permute-start | bytes 1572872 | tf_op jit(solution)/shard_map/ppermute | solution.py:88
  29.6 22.2 %collective-permute-start.2 = (bf16[512,512]{1,0:T(8,128)(2,1)}, bf16[512,512]{1,0:T(8,128)(2,1)S(1)}, u32[]{:S(2)}, u32[]{:S(2)}) collective-permute-start(bf16[512,512]{1,0:T(8,128)(2,1)} %collective-permute-done.1.refs_1_), channel_id=1, source_target_pairs={{0,8},{2,6},{8,16},{10,2},{16,24},{18,10},{24,28},{26,18},{28,20},... | collective-permute-start | bytes 1572872 | tf_op jit(solution)/shard_map/ppermute | solution.py:88
  31.1 14.7 %collective-permute-start.12 = (bf16[512,256]{1,0:T(8,128)(2,1)}, bf16[512,256]{1,0:T(8,128)(2,1)S(1)}, u32[]{:S(2)}, u32[]{:S(2)}) collective-permute-start(bf16[512,256]{1,0:T(8,128)(2,1)} %collective-permute-done.11), channel_id=1, source_target_pairs={{0,8},{2,6},{8,16},{10,2},{16,24},{18,10},{24,28},{26,18},{28,20},... | collective-permute-start | bytes 786440 | tf_op jit(solution)/shard_map/ppermute | solution.py:88
  33.7 14.9 %collective-permute-start.13 = (bf16[512,256]{1,0:T(8,128)(2,1)}, bf16[512,256]{1,0:T(8,128)(2,1)S(1)}, u32[]{:S(2)}, u32[]{:S(2)}) collective-permute-start(bf16[512,256]{1,0:T(8,128)(2,1)} %collective-permute-done.10.refs_1_), channel_id=1, source_target_pairs={{0,8},{2,6},{8,16},{10,2},{16,24},{18,10},{24,28},{26,18},{28,20},... | collective-permute-start | bytes 786440 | tf_op jit(solution)/shard_map/ppermute | solution.py:88
  45.8 7.5 %collective-permute-start.14 = (bf16[512,256]{1,0:T(8,128)(2,1)S(1)}, bf16[512,256]{1,0:T(8,128)(2,1)S(1)}, u32[]{:S(2)}, u32[]{:S(2)}) collective-permute-start(bf16[512,256]{1,0:T(8,128)(2,1)S(1)} %collective-permute-done.12.refs_2_), channel_id=1, source_target_pairs={{0,8},{2,6},{8,16},{10,2},{16,24},{18,10},{24,28},{26,18},{28,20},... | collective-permute-start | bytes 786440 | tf_op jit(solution)/shard_map/ppermute | solution.py:88
  48.6 6.4 %collective-permute-start.15 = (bf16[512,256]{1,0:T(8,128)(2,1)S(1)}, bf16[512,256]{1,0:T(8,128)(2,1)S(1)}, u32[]{:S(2)}, u32[]{:S(2)}) collective-permute-start(bf16[512,256]{1,0:T(8,128)(2,1)S(1)} %collective-permute-done.13.refs_3_), channel_id=1, source_target_pairs={{0,8},{2,6},{8,16},{10,2},{16,24},{18,10},{24,28},{26,18},{28,20},... | collective-permute-start | bytes 786440 | tf_op jit(solution)/shard_map/ppermute | solution.py:88
  50.2 21.7 %collective-permute-start.6 = (bf16[512,512]{1,0:T(8,128)(2,1)S(1)}, bf16[512,512]{1,0:T(8,128)(2,1)S(1)}, u32[]{:S(2)}, u32[]{:S(2)}) collective-permute-start(bf16[512,512]{1,0:T(8,128)(2,1)S(1)} %collective-permute-done.5.refs_2_), channel_id=1, source_target_pairs={{0,8},{2,6},{8,16},{10,2},{16,24},{18,10},{24,28},{26,18},{28,20},... | collective-permute-start | bytes 1572872 | tf_op jit(solution)/shard_map/ppermute | solution.py:88
  51.8 21.7 %collective-permute-start.3 = (bf16[512,512]{1,0:T(8,128)(2,1)S(1)}, bf16[512,512]{1,0:T(8,128)(2,1)S(1)}, u32[]{:S(2)}, u32[]{:S(2)}) collective-permute-start(bf16[512,512]{1,0:T(8,128)(2,1)S(1)} %collective-permute-done.2.refs_3_), channel_id=1, source_target_pairs={{0,8},{2,6},{8,16},{10,2},{16,24},{18,10},{24,28},{26,18},{28,20},... | collective-permute-start | bytes 1572872 | tf_op jit(solution)/shard_map/ppermute | solution.py:88
  53.3 15.7 %collective-permute-start.16 = (bf16[512,256]{1,0:T(8,128)(2,1)S(1)}, bf16[512,256]{1,0:T(8,128)(2,1)S(1)}, u32[]{:S(2)}, u32[]{:S(2)}) collective-permute-start(bf16[512,256]{1,0:T(8,128)(2,1)S(1)} %collective-permute-done.14.refs_4_), channel_id=1, source_target_pairs={{0,8},{2,6},{8,16},{10,2},{16,24},{18,10},{24,28},{26,18},{28,20},... | collective-permute-start | bytes 786440 | tf_op jit(solution)/shard_map/ppermute | solution.py:88
  55.0 16.9 %collective-permute-start.17 = (bf16[512,256]{1,0:T(8,128)(2,1)S(1)}, bf16[512,256]{1,0:T(8,128)(2,1)S(1)}, u32[]{:S(2)}, u32[]{:S(2)}) collective-permute-start(bf16[512,256]{1,0:T(8,128)(2,1)S(1)} %collective-permute-done.15.refs_5_), channel_id=1, source_target_pairs={{0,8},{2,6},{8,16},{10,2},{16,24},{18,10},{24,28},{26,18},{28,20},... | collective-permute-start | bytes 786440 | tf_op jit(solution)/shard_map/ppermute | solution.py:88
  69.0 21.6 %collective-permute-start.38 = (bf16[1024,256]{1,0:T(8,128)(2,1)S(1)}, bf16[1024,256]{1,0:T(8,128)(2,1)S(1)}, u32[]{:S(2)}, u32[]{:S(2)}) collective-permute-start(bf16[1024,256]{1,0:T(8,128)(2,1)S(1)} %pad_maximum_fusion.refs_0_), channel_id=1, source_target_pairs={{0,8},{2,6},{8,16},{10,2},{16,24},{18,10},{24,28},{26,18},{28,20},... | collective-permute-start | bytes 1572872 | tf_op jit(solution)/shard_map/ppermute | solution.py:88
  71.8 22.3 %collective-permute-start.41 = (bf16[1024,256]{1,0:T(8,128)(2,1)S(1)}, bf16[1024,256]{1,0:T(8,128)(2,1)S(1)}, u32[]{:S(2)}, u32[]{:S(2)}) collective-permute-start(bf16[1024,256]{1,0:T(8,128)(2,1)S(1)} %pad_maximum_fusion.refs_0_), channel_id=1, source_target_pairs={{0,2},{2,0},{4,6},{6,4},{8,10},{10,8},{12,14},{14,12},{16,18},{18,... | collective-permute-start | bytes 1572872 | tf_op jit(solution)/shard_map/ppermute | solution.py:75
  71.8 12.0 %collective-permute-start.7 = (bf16[512,512]{1,0:T(8,128)(2,1)S(1)}, bf16[512,512]{1,0:T(8,128)(2,1)S(1)}, u32[]{:S(2)}, u32[]{:S(2)}) collective-permute-start(bf16[512,512]{1,0:T(8,128)(2,1)S(1)} %collective-permute-done.6.refs_4_), channel_id=1, source_target_pairs={{0,8},{2,6},{8,16},{10,2},{16,24},{18,10},{24,28},{26,18},{28,20},... | collective-permute-start | bytes 1572872 | tf_op jit(solution)/shard_map/ppermute | solution.py:88
  73.4 16.0 %collective-permute-start.8 = (bf16[512,512]{1,0:T(8,128)(2,1)S(1)}, bf16[512,512]{1,0:T(8,128)(2,1)S(1)}, u32[]{:S(2)}, u32[]{:S(2)}) collective-permute-start(bf16[512,512]{1,0:T(8,128)(2,1)S(1)} %collective-permute-done.3.refs_0_), channel_id=1, source_target_pairs={{0,8},{2,6},{8,16},{10,2},{16,24},{18,10},{24,28},{26,18},{28,20},... | collective-permute-start | bytes 1572872 | tf_op jit(solution)/shard_map/ppermute | solution.py:88
  79.0 13.2 %collective-permute-start.18 = (f32[288,256]{1,0:T(8,128)S(1)}, f32[288,256]{1,0:T(8,128)S(1)}, u32[]{:S(2)}, u32[]{:S(2)}) collective-permute-start(f32[288,256]{1,0:T(8,128)S(1)} %get-tuple-element.40), channel_id=1, source_target_pairs={{0,2},{2,0},{4,6},{6,4},{8,10},{10,8},{12,14},{14,12},{16,18},{18,... | collective-permute-start | bytes 884744 | tf_op jit(solution)/shard_map/ppermute | solution.py:75
  90.5 17.0 %collective-permute-start.9 = (f32[288,512]{1,0:T(8,128)S(1)}, f32[288,512]{1,0:T(8,128)S(1)}, u32[]{:S(2)}, u32[]{:S(2)}) collective-permute-start(f32[288,512]{1,0:T(8,128)S(1)} %get-tuple-element.35), channel_id=1, source_target_pairs={{0,2},{2,0},{4,6},{6,4},{8,10},{10,8},{12,14},{14,12},{16,18},{18,... | collective-permute-start | bytes 1769480 | tf_op jit(solution)/shard_map/ppermute | solution.py:75
  90.6 16.9 %collective-permute-start.39 = (bf16[1024,256]{1,0:T(8,128)(2,1)S(1)}, bf16[1024,256]{1,0:T(8,128)(2,1)S(1)}, u32[]{:S(2)}, u32[]{:S(2)}) collective-permute-start(bf16[1024,256]{1,0:T(8,128)(2,1)S(1)} %collective-permute-done.38.refs_1_), channel_id=1, source_target_pairs={{0,8},{2,6},{8,16},{10,2},{16,24},{18,10},{24,28},{26,18},{28,20},... | collective-permute-start | bytes 1572872 | tf_op jit(solution)/shard_map/ppermute | solution.py:88
  92.5 6.7 %collective-permute-start.20 = (bf16[288,256]{1,0:T(8,128)(2,1)S(1)}, bf16[288,256]{1,0:T(8,128)(2,1)S(1)}, u32[]{:S(2)}, u32[]{:S(2)}) collective-permute-start(bf16[288,256]{1,0:T(8,128)(2,1)S(1)} %kv.1.refs_0_), channel_id=1, source_target_pairs={{0,4},{2,10},{8,0},{10,18},{16,8},{18,26},{24,16},{26,30},{28,24},... | collective-permute-start | bytes 442376 | tf_op jit(solution)/shard_map/ppermute | solution.py:88
  94.1 21.3 %collective-permute-start.42 = (bf16[1024,256]{1,0:T(8,128)(2,1)S(1)}, bf16[1024,256]{1,0:T(8,128)(2,1)S(1)}, u32[]{:S(2)}, u32[]{:S(2)}) collective-permute-start(bf16[1024,256]{1,0:T(8,128)(2,1)S(1)} %collective-permute-done.41), channel_id=1, source_target_pairs={{0,8},{2,6},{8,16},{10,2},{16,24},{18,10},{24,28},{26,18},{28,20},... | collective-permute-start | bytes 1572872 | tf_op jit(solution)/shard_map/ppermute | solution.py:88
  94.6 7.8 %collective-permute-start.22 = (bf16[288,256]{1,0:T(8,128)(2,1)S(1)}, bf16[288,256]{1,0:T(8,128)(2,1)S(1)}, u32[]{:S(2)}, u32[]{:S(2)}) collective-permute-start(bf16[288,256]{1,0:T(8,128)(2,1)S(1)} %collective-permute-done.19.refs_0_), channel_id=1, source_target_pairs={{0,4},{2,10},{8,0},{10,18},{16,8},{18,26},{24,16},{26,30},{28,24},... | collective-permute-start | bytes 442376 | tf_op jit(solution)/shard_map/ppermute | solution.py:88
  99.2 6.7 %collective-permute-start.24 = (bf16[288,256]{1,0:T(8,128)(2,1)S(1)}, bf16[288,256]{1,0:T(8,128)(2,1)S(1)}, u32[]{:S(2)}, u32[]{:S(2)}) collective-permute-start(bf16[288,256]{1,0:T(8,128)(2,1)S(1)} %collective-permute-done.20.refs_1_), channel_id=1, source_target_pairs={{0,4},{2,10},{8,0},{10,18},{16,8},{18,26},{24,16},{26,30},{28,24},... | collective-permute-start | bytes 442376 | tf_op jit(solution)/shard_map/ppermute | solution.py:88
  102.4 6.7 %collective-permute-start.26 = (bf16[288,256]{1,0:T(8,128)(2,1)S(1)}, bf16[288,256]{1,0:T(8,128)(2,1)S(1)}, u32[]{:S(2)}, u32[]{:S(2)}) collective-permute-start(bf16[288,256]{1,0:T(8,128)(2,1)S(1)} %collective-permute-done.22.refs_2_), channel_id=1, source_target_pairs={{0,4},{2,10},{8,0},{10,18},{16,8},{18,26},{24,16},{26,30},{28,24},... | collective-permute-start | bytes 442376 | tf_op jit(solution)/shard_map/ppermute | solution.py:88
  106.0 6.7 %collective-permute-start.28 = (bf16[288,256]{1,0:T(8,128)(2,1)S(1)}, bf16[288,256]{1,0:T(8,128)(2,1)S(1)}, u32[]{:S(2)}, u32[]{:S(2)}) collective-permute-start(bf16[288,256]{1,0:T(8,128)(2,1)S(1)} %collective-permute-done.24.refs_3_), channel_id=1, source_target_pairs={{0,4},{2,10},{8,0},{10,18},{16,8},{18,26},{24,16},{26,30},{28,24},... | collective-permute-start | bytes 442376 | tf_op jit(solution)/shard_map/ppermute | solution.py:88
  107.5 7.8 %collective-permute-start.21 = (bf16[288,256]{1,0:T(8,128)(2,1)S(1)}, bf16[288,256]{1,0:T(8,128)(2,1)S(1)}, u32[]{:S(2)}, u32[]{:S(2)}) collective-permute-start(bf16[288,256]{1,0:T(8,128)(2,1)S(1)} %collective-permute-done.20.refs_1_), channel_id=1, source_target_pairs={{0,2},{2,0},{4,6},{6,4},{8,10},{10,8},{12,14},{14,12},{16,18},{18,... | collective-permute-start | bytes 442376 | tf_op jit(solution)/shard_map/ppermute | solution.py:75
  107.5 8.3 %collective-permute-start.23 = (bf16[288,256]{1,0:T(8,128)(2,1)S(1)}, bf16[288,256]{1,0:T(8,128)(2,1)S(1)}, u32[]{:S(2)}, u32[]{:S(2)}) collective-permute-start(bf16[288,256]{1,0:T(8,128)(2,1)S(1)} %collective-permute-done.22.refs_2_), channel_id=1, source_target_pairs={{0,2},{2,0},{4,6},{6,4},{8,10},{10,8},{12,14},{14,12},{16,18},{18,... | collective-permute-start | bytes 442376 | tf_op jit(solution)/shard_map/ppermute | solution.py:75
  109.1 6.8 %collective-permute-start.30 = (bf16[288,256]{1,0:T(8,128)(2,1)S(1)}, bf16[288,256]{1,0:T(8,128)(2,1)S(1)}, u32[]{:S(2)}, u32[]{:S(2)}) collective-permute-start(bf16[288,256]{1,0:T(8,128)(2,1)S(1)} %collective-permute-done.26.refs_4_), channel_id=1, source_target_pairs={{0,4},{2,10},{8,0},{10,18},{16,8},{18,26},{24,16},{26,30},{28,24},... | collective-permute-start | bytes 442376 | tf_op jit(solution)/shard_map/ppermute | solution.py:88
  115.9 7.9 %collective-permute-start.29 = (bf16[288,256]{1,0:T(8,128)(2,1)S(1)}, bf16[288,256]{1,0:T(8,128)(2,1)S(1)}, u32[]{:S(2)}, u32[]{:S(2)}) collective-permute-start(bf16[288,256]{1,0:T(8,128)(2,1)S(1)} %collective-permute-done.28.refs_5_), channel_id=1, source_target_pairs={{0,2},{2,0},{4,6},{6,4},{8,10},{10,8},{12,14},{14,12},{16,18},{18,... | collective-permute-start | bytes 442376 | tf_op jit(solution)/shard_map/ppermute | solution.py:75
  115.9 7.8 %collective-permute-start.31 = (bf16[288,256]{1,0:T(8,128)(2,1)S(1)}, bf16[288,256]{1,0:T(8,128)(2,1)S(1)}, u32[]{:S(2)}, u32[]{:S(2)}) collective-permute-start(bf16[288,256]{1,0:T(8,128)(2,1)S(1)} %collective-permute-done.30.refs_6_), channel_id=1, source_target_pairs={{0,2},{2,0},{4,6},{6,4},{8,10},{10,8},{12,14},{14,12},{16,18},{18,... | collective-permute-start | bytes 442376 | tf_op jit(solution)/shard_map/ppermute | solution.py:75
  117.8 5.9 %collective-permute-start.33 = (bf16[288,256]{1,0:T(8,128)(2,1)S(1)}, bf16[288,256]{1,0:T(8,128)(2,1)S(1)}, u32[]{:S(2)}, u32[]{:S(2)}) collective-permute-start(bf16[288,256]{1,0:T(8,128)(2,1)S(1)} %collective-permute-done.32.refs_7_), channel_id=1, source_target_pairs={{0,2},{2,0},{4,6},{6,4},{8,10},{10,8},{12,14},{14,12},{16,18},{18,... | collective-permute-start | bytes 442376 | tf_op jit(solution)/shard_map/ppermute | solution.py:75
  119.6 19.8 %collective-permute-start.40 = (bf16[1024,256]{1,0:T(8,128)(2,1)S(1)}, bf16[1024,256]{1,0:T(8,128)(2,1)S(1)}, u32[]{:S(2)}, u32[]{:S(2)}) collective-permute-start(bf16[1024,256]{1,0:T(8,128)(2,1)S(1)} %collective-permute-done.39.refs_3_), channel_id=1, source_target_pairs={{0,8},{2,6},{8,16},{10,2},{16,24},{18,10},{24,28},{26,18},{28,20},... | collective-permute-start | bytes 1572872 | tf_op jit(solution)/shard_map/ppermute | solution.py:88
  121.2 14.6 %collective-permute-start.43 = (bf16[1024,256]{1,0:T(8,128)(2,1)S(1)}, bf16[1024,256]{1,0:T(8,128)(2,1)S(1)}, u32[]{:S(2)}, u32[]{:S(2)}) collective-permute-start(bf16[1024,256]{1,0:T(8,128)(2,1)S(1)} %collective-permute-done.42.refs_2_), channel_id=1, source_target_pairs={{0,8},{2,6},{8,16},{10,2},{16,24},{18,10},{24,28},{26,18},{28,20},... | collective-permute-start | bytes 1572872 | tf_op jit(solution)/shard_map/ppermute | solution.py:88
  124.8 8.9 %collective-permute-start.34 = (bf16[288,512]{1,0:T(8,128)(2,1)S(1)}, bf16[288,512]{1,0:T(8,128)(2,1)S(1)}, u32[]{:S(2)}, u32[]{:S(2)}) collective-permute-start(bf16[288,512]{1,0:T(8,128)(2,1)S(1)} %shard_map.95.mine), channel_id=1, source_target_pairs={{0,1},{1,0},{2,3},{3,2},{4,5},{5,4},{6,7},{7,6},{8,9},{9,8},{10,11... | collective-permute-start | bytes 884744 | tf_op jit(solution)/shard_map/ppermute | solution.py:79
  125.4 18.9 %collective-permute-start.35 = (bf16[288,512]{1,0:T(8,128)(2,1)S(1)}, bf16[288,512]{1,0:T(8,128)(2,1)S(1)}, u32[]{:S(2)}, u32[]{:S(2)}) collective-permute-start(bf16[288,512]{1,0:T(8,128)(2,1)S(1)} %shard_map.95.mine), channel_id=1, source_target_pairs={{0,2},{2,0},{4,6},{6,4},{8,10},{10,8},{12,14},{14,12},{16,18},{18,... | collective-permute-start | bytes 884744 | tf_op jit(solution)/shard_map/ppermute | solution.py:75
  133.8 10.6 %collective-permute-start.36 = (bf16[288,512]{1,0:T(8,128)(2,1)S(1)}, bf16[288,512]{1,0:T(8,128)(2,1)S(1)}, u32[]{:S(2)}, u32[]{:S(2)}) collective-permute-start(bf16[288,512]{1,0:T(8,128)(2,1)S(1)} %collective-permute-done.34.across), channel_id=1, source_target_pairs={{0,2},{2,0},{4,6},{6,4},{8,10},{10,8},{12,14},{14,12},{16,18},{18,... | collective-permute-start | bytes 884744 | tf_op jit(solution)/shard_map/ppermute | solution.py:75
  135.8 15.0 %collective-permute-start.44 = (bf16[1024,256]{1,0:T(8,128)(2,1)S(1)}, bf16[1024,256]{1,0:T(8,128)(2,1)S(1)}, u32[]{:S(2)}, u32[]{:S(2)}) collective-permute-start(bf16[1024,256]{1,0:T(8,128)(2,1)S(1)} %collective-permute-done.43.refs_4_), channel_id=1, source_target_pairs={{0,8},{2,6},{8,16},{10,2},{16,24},{18,10},{24,28},{26,18},{28,20},... | collective-permute-start | bytes 1572872 | tf_op jit(solution)/shard_map/ppermute | solution.py:88
  139.4 13.4 %collective-permute-start.45 = (bf16[1024,256]{1,0:T(8,128)(2,1)S(1)}, bf16[1024,256]{1,0:T(8,128)(2,1)S(1)}, u32[]{:S(2)}, u32[]{:S(2)}) collective-permute-start(bf16[1024,256]{1,0:T(8,128)(2,1)S(1)} %collective-permute-done.40.refs_0_), channel_id=1, source_target_pairs={{0,8},{2,6},{8,16},{10,2},{16,24},{18,10},{24,28},{26,18},{28,20},... | collective-permute-start | bytes 1572872 | tf_op jit(solution)/shard_map/ppermute | solution.py:88
  148.6 11.5 %collective-permute-start.49 = (bf16[5,144,256]{2,1,0:T(8,128)(2,1)S(1)}, bf16[5,144,256]{2,1,0:T(8,128)(2,1)S(1)}, u32[]{:S(2)}, u32[]{:S(2)}) collective-permute-start(bf16[5,144,256]{2,1,0:T(8,128)(2,1)S(1)} %get-tuple-element.50), channel_id=1, source_target_pairs={{0,1},{1,0},{2,3},{3,2},{4,5},{5,4},{6,7},{7,6},{8,9},{9,8},{10,11... | collective-permute-start | bytes 1105928 | tf_op jit(solution)/shard_map/ppermute | solution.py:79
  149.1 11.0 %collective-permute-start.50 = (bf16[5,144,256]{2,1,0:T(8,128)(2,1)S(1)}, bf16[5,144,256]{2,1,0:T(8,128)(2,1)S(1)}, u32[]{:S(2)}, u32[]{:S(2)}) collective-permute-start(bf16[5,144,256]{2,1,0:T(8,128)(2,1)S(1)} %get-tuple-element.51), channel_id=1, source_target_pairs={{0,2},{2,0},{4,6},{6,4},{8,10},{10,8},{12,14},{14,12},{16,18},{18,... | collective-permute-start | bytes 1105928 | tf_op jit(solution)/shard_map/ppermute | solution.py:75
  149.1 16.9 %collective-permute-start.51 = (bf16[5,144,256]{2,1,0:T(8,128)(2,1)S(1)}, bf16[5,144,256]{2,1,0:T(8,128)(2,1)S(1)}, u32[]{:S(2)}, u32[]{:S(2)}) collective-permute-start(bf16[5,144,256]{2,1,0:T(8,128)(2,1)S(1)} %get-tuple-element.52), channel_id=1, source_target_pairs={{0,3},{1,2},{2,1},{3,0},{4,7},{5,6},{6,5},{7,4},{8,11},{9,10},{10,... | collective-permute-start | bytes 1105928 | tf_op jit(solution)/shard_map/ppermute | solution.py:84
  155.9 16.4 %collective-permute-start.46 = (bf16[3,144,256]{2,1,0:T(8,128)(2,1)S(1)}, bf16[3,144,256]{2,1,0:T(8,128)(2,1)S(1)}, u32[]{:S(2)}, u32[]{:S(2)}) collective-permute-start(bf16[3,144,256]{2,1,0:T(8,128)(2,1)S(1)} %get-tuple-element.46), channel_id=1, source_target_pairs={{0,1},{1,0},{2,3},{3,2},{4,5},{5,4},{6,7},{7,6},{8,9},{9,8},{10,11... | collective-permute-start | bytes 663560 | tf_op jit(solution)/shard_map/ppermute | solution.py:79
  156.5 15.8 %collective-permute-start.47 = (bf16[3,144,256]{2,1,0:T(8,128)(2,1)S(1)}, bf16[3,144,256]{2,1,0:T(8,128)(2,1)S(1)}, u32[]{:S(2)}, u32[]{:S(2)}) collective-permute-start(bf16[3,144,256]{2,1,0:T(8,128)(2,1)S(1)} %get-tuple-element.47), channel_id=1, source_target_pairs={{0,2},{2,0},{4,6},{6,4},{8,10},{10,8},{12,14},{14,12},{16,18},{18,... | collective-permute-start | bytes 663560 | tf_op jit(solution)/shard_map/ppermute | solution.py:75
  160.1 12.6 %collective-permute-start.48 = (bf16[3,144,256]{2,1,0:T(8,128)(2,1)S(1)}, bf16[3,144,256]{2,1,0:T(8,128)(2,1)S(1)}, u32[]{:S(2)}, u32[]{:S(2)}) collective-permute-start(bf16[3,144,256]{2,1,0:T(8,128)(2,1)S(1)} %get-tuple-element.48), channel_id=1, source_target_pairs={{0,3},{1,2},{2,1},{3,0},{4,7},{5,6},{6,5},{7,4},{8,11},{9,10},{10,... | collective-permute-start | bytes 663560 | tf_op jit(solution)/shard_map/ppermute | solution.py:84
  (12 other events, 62.3 us)
where the time goes:
time: 176 us; the launch traced here: 174 us
  waiting for transfers between devices  79.9 us (45%)
  starting transfers between devices  58.9 us (33%)
  Pallas kernels  24.9 us (14%)
  local copies, waits for them, and re-layouts  7.41 us (4%)
  other arithmetic  2.85 us (2%)
    ppermute x28, waiting for transfers between devices, pass_on(): return lax.ppermute(value, 'seq', ring_perm(seq_size, turn))  56.1 us
    ppermute x28, starting transfers between devices, pass_on(): return lax.ppermute(value, 'seq', ring_perm(seq_size, turn))  51 us
    ppermute x4, waiting for transfers between devices, swap_head(): return lax.ppermute(value, 'head', [(0, 1), (1, 0)])  17.4 us
    pallas_call x2, Pallas kernels, project_out(): pl.pallas_call(functools.partial(out_kernel, pieces), out_shape=(shape,)...  7.35 us
    ppermute x2, waiting for transfers between devices, swap_both(): return lax.ppermute(value, ('seq', 'head'), pairs)  6.31 us
    pallas_call x3, Pallas kernels, project(): pl.pallas_call(functools.partial(project_kernel, start, count), out_shape...  6.11 us
    unnamed x17, local copies, waits for them, and re-layouts  5.46 us
    pallas_call x1, Pallas kernels, norm(): pl.pallas_call(norm_kernel, out_shape=(shape, shape), in_specs=[SMEM, VME...  4.76 us
  transfers between devices with their start and end apart: 52, of which 23 were waited for; matrix products, arithmetic and copies ran while one was open for 1% of the time, Pallas kernels for 11%

commit v1 on v0

--- a/solution.py
+++ b/solution.py
@@ -101,6 +101,46 @@
     return held
 
 
+def prepare_kernel(place, w_key, w_value, w_query, w_out, pair, *refs):
+    parts, (near, far, sems) = refs[:-3], refs[-3:]
+    columns = near.shape[1]
+    width = parts[0].shape[1]
+    here = pl.multiple_of(place[0] * columns, 128)
+    there = pl.multiple_of((1 - place[0]) * columns, 128)
+    copies = [
+        (w_key, pair.at[:, :HEAD_DIM]),
+        (w_value, pair.at[:, HEAD_DIM:]),
+        (w_out.at[:, pl.ds(here, columns)], near),
+        (w_out.at[:, pl.ds(there, columns)], far),
+    ]
+    for index, part in enumerate(parts):
+        span = slice(index * width, (index + 1) * width)
+        copies.append((w_query.at[:, span], part))
+    copies = [
+        pltpu.make_async_copy(old, new, sems.at[index])
+        for index, (old, new) in enumerate(copies)
+    ]
+    for copy in copies:
+        copy.start()
+    for copy in copies:
+        copy.wait()
+
+
+def prepare(place, w_key, w_value, w_query, w_out, groups):
+    depth, width = w_query.shape
+    shapes = [(depth, 2 * HEAD_DIM)] + [(depth, width // groups)] * groups
+    shapes += [(w_out.shape[0], w_out.shape[1] // 2)] * 2
+    return pl.pallas_call(
+        prepare_kernel,
+        out_shape=[jax.ShapeDtypeStruct(one, jnp.bfloat16) for one in shapes],
+        in_specs=[SMEM] + [HBM] * 4,
+        out_specs=[VMEM] * len(shapes),
+        scratch_shapes=[pltpu.SemaphoreType.DMA((4 + groups,))],
+        cost_estimate=estimate(1),
+        name="prep",
+    )(place, w_key, w_value, w_query, w_out)
+
+
 def norm_kernel(table, hidden, gain, mine, other):
     slots, rows, depth = mine.shape
     width = hidden.shape[1]
@@ -214,21 +254,13 @@
         out_specs=VMEM,
         compiler_params=GRANT,
         cost_estimate=estimate(2),
-        name="qs",
     )(keep, got, bias, cosine, sine)
 
 
-def attend_kernel(first, count, offset, table, query, *refs):
-    inputs = len(refs) - (7 if first else 8)
-    carried = () if first else refs[inputs - 3 : inputs]
-    sources = refs[: inputs - (0 if first else 3)]
-    if first:
-        high, weight, mixture = refs[inputs : inputs + 3]
-        pairs, sems, even, odd = refs[inputs + 3 :]
-    else:
-        out = refs[inputs]
-        pairs, sems, even, odd, high, weight, mixture = refs[inputs + 1 :]
-    rows, _ = sources[0].shape[-2:]
+def attend_kernel(count, offset, table, query, *refs):
+    sources = refs[:count]
+    out, pairs, sems, even, odd, high, weight, mixture = refs[count:]
+    rows = sources[0].shape[0]
     lanes = query.shape[1]
     shard = table[0]
     factor = HEAD_DIM ** (-0.5) * LOG2E
@@ -239,20 +271,16 @@
     def wait(at):
         pltpu.make_async_copy(pairs.at[at], pairs.at[at], sems.at[at]).wait()
 
-    start = 1 if first else 0
-    if first:
-        copy(0, 0)
+    copy(0, 0)
     needed = jnp.int32(0)
-    for slot in range(start, count):
+    for slot in range(1, count):
         seen = table[offset + slot] < shard
 
         @pl.when(seen)
         def _(slot=slot, needed=needed):
-            copy(slot, needed + start)
+            copy(slot, needed + 1)
 
         needed = needed + seen.astype(jnp.int32)
-    for new, old in zip((high, weight, mixture), carried):
-        new[...] = old[...]
 
     def keys_of(at, size):
         return pairs[pl.ds(at, size), :, :HEAD_DIM].reshape(size * rows, HEAD_DIM)
@@ -275,21 +303,20 @@
         weight[...] = added
         mixture[...] = mixed
 
-    if first:
-        wait(0)
-        scores = dot(keys_of(0, 1), query[...])
-        row = lax.broadcasted_iota(jnp.int32, scores.shape, 0)
-        lane = lax.rem(lax.broadcasted_iota(jnp.int32, (1, lanes), 1), rows)
-        update(jnp.where(row <= lane, scores, -jnp.inf), values_of(0, 1), True)
+    wait(0)
+    scores = dot(keys_of(0, 1), query[...])
+    row = lax.broadcasted_iota(jnp.int32, scores.shape, 0)
+    lane = lax.rem(lax.broadcasted_iota(jnp.int32, (1, lanes), 1), rows)
+    update(jnp.where(row <= lane, scores, -jnp.inf), values_of(0, 1), True)
 
     single = lax.rem(needed, 2)
 
     @pl.when(single == 1)
     def _():
-        wait(start)
-        update(dot(keys_of(start, 1), query[...]), values_of(start, 1), False)
-
-    begin = start + single
+        wait(1)
+        update(dot(keys_of(1, 1), query[...]), values_of(1, 1), False)
+
+    begin = 1 + single
     turns = needed // 2
 
     def arrive(turn):
@@ -318,69 +345,59 @@
             def _():
                 step(2 * index + 1, odd, even)
 
-    if not first:
-        value = (mixture[...] / weight[...]).T
-        for head in range(lanes // rows):
-            out[:, head * HEAD_DIM : (head + 1) * HEAD_DIM] = value[
-                head * rows : (head + 1) * rows
-            ].astype(jnp.bfloat16)
-
-
-def attend(table, query, sources, offset, carried):
+    value = (mixture[...] / weight[...]).T
+    for head in range(lanes // rows):
+        out[:, head * HEAD_DIM : (head + 1) * HEAD_DIM] = value[
+            head * rows : (head + 1) * rows
+        ].astype(jnp.bfloat16)
+
+
+def attend(table, query, sources, offset):
     count = len(sources)
     lanes = query.shape[1]
-    rows = sources[0].shape[-2]
-    first = not carried
-    state = [
-        ((1, lanes), jnp.float32),
-        ((1, lanes), jnp.float32),
-        ((HEAD_DIM, lanes), jnp.float32),
-    ]
-    if first:
-        out_shape = tuple(jax.ShapeDtypeStruct(*one) for one in state)
-        out_specs = (VMEM,) * 3
-    else:
-        out_shape = jax.ShapeDtypeStruct((rows, lanes // rows * HEAD_DIM), jnp.bfloat16)
-        out_specs = VMEM
-    scratch = [
-        pltpu.VMEM((count, rows, 2 * HEAD_DIM), jnp.bfloat16),
-        pltpu.SemaphoreType.DMA((count,)),
-        pltpu.VMEM((2 * rows, lanes), jnp.float32),
-        pltpu.VMEM((2 * rows, lanes), jnp.float32),
-    ]
-    if not first:
-        scratch += [pltpu.VMEM(*one) for one in state]
-    return pl.pallas_call(
-        functools.partial(attend_kernel, first, count, offset),
-        out_shape=out_shape,
-        in_specs=[SMEM, VMEM] + [HBM] * len(sources) + [VMEM] * len(carried),
-        out_specs=out_specs,
-        scratch_shapes=scratch,
+    rows = sources[0].shape[0]
+    shape = (rows, lanes // rows * HEAD_DIM)
+    return pl.pallas_call(
+        functools.partial(attend_kernel, count, offset),
+        out_shape=jax.ShapeDtypeStruct(shape, jnp.bfloat16),
+        in_specs=[SMEM, VMEM] + [HBM] * count,
+        out_specs=VMEM,
+        scratch_shapes=[
+            pltpu.VMEM((count, rows, 2 * HEAD_DIM), jnp.bfloat16),
+            pltpu.SemaphoreType.DMA((count,)),
+            pltpu.VMEM((2 * rows, lanes), jnp.float32),
+            pltpu.VMEM((2 * rows, lanes), jnp.float32),
+            pltpu.VMEM((1, lanes), jnp.float32),
+            pltpu.VMEM((1, lanes), jnp.float32),
+            pltpu.VMEM((HEAD_DIM, lanes), jnp.float32),
+        ],
         compiler_params=GRANT,
         cost_estimate=estimate(8),
-    )(table, query, *sources, *carried)
-
-
-def out_kernel(pieces, place, mine, across, mine_other, across_other, *refs):
-    weights = refs[:pieces]
-    keep, keep_other, send, send_other, source, block, sems, weight_sems = refs[pieces:]
-    rows = mine.shape[0] // 2
-    depth = mine.shape[1]
+    )(table, query, *sources)
+
+
+def out_kernel(pieces, groups, place, *refs):
+    weights = refs[4 * groups : 4 * groups + pieces]
+    keep, keep_other, send, send_other, source, block, sems, weight_sems = refs[-8:]
+    rows = refs[0].shape[0] // 2
+    width = refs[0].shape[1]
+    depth = width * groups
     half = place[0]
     near = pl.ds(pl.multiple_of(half * rows, 16), rows)
     far = pl.ds(pl.multiple_of((1 - half) * rows, 16), rows)
     copies = []
-    for group, (own, other) in enumerate(((mine, mine_other), (across, across_other))):
-        for part, (ref, span) in enumerate(
-            ((own, near), (other, near), (own, far), (other, far))
-        ):
-            copies.append(
-                pltpu.make_async_copy(
-                    ref.at[span],
-                    source.at[group, pl.ds(part * rows, rows)],
-                    sems.at[group, part],
+    for side in range(2):
+        for index in range(groups):
+            own, other = refs[side * groups + index], refs[(2 + side) * groups + index]
+            for part, (ref, span) in enumerate(
+                ((own, near), (other, near), (own, far), (other, far))
+            ):
+                place_at = (side, pl.ds(part * rows, rows), pl.ds(index * width, width))
+                copies.append(
+                    pltpu.make_async_copy(
+                        ref.at[span], source.at[place_at], sems.at[side, index, part]
+                    )
                 )
-            )
     for copy in copies:
         copy.start()
     for piece in range(pieces):
@@ -404,18 +421,19 @@
 
 def project_out(place, attended, weights):
     pieces = len(weights)
-    rows, depth = attended[0].shape
+    groups = len(attended) // 4
+    rows, depth = attended[0].shape[0], weights[0].shape[0] // 2
     columns = weights[0].shape[1]
     shape = jax.ShapeDtypeStruct((pieces, rows // 2, columns), jnp.bfloat16)
     return pl.pallas_call(
-        functools.partial(out_kernel, pieces),
+        functools.partial(out_kernel, pieces, groups),
         out_shape=(shape,) * 4,
-        in_specs=[SMEM] + [HBM] * (4 + pieces),
+        in_specs=[SMEM] + [HBM] * (4 * groups + pieces),
         out_specs=(VMEM,) * 4,
         scratch_shapes=[
             pltpu.VMEM((2, 2 * rows, depth), jnp.bfloat16),
             pltpu.VMEM((pieces, 2 * depth, columns), jnp.bfloat16),
-            pltpu.SemaphoreType.DMA((2, 4)),
+            pltpu.SemaphoreType.DMA((2, groups, 4)),
             pltpu.SemaphoreType.DMA((pieces,)),
         ],
         compiler_params=GRANT,
@@ -474,15 +492,21 @@
     rows, width = hidden.shape
     depth = w_query.shape[0]
     slots = seq_size // 2
+    groups = 2
     shard = lax.axis_index("seq")
     side = lax.axis_index("head")
     table = jnp.stack(slot_shards(seq_size, shard) + slot_shards(seq_size, shard, -1))
     place = jnp.reshape(side, (1,)).astype(jnp.int32)
 
-    w_kv = jnp.concatenate([w_key, w_value], axis=1)
+    w_kv, *w_queries, near, far = prepare(place, w_key, w_value, w_query, w_out, groups)
     w_kv_other = swap_core(w_kv, seq_size)
     kv_weights = ring_gather(w_kv, w_kv_other, seq_size)
+    q_weights = []
+    for weight in w_queries:
+        weight_other = swap_core(weight, seq_size)
+        q_weights.append(ring_gather(weight, weight_other, seq_size))
     mine, for_other = norm(table, hidden, norm_gain.reshape(1, width), slots, depth)
+
     positions = shard * rows + jnp.arange(rows, dtype=jnp.int32)
     half_dim = HEAD_DIM // 2
     freq = ROPE_BASE ** (-2.0 * jnp.arange(half_dim, dtype=jnp.float32) / HEAD_DIM)
@@ -491,7 +515,6 @@
     sine = jnp.sin(angles)
     cosine = jnp.concatenate([cosine, cosine], axis=1)
     sine = jnp.concatenate([-sine, sine], axis=1)
-
     bias_kv = jnp.concatenate([bias_key, bias_value]).astype(jnp.float32)[None]
     bias_query = bias_query.astype(jnp.float32)[None]
     for_other, cosine, sine, bias_kv, bias_query = lax.optimization_barrier(
@@ -504,35 +527,38 @@
     own_kv = keys_values(keep, got, bias_kv, cosine, sine)
     other_kv = swap_core(own_kv, seq_size)
     held = ring_gather(own_kv, other_kv, seq_size, -1)
-    swapped = [other_kv]
+    tokens = held + [other_kv]
     for one in held[1:]:
-        swapped.append(swap_core(one, seq_size))
-
-    w_query_other = swap_core(w_query, seq_size)
-    q_weights = ring_gather(w_query, w_query_other, seq_size)
-    early = slots - 3
-    sums = project(mine, other, q_weights[:early], 0, ())
-    keep, send = project(mine, other, q_weights[early:], early, sums)
-    got = swap_core(send, seq_size)
-    query = queries(keep, got, bias_query, cosine, sine)
-    state = attend(table, query, held, 2 * slots, ())
-    attended = attend(table, query, swapped, 3 * slots, state)
-
-    columns = w_out.shape[1] // 2
-    near = lax.dynamic_slice_in_dim(w_out, side * columns, columns, 1)
-    far = lax.dynamic_slice_in_dim(w_out, (1 - side) * columns, columns, 1)
+        tokens.append(swap_core(one, seq_size))
+
+    columns = w_query.shape[1] // groups
+    attended = []
+    for index, weights in enumerate(q_weights):
+        sums = ()
+        start = 0
+        for count in (slots - 3, 3):
+            sums = project(mine, other, weights[start : start + count], start, sums)
+            start += count
+        keep, send = sums
+        got = swap_core(send, seq_size)
+        bias = bias_query[:, index * columns : (index + 1) * columns]
+        query = queries(keep, got, bias, cosine, sine)
+        attended.append(attend(table, query, tokens, 2 * slots))
+
     far = swap_head(far)
     piece = jnp.concatenate([near, far])
     piece_other = swap_core(piece, seq_size)
     out_weights = ring_gather(piece, piece_other, seq_size)
 
-    across = swap_head(attended)
-    attended_other = swap_core(attended, seq_size)
-    across_other = swap_core(across, seq_size)
-    operands = (attended, across, attended_other, across_other)
+    across, attended_other, across_other = [], [], []
+    for one in attended:
+        across.append(swap_head(one))
+        attended_other.append(swap_core(one, seq_size))
+        across_other.append(swap_core(across[-1], seq_size))
+    operands = attended + across + attended_other + across_other
     whole = None
     start = 0
-    for count in (slots - 3, 3):
+    for count in (slots - 5, 2, 2, 1):
         keep, keep_other, send, send_other = project_out(
             place, operands, out_weights[start : start + count]
         )

time: 176 us -> 174 us (0.989)
  the two profiles are of different devices: /device:TPU:0 before, /device:TPU:26 now
where the time goes in v1:
time: 174 us; the launch traced here: 173 us
  waiting for transfers between devices  87.9 us (51%)
  Pallas kernels  40.5 us (23%)
  starting transfers between devices  33.9 us (19%)
  local copies, waits for them, and re-layouts  8.18 us (5%)
  other arithmetic  2.11 us (1%)
    ppermute x35, waiting for transfers between devices, pass_on(): return lax.ppermute(value, 'seq', ring_perm(seq_size, turn))  72.9 us
    ppermute x35, starting transfers between devices, pass_on(): return lax.ppermute(value, 'seq', ring_perm(seq_size, turn))  19.1 us
    pallas_call x2, Pallas kernels, attend(): pl.pallas_call(functools.partial(attend_kernel, count, offset), out_shape...  17.3 us
    ppermute x7, waiting for transfers between devices, swap_head(): return lax.ppermute(value, 'head', [(0, 1), (1, 0)])  9.44 us
    ppermute x7, starting transfers between devices, swap_head(): return lax.ppermute(value, 'head', [(0, 1), (1, 0)])  7.34 us
    unnamed x13, local copies, waits for them, and re-layouts  7.31 us
    pallas_call x4, Pallas kernels, place_part(): pl.pallas_call(functools.partial(place_kernel, start, slots, width), out_...  5.67 us
    pallas_call x4, Pallas kernels, project_out(): pl.pallas_call(functools.partial(out_kernel, pieces, groups), out_shape=(...  5.28 us
  transfers between devices with their start and end apart: 70, of which 34 were waited for; matrix products, arithmetic and copies ran while one was open for 1% of the time, Pallas kernels for 20%

profile of v1, /device:TPU:26, one launch (start us, length us, event | category | flops | bytes accessed | tf_op | source)
XLA Modules:
  0.0 173.2 jit_solution(2093530849454845038)
XLA Ops:
  2.9 2.3 %copy-done = bf16[288,8192]{1,0:T(8,128)(2,1)S(1)} copy-done((bf16[288,8192]{1,0:T(8,128)(2,1)S(1)}, bf16[288,8192]{1,0:T(8,128)(2,1)}, u32[]{:S(2)}) %copy-start) | copy-done | bytes 4718616
  5.2 4.8 %norm.1 = (bf16[8,288,512]{2,1,0:T(8,128)(2,1)S(1)}, bf16[8,288,512]{2,1,0:T(8,128)(2,1)}) custom-call(s32[32]{0:T(128)S(1)} %stack.125.table, bf16[288,8192]{1,0:T(8,128)(2,1)S(1)} %copy-done, bf16[1,8192]{1,0:T(2,128)(2,1)S(1)} %reshape.46.gain), custom_call_target="tpu_custom_call" | custom-call | flops 4000000000 | bytes 1000000 | tf_op jit(solution)/shard_map/norm/pallas_call | solution.py:175
  10.0 1.4 copy-done.4
  11.6 2.5 %prep.1 = (bf16[512,256]{1,0:T(8,128)(2,1)}, bf16[512,256]{1,0:T(8,128)(2,1)}, bf16[512,256]{1,0:T(8,128)(2,1)}, bf16[512,256]{1,0:T(8,128)(2,1)}, bf16[512,256]{1,0:T(8,128)(2,1)}) custom-call(s32[1]{0:T(128)} %bitcast.30.place, bf16[512,128]{1,0:T(8,128)(2,1)} %w_key.1, bf16[512,128]{1,0:T(8,128)(2,1)} %w_value.1, bf16[512,512]{1,0:T(8,128)(2,1)} %w_query.1, ...), custom_call_target="tpu_custom_call" | custom-call | flops 1000000000 | bytes 1000000 | tf_op jit(solution)/shard_map/prep/pallas_call | solution.py:133
  16.4 4.3 %collective-permute-done.10.refs_1_ = bf16[512,256]{1,0:T(8,128)(2,1)S(1)} collective-permute-done((bf16[512,256]{1,0:T(8,128)(2,1)}, bf16[512,256]{1,0:T(8,128)(2,1)S(1)}, u32[]{:S(2)}, u32[]{:S(2)}) %collective-permute-start.10) | collective-permute-done | bytes 262176 | tf_op jit(solution)/shard_map/ppermute | solution.py:88
  21.6 1.9 %collective-permute-done.34.refs_1_ = bf16[512,256]{1,0:T(8,128)(2,1)S(1)} collective-permute-done((bf16[512,256]{1,0:T(8,128)(2,1)}, bf16[512,256]{1,0:T(8,128)(2,1)S(1)}, u32[]{:S(2)}, u32[]{:S(2)}) %collective-permute-start.34) | collective-permute-done | bytes 262176 | tf_op jit(solution)/shard_map/ppermute | solution.py:88
  23.5 1.5 collective-permute-start.49
  25.0 2.0 %collective-permute-done.13.refs_3_ = bf16[512,256]{1,0:T(8,128)(2,1)S(1)} collective-permute-done((bf16[512,256]{1,0:T(8,128)(2,1)S(1)}, bf16[512,256]{1,0:T(8,128)(2,1)S(1)}, u32[]{:S(2)}, u32[]{:S(2)}) %collective-permute-start.13) | collective-permute-done | bytes 262176 | tf_op jit(solution)/shard_map/ppermute | solution.py:88
  27.5 2.4 %collective-permute-done.12.refs_2_ = bf16[512,256]{1,0:T(8,128)(2,1)S(1)} collective-permute-done((bf16[512,256]{1,0:T(8,128)(2,1)S(1)}, bf16[512,256]{1,0:T(8,128)(2,1)S(1)}, u32[]{:S(2)}, u32[]{:S(2)}) %collective-permute-start.12) | collective-permute-done | bytes 262176 | tf_op jit(solution)/shard_map/ppermute | solution.py:88
  32.0 1.4 collective-permute-done.15.refs_5_
  33.9 2.4 %collective-permute-done.14.refs_4_ = bf16[512,256]{1,0:T(8,128)(2,1)S(1)} collective-permute-done((bf16[512,256]{1,0:T(8,128)(2,1)S(1)}, bf16[512,256]{1,0:T(8,128)(2,1)S(1)}, u32[]{:S(2)}, u32[]{:S(2)}) %collective-permute-start.14) | collective-permute-done | bytes 262176 | tf_op jit(solution)/shard_map/ppermute | solution.py:88
  37.7 1.4 collective-permute-done.1.refs_1_
  39.1 2.8 %collective-permute-done.38.refs_2_ = bf16[512,256]{1,0:T(8,128)(2,1)S(1)} collective-permute-done((bf16[512,256]{1,0:T(8,128)(2,1)S(1)}, bf16[512,256]{1,0:T(8,128)(2,1)S(1)}, u32[]{:S(2)}, u32[]{:S(2)}) %collective-permute-start.38) | collective-permute-done | bytes 262176 | tf_op jit(solution)/shard_map/ppermute | solution.py:88
  42.3 2.4 %collective-permute-done.17.refs_7_ = bf16[512,256]{1,0:T(8,128)(2,1)S(1)} collective-permute-done((bf16[512,256]{1,0:T(8,128)(2,1)S(1)}, bf16[512,256]{1,0:T(8,128)(2,1)S(1)}, u32[]{:S(2)}, u32[]{:S(2)}) %collective-permute-start.17) | collective-permute-done | bytes 262176 | tf_op jit(solution)/shard_map/ppermute | solution.py:88
  45.2 2.4 %collective-permute-done.16.refs_6_ = bf16[512,256]{1,0:T(8,128)(2,1)S(1)} collective-permute-done((bf16[512,256]{1,0:T(8,128)(2,1)S(1)}, bf16[512,256]{1,0:T(8,128)(2,1)S(1)}, u32[]{:S(2)}, u32[]{:S(2)}) %collective-permute-start.16) | collective-permute-done | bytes 262176 | tf_op jit(solution)/shard_map/ppermute | solution.py:88
  49.4 1.7 copy-done.5
  51.0 1.4 shard_map.94
  53.6 2.4 %collective-permute-done.2.refs_3_ = bf16[512,256]{1,0:T(8,128)(2,1)S(1)} collective-permute-done((bf16[512,256]{1,0:T(8,128)(2,1)S(1)}, bf16[512,256]{1,0:T(8,128)(2,1)S(1)}, u32[]{:S(2)}, u32[]{:S(2)}) %collective-permute-start.2) | collective-permute-done | bytes 262176 | tf_op jit(solution)/shard_map/ppermute | solution.py:88
  56.4 2.4 %collective-permute-done.39.refs_4_ = bf16[512,256]{1,0:T(8,128)(2,1)S(1)} collective-permute-done((bf16[512,256]{1,0:T(8,128)(2,1)S(1)}, bf16[512,256]{1,0:T(8,128)(2,1)S(1)}, u32[]{:S(2)}, u32[]{:S(2)}) %collective-permute-start.39) | collective-permute-done | bytes 262176 | tf_op jit(solution)/shard_map/ppermute | solution.py:88
  59.7 7.5 %collective-permute-done.36.refs_0_ = bf16[512,256]{1,0:T(8,128)(2,1)S(1)} collective-permute-done((bf16[512,256]{1,0:T(8,128)(2,1)S(1)}, bf16[512,256]{1,0:T(8,128)(2,1)S(1)}, u32[]{:S(2)}, u32[]{:S(2)}) %collective-permute-start.36) | collective-permute-done | bytes 262176 | tf_op jit(solution)/shard_map/ppermute | solution.py:88
  67.6 2.4 %collective-permute-done.6.refs_4_ = bf16[512,256]{1,0:T(8,128)(2,1)S(1)} collective-permute-done((bf16[512,256]{1,0:T(8,128)(2,1)S(1)}, bf16[512,256]{1,0:T(8,128)(2,1)S(1)}, u32[]{:S(2)}, u32[]{:S(2)}) %collective-permute-start.6) | collective-permute-done | bytes 262176 | tf_op jit(solution)/shard_map/ppermute | solution.py:88
  72.0 1.6 collective-permute-done.3.refs_0_
  74.9 4.3 %collective-permute-done.41.refs_2_ = bf16[512,256]{1,0:T(8,128)(2,1)S(1)} collective-permute-done((bf16[512,256]{1,0:T(8,128)(2,1)S(1)}, bf16[512,256]{1,0:T(8,128)(2,1)S(1)}, u32[]{:S(2)}, u32[]{:S(2)}) %collective-permute-start.41) | collective-permute-done | bytes 262176 | tf_op jit(solution)/shard_map/ppermute | solution.py:88
  80.3 6.0 %collective-permute-done.8.refs_2_ = bf16[512,256]{1,0:T(8,128)(2,1)S(1)} collective-permute-done((bf16[512,256]{1,0:T(8,128)(2,1)S(1)}, bf16[512,256]{1,0:T(8,128)(2,1)S(1)}, u32[]{:S(2)}, u32[]{:S(2)}) %collective-permute-start.8) | collective-permute-done | bytes 262176 | tf_op jit(solution)/shard_map/ppermute | solution.py:88
  86.8 1.6 collective-permute-start.21
  89.6 4.4 %collective-permute-done.58.refs_10_ = bf16[1024,256]{1,0:T(8,128)(2,1)S(1)} collective-permute-done((bf16[1024,256]{1,0:T(8,128)(2,1)S(1)}, bf16[1024,256]{1,0:T(8,128)(2,1)S(1)}, u32[]{:S(2)}, u32[]{:S(2)}) %collective-permute-start.58) | collective-permute-done | bytes 524320 | tf_op jit(solution)/shard_map/ppermute | solution.py:88
  95.2 1.6 collective-permute-done.22.refs_3_
  96.8 1.6 collective-permute-start.24
  98.3 5.6 %collective-permute-done.51.refs_8_ = bf16[1024,256]{1,0:T(8,128)(2,1)S(1)} collective-permute-done((bf16[1024,256]{1,0:T(8,128)(2,1)S(1)}, bf16[1024,256]{1,0:T(8,128)(2,1)S(1)}, u32[]{:S(2)}, u32[]{:S(2)}) %collective-permute-start.51) | collective-permute-done | bytes 524320 | tf_op jit(solution)/shard_map/ppermute | solution.py:88
  106.3 3.2 %collective-permute-done.25.refs_6_ = bf16[288,256]{1,0:T(8,128)(2,1)S(1)} collective-permute-done((bf16[288,256]{1,0:T(8,128)(2,1)S(1)}, bf16[288,256]{1,0:T(8,128)(2,1)S(1)}, u32[]{:S(2)}, u32[]{:S(2)}) %collective-permute-start.25) | collective-permute-done | bytes 147488 | tf_op jit(solution)/shard_map/ppermute | solution.py:88
  109.6 1.6 collective-permute-done.26.refs_7_
  112.5 8.5 %shard_map.99.refs_1_ = bf16[288,256]{1,0:T(8,128)(2,1)S(1)} custom-call(s32[32]{0:T(128)S(1)} %stack.125.table, bf16[128,576]{1,0:T(8,128)(2,1)S(1)} %shard_map.98.query, bf16[288,256]{1,0:T(8,128)(2,1)S(1)} %kv.1.refs_0_, bf16[288,256]{1,0:T(8,128)(2,1)S(1)} %collective-permute-done.19.refs_1_, bf16[288,256]{1,0:T(8,128)(2,1)S(1)} %collective-permute-done.21.refs_2_, ...), custom_call_target="tpu_custom_call" | custom-call | flops 8000000000 | bytes 1000000 | tf_op jit(solution)/shard_map/pallas_call | solution.py:360
  121.1 1.6 collective-permute-start.44
  122.7 8.7 %shard_map.95.refs_0_ = bf16[288,256]{1,0:T(8,128)(2,1)S(1)} custom-call(s32[32]{0:T(128)S(1)} %stack.125.table, bf16[128,576]{1,0:T(8,128)(2,1)S(1)} %shard_map.93.query, bf16[288,256]{1,0:T(8,128)(2,1)S(1)} %kv.1.refs_0_, bf16[288,256]{1,0:T(8,128)(2,1)S(1)} %collective-permute-done.19.refs_1_, bf16[288,256]{1,0:T(8,128)(2,1)S(1)} %collective-permute-done.21.refs_2_, ...), custom_call_target="tpu_custom_call" | custom-call | flops 8000000000 | bytes 1000000 | tf_op jit(solution)/shard_map/pallas_call | solution.py:360
  133.7 4.1 %collective-permute-done.43.refs_2_ = bf16[288,256]{1,0:T(8,128)(2,1)S(1)} collective-permute-done((bf16[288,256]{1,0:T(8,128)(2,1)S(1)}, bf16[288,256]{1,0:T(8,128)(2,1)S(1)}, u32[]{:S(2)}, u32[]{:S(2)}) %collective-permute-start.43) | collective-permute-done | bytes 147488 | tf_op jit(solution)/shard_map/ppermute | solution.py:79
  139.1 1.8 %shard_map.103 = (bf16[3,144,256]{2,1,0:T(8,128)(2,1)S(1)}, bf16[3,144,256]{2,1,0:T(8,128)(2,1)S(1)}, bf16[3,144,256]{2,1,0:T(8,128)(2,1)S(1)}, bf16[3,144,256]{2,1,0:T(8,128)(2,1)S(1)}) custom-call(s32[1]{0:T(128)} %bitcast.30.place, bf16[288,256]{1,0:T(8,128)(2,1)S(1)} %shard_map.95.refs_0_, bf16[288,256]{1,0:T(8,128)(2,1)S(1)} %shard_map.99.refs_1_, ...), custom_call_target="tpu_custom_call" | custom-call | flops 3000000000 | bytes 1000000 | tf_op jit(solution)/shard_map/pallas_call | solution.py:428
  141.5 1.6 collective-permute-start.69
  143.2 1.3 shard_map.102
  144.5 2.7 %collective-permute-done.60.refs_9_ = bf16[1024,256]{1,0:T(8,128)(2,1)S(1)} collective-permute-done((bf16[1024,256]{1,0:T(8,128)(2,1)S(1)}, bf16[1024,256]{1,0:T(8,128)(2,1)S(1)}, u32[]{:S(2)}, u32[]{:S(2)}) %collective-permute-start.60) | collective-permute-done | bytes 524320 | tf_op jit(solution)/shard_map/ppermute | solution.py:88
  147.7 1.3 shard_map.101
  149.0 3.8 %collective-permute-done.53.refs_8_ = bf16[1024,256]{1,0:T(8,128)(2,1)S(1)} collective-permute-done((bf16[1024,256]{1,0:T(8,128)(2,1)S(1)}, bf16[1024,256]{1,0:T(8,128)(2,1)S(1)}, u32[]{:S(2)}, u32[]{:S(2)}) %collective-permute-start.53) | collective-permute-done | bytes 524320 | tf_op jit(solution)/shard_map/ppermute | solution.py:88
  152.8 3.7 %collective-permute-done.64.refs_1_ = bf16[2,144,256]{2,1,0:T(8,128)(2,1)S(1)} collective-permute-done((bf16[2,144,256]{2,1,0:T(8,128)(2,1)S(1)}, bf16[2,144,256]{2,1,0:T(8,128)(2,1)S(1)}, u32[]{:S(2)}, u32[]{:S(2)}) %collective-permute-start.64) | collective-permute-done | bytes 147488 | tf_op jit(solution)/shard_map/ppermute | solution.py:79
  159.6 1.5 shard_map.104.refs_4_
  161.1 1.5 collective-permute-start.54
  162.8 1.4 shard_map.105.refs_4_
  166.0 3.0 %collective-permute-done.63.refs_3_ = bf16[2,144,256]{2,1,0:T(8,128)(2,1)S(1)} collective-permute-done((bf16[2,144,256]{2,1,0:T(8,128)(2,1)S(1)}, bf16[2,144,256]{2,1,0:T(8,128)(2,1)S(1)}, u32[]{:S(2)}, u32[]{:S(2)}) %collective-permute-start.63) | collective-permute-done | bytes 147488 | tf_op jit(solution)/shard_map/ppermute | solution.py:84
  169.0 1.4 shard_map.106.refs_4_
  170.5 1.3 collective-permute-done.56.refs_3_
  (135 shorter events, 38.3 us)
Async XLA Ops:
  11.5 36.4 %collective-permute-start = (bf16[8,288,512]{2,1,0:T(8,128)(2,1)}, bf16[8,288,512]{2,1,0:T(8,128)(2,1)S(1)}, u32[]{:S(2)}, u32[]{:S(2)}) collective-permute-start(bf16[8,288,512]{2,1,0:T(8,128)(2,1)} %get-tuple-element.45), channel_id=1, source_target_pairs={{0,2},{2,0},{4,6},{6,4},{8,10},{10,8},{12,14},{14,12},{16,18},{18,... | collective-permute-start | bytes 7077896 | tf_op jit(solution)/shard_map/ppermute | solution.py:75
  14.9 6.7 %collective-permute-start.37 = (bf16[512,256]{1,0:T(8,128)(2,1)}, bf16[512,256]{1,0:T(8,128)(2,1)S(1)}, u32[]{:S(2)}, u32[]{:S(2)}) collective-permute-start(bf16[512,256]{1,0:T(8,128)(2,1)} %get-tuple-element.58.refs_0_), channel_id=1, source_target_pairs={{0,2},{2,0},{4,6},{6,4},{8,10},{10,8},{12,14},{14,12},{16,18},{18,... | collective-permute-start | bytes 786440 | tf_op jit(solution)/shard_map/ppermute | solution.py:75
  15.1 8.4 %collective-permute-start.34 = (bf16[512,256]{1,0:T(8,128)(2,1)}, bf16[512,256]{1,0:T(8,128)(2,1)S(1)}, u32[]{:S(2)}, u32[]{:S(2)}) collective-permute-start(bf16[512,256]{1,0:T(8,128)(2,1)} %get-tuple-element.58.refs_0_), channel_id=1, source_target_pairs={{0,8},{2,6},{8,16},{10,2},{16,24},{18,10},{24,28},{26,18},{28,20},... | collective-permute-start | bytes 786440 | tf_op jit(solution)/shard_map/ppermute | solution.py:88
  21.2 8.7 %collective-permute-start.12 = (bf16[512,256]{1,0:T(8,128)(2,1)S(1)}, bf16[512,256]{1,0:T(8,128)(2,1)S(1)}, u32[]{:S(2)}, u32[]{:S(2)}) collective-permute-start(bf16[512,256]{1,0:T(8,128)(2,1)S(1)} %collective-permute-done.11), channel_id=1, source_target_pairs={{0,8},{2,6},{8,16},{10,2},{16,24},{18,10},{24,28},{26,18},{28,20},... | collective-permute-start | bytes 786440 | tf_op jit(solution)/shard_map/ppermute | solution.py:88
  21.6 8.7 %collective-permute-start.4 = (bf16[512,256]{1,0:T(8,128)(2,1)}, bf16[512,256]{1,0:T(8,128)(2,1)S(1)}, u32[]{:S(2)}, u32[]{:S(2)}) collective-permute-start(bf16[512,256]{1,0:T(8,128)(2,1)} %get-tuple-element.46.refs_0_), channel_id=1, source_target_pairs={{0,2},{2,0},{4,6},{6,4},{8,10},{10,8},{12,14},{14,12},{16,18},{18,... | collective-permute-start | bytes 786440 | tf_op jit(solution)/shard_map/ppermute | solution.py:75
  23.5 8.1 %collective-permute-start.49 = (bf16[512,256]{1,0:T(8,128)(2,1)}, bf16[512,256]{1,0:T(8,128)(2,1)S(1)}, u32[]{:S(2)}, u32[]{:S(2)}) collective-permute-start(bf16[512,256]{1,0:T(8,128)(2,1)} %get-tuple-element.64), channel_id=1, source_target_pairs={{0,1},{1,0},{2,3},{3,2},{4,5},{5,4},{6,7},{7,6},{8,9},{9,8},{10,11... | collective-permute-start | bytes 786440 | tf_op jit(solution)/shard_map/ppermute | solution.py:79
  30.4 8.7 %collective-permute-start.1 = (bf16[512,256]{1,0:T(8,128)(2,1)}, bf16[512,256]{1,0:T(8,128)(2,1)S(1)}, u32[]{:S(2)}, u32[]{:S(2)}) collective-permute-start(bf16[512,256]{1,0:T(8,128)(2,1)} %get-tuple-element.46.refs_0_), channel_id=1, source_target_pairs={{0,8},{2,6},{8,16},{10,2},{16,24},{18,10},{24,28},{26,18},{28,20},... | collective-permute-start | bytes 786440 | tf_op jit(solution)/shard_map/ppermute | solution.py:88
  31.6 10.3 %collective-permute-start.38 = (bf16[512,256]{1,0:T(8,128)(2,1)S(1)}, bf16[512,256]{1,0:T(8,128)(2,1)S(1)}, u32[]{:S(2)}, u32[]{:S(2)}) collective-permute-start(bf16[512,256]{1,0:T(8,128)(2,1)S(1)} %collective-permute-done.37), channel_id=1, source_target_pairs={{0,8},{2,6},{8,16},{10,2},{16,24},{18,10},{24,28},{26,18},{28,20},... | collective-permute-start | bytes 786440 | tf_op jit(solution)/shard_map/ppermute | solution.py:88
  33.5 11.2 %collective-permute-start.17 = (bf16[512,256]{1,0:T(8,128)(2,1)S(1)}, bf16[512,256]{1,0:T(8,128)(2,1)S(1)}, u32[]{:S(2)}, u32[]{:S(2)}) collective-permute-start(bf16[512,256]{1,0:T(8,128)(2,1)S(1)} %collective-permute-done.15.refs_5_), channel_id=1, source_target_pairs={{0,8},{2,6},{8,16},{10,2},{16,24},{18,10},{24,28},{26,18},{28,20},... | collective-permute-start | bytes 786440 | tf_op jit(solution)/shard_map/ppermute | solution.py:88
  36.3 11.2 %collective-permute-start.16 = (bf16[512,256]{1,0:T(8,128)(2,1)S(1)}, bf16[512,256]{1,0:T(8,128)(2,1)S(1)}, u32[]{:S(2)}, u32[]{:S(2)}) collective-permute-start(bf16[512,256]{1,0:T(8,128)(2,1)S(1)} %collective-permute-done.14.refs_4_), channel_id=1, source_target_pairs={{0,8},{2,6},{8,16},{10,2},{16,24},{18,10},{24,28},{26,18},{28,20},... | collective-permute-start | bytes 786440 | tf_op jit(solution)/shard_map/ppermute | solution.py:88
  39.1 34.9 %collective-permute-start.57 = (bf16[1024,256]{1,0:T(8,128)(2,1)S(1)}, bf16[1024,256]{1,0:T(8,128)(2,1)S(1)}, u32[]{:S(2)}, u32[]{:S(2)}) collective-permute-start(bf16[1024,256]{1,0:T(8,128)(2,1)S(1)} %constant_dynamic-update-slice_fusion.refs_8_), channel_id=1, source_target_pairs={{0,2},{2,0},{4,6},{6,4},{8,10},{10,8},{12,14},{14,12},{16,18},{18,... | collective-permute-start | bytes 1572872 | tf_op jit(solution)/shard_map/ppermute | solution.py:75
  41.9 10.5 %collective-permute-start.35 = (bf16[512,256]{1,0:T(8,128)(2,1)S(1)}, bf16[512,256]{1,0:T(8,128)(2,1)S(1)}, u32[]{:S(2)}, u32[]{:S(2)}) collective-permute-start(bf16[512,256]{1,0:T(8,128)(2,1)S(1)} %collective-permute-done.34.refs_1_), channel_id=1, source_target_pairs={{0,8},{2,6},{8,16},{10,2},{16,24},{18,10},{24,28},{26,18},{28,20},... | collective-permute-start | bytes 786440 | tf_op jit(solution)/shard_map/ppermute | solution.py:88
  44.7 8.4 %collective-permute-start.5 = (bf16[512,256]{1,0:T(8,128)(2,1)S(1)}, bf16[512,256]{1,0:T(8,128)(2,1)S(1)}, u32[]{:S(2)}, u32[]{:S(2)}) collective-permute-start(bf16[512,256]{1,0:T(8,128)(2,1)S(1)} %collective-permute-done.4), channel_id=1, source_target_pairs={{0,8},{2,6},{8,16},{10,2},{16,24},{18,10},{24,28},{26,18},{28,20},... | collective-permute-start | bytes 786440 | tf_op jit(solution)/shard_map/ppermute | solution.py:88
  47.5 8.4 %collective-permute-start.2 = (bf16[512,256]{1,0:T(8,128)(2,1)S(1)}, bf16[512,256]{1,0:T(8,128)(2,1)S(1)}, u32[]{:S(2)}, u32[]{:S(2)}) collective-permute-start(bf16[512,256]{1,0:T(8,128)(2,1)S(1)} %collective-permute-done.1.refs_1_), channel_id=1, source_target_pairs={{0,8},{2,6},{8,16},{10,2},{16,24},{18,10},{24,28},{26,18},{28,20},... | collective-permute-start | bytes 786440 | tf_op jit(solution)/shard_map/ppermute | solution.py:88
  48.0 10.8 %collective-permute-start.39 = (bf16[512,256]{1,0:T(8,128)(2,1)S(1)}, bf16[512,256]{1,0:T(8,128)(2,1)S(1)}, u32[]{:S(2)}, u32[]{:S(2)}) collective-permute-start(bf16[512,256]{1,0:T(8,128)(2,1)S(1)} %collective-permute-done.38.refs_2_), channel_id=1, source_target_pairs={{0,8},{2,6},{8,16},{10,2},{16,24},{18,10},{24,28},{26,18},{28,20},... | collective-permute-start | bytes 786440 | tf_op jit(solution)/shard_map/ppermute | solution.py:88
  52.4 22.0 %collective-permute-start.50 = (bf16[1024,256]{1,0:T(8,128)(2,1)S(1)}, bf16[1024,256]{1,0:T(8,128)(2,1)S(1)}, u32[]{:S(2)}, u32[]{:S(2)}) collective-permute-start(bf16[1024,256]{1,0:T(8,128)(2,1)S(1)} %constant_dynamic-update-slice_fusion.refs_8_), channel_id=1, source_target_pairs={{0,8},{2,6},{8,16},{10,2},{16,24},{18,10},{24,28},{26,18},{28,20},... | collective-permute-start | bytes 1572872 | tf_op jit(solution)/shard_map/ppermute | solution.py:88
  53.1 14.0 %collective-permute-start.36 = (bf16[512,256]{1,0:T(8,128)(2,1)S(1)}, bf16[512,256]{1,0:T(8,128)(2,1)S(1)}, u32[]{:S(2)}, u32[]{:S(2)}) collective-permute-start(bf16[512,256]{1,0:T(8,128)(2,1)S(1)} %collective-permute-done.35.refs_3_), channel_id=1, source_target_pairs={{0,8},{2,6},{8,16},{10,2},{16,24},{18,10},{24,28},{26,18},{28,20},... | collective-permute-start | bytes 786440 | tf_op jit(solution)/shard_map/ppermute | solution.py:88
  55.9 14.0 %collective-permute-start.6 = (bf16[512,256]{1,0:T(8,128)(2,1)S(1)}, bf16[512,256]{1,0:T(8,128)(2,1)S(1)}, u32[]{:S(2)}, u32[]{:S(2)}) collective-permute-start(bf16[512,256]{1,0:T(8,128)(2,1)S(1)} %collective-permute-done.5.refs_2_), channel_id=1, source_target_pairs={{0,8},{2,6},{8,16},{10,2},{16,24},{18,10},{24,28},{26,18},{28,20},... | collective-permute-start | bytes 786440 | tf_op jit(solution)/shard_map/ppermute | solution.py:88
  58.7 11.7 %collective-permute-start.18 = (f32[288,256]{1,0:T(8,128)S(1)}, f32[288,256]{1,0:T(8,128)S(1)}, u32[]{:S(2)}, u32[]{:S(2)}) collective-permute-start(f32[288,256]{1,0:T(8,128)S(1)} %get-tuple-element.56), channel_id=1, source_target_pairs={{0,2},{2,0},{4,6},{6,4},{8,10},{10,8},{12,14},{14,12},{16,18},{18,... | collective-permute-start | bytes 884744 | tf_op jit(solution)/shard_map/ppermute | solution.py:75
  70.0 9.2 %collective-permute-start.40 = (bf16[512,256]{1,0:T(8,128)(2,1)S(1)}, bf16[512,256]{1,0:T(8,128)(2,1)S(1)}, u32[]{:S(2)}, u32[]{:S(2)}) collective-permute-start(bf16[512,256]{1,0:T(8,128)(2,1)S(1)} %collective-permute-done.39.refs_4_), channel_id=1, source_target_pairs={{0,8},{2,6},{8,16},{10,2},{16,24},{18,10},{24,28},{26,18},{28,20},... | collective-permute-start | bytes 786440 | tf_op jit(solution)/shard_map/ppermute | solution.py:88
  70.4 8.7 %collective-permute-start.41 = (bf16[512,256]{1,0:T(8,128)(2,1)S(1)}, bf16[512,256]{1,0:T(8,128)(2,1)S(1)}, u32[]{:S(2)}, u32[]{:S(2)}) collective-permute-start(bf16[512,256]{1,0:T(8,128)(2,1)S(1)} %collective-permute-done.36.refs_0_), channel_id=1, source_target_pairs={{0,8},{2,6},{8,16},{10,2},{16,24},{18,10},{24,28},{26,18},{28,20},... | collective-permute-start | bytes 786440 | tf_op jit(solution)/shard_map/ppermute | solution.py:88
  73.5 13.3 %collective-permute-start.7 = (bf16[512,256]{1,0:T(8,128)(2,1)S(1)}, bf16[512,256]{1,0:T(8,128)(2,1)S(1)}, u32[]{:S(2)}, u32[]{:S(2)}) collective-permute-start(bf16[512,256]{1,0:T(8,128)(2,1)S(1)} %collective-permute-done.6.refs_4_), channel_id=1, source_target_pairs={{0,8},{2,6},{8,16},{10,2},{16,24},{18,10},{24,28},{26,18},{28,20},... | collective-permute-start | bytes 786440 | tf_op jit(solution)/shard_map/ppermute | solution.py:88
  74.0 12.4 %collective-permute-start.8 = (bf16[512,256]{1,0:T(8,128)(2,1)S(1)}, bf16[512,256]{1,0:T(8,128)(2,1)S(1)}, u32[]{:S(2)}, u32[]{:S(2)}) collective-permute-start(bf16[512,256]{1,0:T(8,128)(2,1)S(1)} %collective-permute-done.3.refs_0_), channel_id=1, source_target_pairs={{0,8},{2,6},{8,16},{10,2},{16,24},{18,10},{24,28},{26,18},{28,20},... | collective-permute-start | bytes 786440 | tf_op jit(solution)/shard_map/ppermute | solution.py:88
  74.5 19.6 %collective-permute-start.58 = (bf16[1024,256]{1,0:T(8,128)(2,1)S(1)}, bf16[1024,256]{1,0:T(8,128)(2,1)S(1)}, u32[]{:S(2)}, u32[]{:S(2)}) collective-permute-start(bf16[1024,256]{1,0:T(8,128)(2,1)S(1)} %collective-permute-done.57), channel_id=1, source_target_pairs={{0,8},{2,6},{8,16},{10,2},{16,24},{18,10},{24,28},{26,18},{28,20},... | collective-permute-start | bytes 1572872 | tf_op jit(solution)/shard_map/ppermute | solution.py:88
  79.2 7.7 %collective-permute-start.20 = (bf16[288,256]{1,0:T(8,128)(2,1)S(1)}, bf16[288,256]{1,0:T(8,128)(2,1)S(1)}, u32[]{:S(2)}, u32[]{:S(2)}) collective-permute-start(bf16[288,256]{1,0:T(8,128)(2,1)S(1)} %kv.1.refs_0_), channel_id=1, source_target_pairs={{0,2},{2,0},{4,6},{6,4},{8,10},{10,8},{12,14},{14,12},{16,18},{18,... | collective-permute-start | bytes 442376 | tf_op jit(solution)/shard_map/ppermute | solution.py:75
  79.2 9.3 %collective-permute-start.19 = (bf16[288,256]{1,0:T(8,128)(2,1)S(1)}, bf16[288,256]{1,0:T(8,128)(2,1)S(1)}, u32[]{:S(2)}, u32[]{:S(2)}) collective-permute-start(bf16[288,256]{1,0:T(8,128)(2,1)S(1)} %kv.1.refs_0_), channel_id=1, source_target_pairs={{0,4},{2,10},{8,0},{10,18},{16,8},{18,26},{24,16},{26,30},{28,24},... | collective-permute-start | bytes 442376 | tf_op jit(solution)/shard_map/ppermute | solution.py:88
  86.4 17.6 %collective-permute-start.51 = (bf16[1024,256]{1,0:T(8,128)(2,1)S(1)}, bf16[1024,256]{1,0:T(8,128)(2,1)S(1)}, u32[]{:S(2)}, u32[]{:S(2)}) collective-permute-start(bf16[1024,256]{1,0:T(8,128)(2,1)S(1)} %collective-permute-done.50.refs_9_), channel_id=1, source_target_pairs={{0,8},{2,6},{8,16},{10,2},{16,24},{18,10},{24,28},{26,18},{28,20},... | collective-permute-start | bytes 1572872 | tf_op jit(solution)/shard_map/ppermute | solution.py:88
  86.8 17.1 %collective-permute-start.42 = (f32[288,256]{1,0:T(8,128)S(1)}, f32[288,256]{1,0:T(8,128)S(1)}, u32[]{:S(2)}, u32[]{:S(2)}) collective-permute-start(f32[288,256]{1,0:T(8,128)S(1)} %get-tuple-element.62), channel_id=1, source_target_pairs={{0,2},{2,0},{4,6},{6,4},{8,10},{10,8},{12,14},{14,12},{16,18},{18,... | collective-permute-start | bytes 884744 | tf_op jit(solution)/shard_map/ppermute | solution.py:75
  86.8 7.2 %collective-permute-start.21 = (bf16[288,256]{1,0:T(8,128)(2,1)S(1)}, bf16[288,256]{1,0:T(8,128)(2,1)S(1)}, u32[]{:S(2)}, u32[]{:S(2)}) collective-permute-start(bf16[288,256]{1,0:T(8,128)(2,1)S(1)} %collective-permute-done.20.refs_8_), channel_id=1, source_target_pairs={{0,4},{2,10},{8,0},{10,18},{16,8},{18,26},{24,16},{26,30},{28,24},... | collective-permute-start | bytes 442376 | tf_op jit(solution)/shard_map/ppermute | solution.py:88
  88.5 8.3 %collective-permute-start.22 = (bf16[288,256]{1,0:T(8,128)(2,1)S(1)}, bf16[288,256]{1,0:T(8,128)(2,1)S(1)}, u32[]{:S(2)}, u32[]{:S(2)}) collective-permute-start(bf16[288,256]{1,0:T(8,128)(2,1)S(1)} %collective-permute-done.19.refs_1_), channel_id=1, source_target_pairs={{0,4},{2,10},{8,0},{10,18},{16,8},{18,26},{24,16},{26,30},{28,24},... | collective-permute-start | bytes 442376 | tf_op jit(solution)/shard_map/ppermute | solution.py:88
  94.0 11.6 %collective-permute-start.9 = (f32[288,256]{1,0:T(8,128)S(1)}, f32[288,256]{1,0:T(8,128)S(1)}, u32[]{:S(2)}, u32[]{:S(2)}) collective-permute-start(f32[288,256]{1,0:T(8,128)S(1)} %get-tuple-element.50), channel_id=1, source_target_pairs={{0,2},{2,0},{4,6},{6,4},{8,10},{10,8},{12,14},{14,12},{16,18},{18,... | collective-permute-start | bytes 884744 | tf_op jit(solution)/shard_map/ppermute | solution.py:75
  94.0 10.4 %collective-permute-start.23 = (bf16[288,256]{1,0:T(8,128)(2,1)S(1)}, bf16[288,256]{1,0:T(8,128)(2,1)S(1)}, u32[]{:S(2)}, u32[]{:S(2)}) collective-permute-start(bf16[288,256]{1,0:T(8,128)(2,1)S(1)} %collective-permute-done.21.refs_2_), channel_id=1, source_target_pairs={{0,4},{2,10},{8,0},{10,18},{16,8},{18,26},{24,16},{26,30},{28,24},... | collective-permute-start | bytes 442376 | tf_op jit(solution)/shard_map/ppermute | solution.py:88
  96.8 8.2 %collective-permute-start.24 = (bf16[288,256]{1,0:T(8,128)(2,1)S(1)}, bf16[288,256]{1,0:T(8,128)(2,1)S(1)}, u32[]{:S(2)}, u32[]{:S(2)}) collective-permute-start(bf16[288,256]{1,0:T(8,128)(2,1)S(1)} %collective-permute-done.22.refs_3_), channel_id=1, source_target_pairs={{0,4},{2,10},{8,0},{10,18},{16,8},{18,26},{24,16},{26,30},{28,24},... | collective-permute-start | bytes 442376 | tf_op jit(solution)/shard_map/ppermute | solution.py:88
  111.4 21.7 %collective-permute-start.59 = (bf16[1024,256]{1,0:T(8,128)(2,1)S(1)}, bf16[1024,256]{1,0:T(8,128)(2,1)S(1)}, u32[]{:S(2)}, u32[]{:S(2)}) collective-permute-start(bf16[1024,256]{1,0:T(8,128)(2,1)S(1)} %collective-permute-done.58.refs_10_), channel_id=1, source_target_pairs={{0,8},{2,6},{8,16},{10,2},{16,24},{18,10},{24,28},{26,18},{28,20},... | collective-permute-start | bytes 1572872 | tf_op jit(solution)/shard_map/ppermute | solution.py:88
  111.9 26.1 %collective-permute-start.52 = (bf16[1024,256]{1,0:T(8,128)(2,1)S(1)}, bf16[1024,256]{1,0:T(8,128)(2,1)S(1)}, u32[]{:S(2)}, u32[]{:S(2)}) collective-permute-start(bf16[1024,256]{1,0:T(8,128)(2,1)S(1)} %collective-permute-done.51.refs_8_), channel_id=1, source_target_pairs={{0,8},{2,6},{8,16},{10,2},{16,24},{18,10},{24,28},{26,18},{28,20},... | collective-permute-start | bytes 1572872 | tf_op jit(solution)/shard_map/ppermute | solution.py:88
  121.1 12.1 %collective-permute-start.44 = (bf16[288,256]{1,0:T(8,128)(2,1)S(1)}, bf16[288,256]{1,0:T(8,128)(2,1)S(1)}, u32[]{:S(2)}, u32[]{:S(2)}) collective-permute-start(bf16[288,256]{1,0:T(8,128)(2,1)S(1)} %shard_map.99.refs_1_), channel_id=1, source_target_pairs={{0,1},{1,0},{2,3},{3,2},{4,5},{5,4},{6,7},{7,6},{8,9},{9,8},{10,11... | collective-permute-start | bytes 442376 | tf_op jit(solution)/shard_map/ppermute | solution.py:79
  138.0 9.2 %collective-permute-start.60 = (bf16[1024,256]{1,0:T(8,128)(2,1)S(1)}, bf16[1024,256]{1,0:T(8,128)(2,1)S(1)}, u32[]{:S(2)}, u32[]{:S(2)}) collective-permute-start(bf16[1024,256]{1,0:T(8,128)(2,1)S(1)} %collective-permute-done.59.refs_9_), channel_id=1, source_target_pairs={{0,8},{2,6},{8,16},{10,2},{16,24},{18,10},{24,28},{26,18},{28,20},... | collective-permute-start | bytes 1572872 | tf_op jit(solution)/shard_map/ppermute | solution.py:88
  138.0 14.8 %collective-permute-start.53 = (bf16[1024,256]{1,0:T(8,128)(2,1)S(1)}, bf16[1024,256]{1,0:T(8,128)(2,1)S(1)}, u32[]{:S(2)}, u32[]{:S(2)}) collective-permute-start(bf16[1024,256]{1,0:T(8,128)(2,1)S(1)} %collective-permute-done.52.refs_8_), channel_id=1, source_target_pairs={{0,8},{2,6},{8,16},{10,2},{16,24},{18,10},{24,28},{26,18},{28,20},... | collective-permute-start | bytes 1572872 | tf_op jit(solution)/shard_map/ppermute | solution.py:88
  141.0 16.4 %collective-permute-start.67 = (bf16[3,144,256]{2,1,0:T(8,128)(2,1)S(1)}, bf16[3,144,256]{2,1,0:T(8,128)(2,1)S(1)}, u32[]{:S(2)}, u32[]{:S(2)}) collective-permute-start(bf16[3,144,256]{2,1,0:T(8,128)(2,1)S(1)} %get-tuple-element.78), channel_id=1, source_target_pairs={{0,1},{1,0},{2,3},{3,2},{4,5},{5,4},{6,7},{7,6},{8,9},{9,8},{10,11... | collective-permute-start | bytes 663560 | tf_op jit(solution)/shard_map/ppermute | solution.py:79
  141.5 17.0 %collective-permute-start.68 = (bf16[3,144,256]{2,1,0:T(8,128)(2,1)S(1)}, bf16[3,144,256]{2,1,0:T(8,128)(2,1)S(1)}, u32[]{:S(2)}, u32[]{:S(2)}) collective-permute-start(bf16[3,144,256]{2,1,0:T(8,128)(2,1)S(1)} %get-tuple-element.79), channel_id=1, source_target_pairs={{0,2},{2,0},{4,6},{6,4},{8,10},{10,8},{12,14},{14,12},{16,18},{18,... | collective-permute-start | bytes 663560 | tf_op jit(solution)/shard_map/ppermute | solution.py:75
  141.5 17.8 %collective-permute-start.69 = (bf16[3,144,256]{2,1,0:T(8,128)(2,1)S(1)}, bf16[3,144,256]{2,1,0:T(8,128)(2,1)S(1)}, u32[]{:S(2)}, u32[]{:S(2)}) collective-permute-start(bf16[3,144,256]{2,1,0:T(8,128)(2,1)S(1)} %get-tuple-element.80), channel_id=1, source_target_pairs={{0,3},{1,2},{2,1},{3,0},{4,7},{5,6},{6,5},{7,4},{8,11},{9,10},{10,... | collective-permute-start | bytes 663560 | tf_op jit(solution)/shard_map/ppermute | solution.py:84
  147.2 9.3 %collective-permute-start.64 = (bf16[2,144,256]{2,1,0:T(8,128)(2,1)S(1)}, bf16[2,144,256]{2,1,0:T(8,128)(2,1)S(1)}, u32[]{:S(2)}, u32[]{:S(2)}) collective-permute-start(bf16[2,144,256]{2,1,0:T(8,128)(2,1)S(1)} %get-tuple-element.74), channel_id=1, source_target_pairs={{0,1},{1,0},{2,3},{3,2},{4,5},{5,4},{6,7},{7,6},{8,9},{9,8},{10,11... | collective-permute-start | bytes 442376 | tf_op jit(solution)/shard_map/ppermute | solution.py:79
  152.8 8.3 %collective-permute-start.65 = (bf16[2,144,256]{2,1,0:T(8,128)(2,1)S(1)}, bf16[2,144,256]{2,1,0:T(8,128)(2,1)S(1)}, u32[]{:S(2)}, u32[]{:S(2)}) collective-permute-start(bf16[2,144,256]{2,1,0:T(8,128)(2,1)S(1)} %get-tuple-element.75), channel_id=1, source_target_pairs={{0,2},{2,0},{4,6},{6,4},{8,10},{10,8},{12,14},{14,12},{16,18},{18,... | collective-permute-start | bytes 442376 | tf_op jit(solution)/shard_map/ppermute | solution.py:75
  157.4 7.7 %collective-permute-start.61 = (bf16[2,144,256]{2,1,0:T(8,128)(2,1)S(1)}, bf16[2,144,256]{2,1,0:T(8,128)(2,1)S(1)}, u32[]{:S(2)}, u32[]{:S(2)}) collective-permute-start(bf16[2,144,256]{2,1,0:T(8,128)(2,1)S(1)} %get-tuple-element.70), channel_id=1, source_target_pairs={{0,1},{1,0},{2,3},{3,2},{4,5},{5,4},{6,7},{7,6},{8,9},{9,8},{10,11... | collective-permute-start | bytes 442376 | tf_op jit(solution)/shard_map/ppermute | solution.py:79
  158.5 7.5 %collective-permute-start.62 = (bf16[2,144,256]{2,1,0:T(8,128)(2,1)S(1)}, bf16[2,144,256]{2,1,0:T(8,128)(2,1)S(1)}, u32[]{:S(2)}, u32[]{:S(2)}) collective-permute-start(bf16[2,144,256]{2,1,0:T(8,128)(2,1)S(1)} %get-tuple-element.71), channel_id=1, source_target_pairs={{0,2},{2,0},{4,6},{6,4},{8,10},{10,8},{12,14},{14,12},{16,18},{18,... | collective-permute-start | bytes 442376 | tf_op jit(solution)/shard_map/ppermute | solution.py:75
  159.3 9.7 %collective-permute-start.63 = (bf16[2,144,256]{2,1,0:T(8,128)(2,1)S(1)}, bf16[2,144,256]{2,1,0:T(8,128)(2,1)S(1)}, u32[]{:S(2)}, u32[]{:S(2)}) collective-permute-start(bf16[2,144,256]{2,1,0:T(8,128)(2,1)S(1)} %get-tuple-element.72), channel_id=1, source_target_pairs={{0,3},{1,2},{2,1},{3,0},{4,7},{5,6},{6,5},{7,4},{8,11},{9,10},{10,... | collective-permute-start | bytes 442376 | tf_op jit(solution)/shard_map/ppermute | solution.py:84
  161.1 9.3 %collective-permute-start.54 = (bf16[1,144,256]{2,1,0:T(8,128)(2,1)S(1)}, bf16[1,144,256]{2,1,0:T(8,128)(2,1)S(1)}, u32[]{:S(2)}, u32[]{:S(2)}) collective-permute-start(bf16[1,144,256]{2,1,0:T(8,128)(2,1)S(1)} %get-tuple-element.66), channel_id=1, source_target_pairs={{0,1},{1,0},{2,3},{3,2},{4,5},{5,4},{6,7},{7,6},{8,9},{9,8},{10,11... | collective-permute-start | bytes 221192 | tf_op jit(solution)/shard_map/ppermute | solution.py:79
  162.7 7.8 %collective-permute-start.55 = (bf16[1,144,256]{2,1,0:T(8,128)(2,1)S(1)}, bf16[1,144,256]{2,1,0:T(8,128)(2,1)S(1)}, u32[]{:S(2)}, u32[]{:S(2)}) collective-permute-start(bf16[1,144,256]{2,1,0:T(8,128)(2,1)S(1)} %get-tuple-element.67), channel_id=1, source_target_pairs={{0,2},{2,0},{4,6},{6,4},{8,10},{10,8},{12,14},{14,12},{16,18},{18,... | collective-permute-start | bytes 221192 | tf_op jit(solution)/shard_map/ppermute | solution.py:75
  (28 other events, 139.2 us)

commit v2 on v1

--- a/solution.py
+++ b/solution.py
@@ -88,11 +88,11 @@
     return lax.ppermute(value, "seq", ring_perm(seq_size, turn))
 
 
-def ring_gather(own, other, seq_size, turn=1):
+def ring_gather(own, other, seq_size, turn=1, begin=1):
     half = seq_size // 4
-    held = [own]
+    held = [own] if begin == 1 else [own, other]
     first, second = own, other
-    for step in range(1, half + 1):
+    for step in range(begin, half + 1):
         first = pass_on(first, seq_size, turn)
         held.append(first)
         if step < half:
@@ -101,24 +101,10 @@
     return held
 
 
-def prepare_kernel(place, w_key, w_value, w_query, w_out, pair, *refs):
-    parts, (near, far, sems) = refs[:-3], refs[-3:]
-    columns = near.shape[1]
-    width = parts[0].shape[1]
-    here = pl.multiple_of(place[0] * columns, 128)
-    there = pl.multiple_of((1 - place[0]) * columns, 128)
-    copies = [
-        (w_key, pair.at[:, :HEAD_DIM]),
-        (w_value, pair.at[:, HEAD_DIM:]),
-        (w_out.at[:, pl.ds(here, columns)], near),
-        (w_out.at[:, pl.ds(there, columns)], far),
-    ]
-    for index, part in enumerate(parts):
-        span = slice(index * width, (index + 1) * width)
-        copies.append((w_query.at[:, span], part))
+def copy_all(pairs, sems):
     copies = [
         pltpu.make_async_copy(old, new, sems.at[index])
-        for index, (old, new) in enumerate(copies)
+        for index, (old, new) in enumerate(pairs)
     ]
     for copy in copies:
         copy.start()
@@ -126,19 +112,62 @@
         copy.wait()
 
 
-def prepare(place, w_key, w_value, w_query, w_out, groups):
-    depth, width = w_query.shape
-    shapes = [(depth, 2 * HEAD_DIM)] + [(depth, width // groups)] * groups
-    shapes += [(w_out.shape[0], w_out.shape[1] // 2)] * 2
-    return pl.pallas_call(
-        prepare_kernel,
-        out_shape=[jax.ShapeDtypeStruct(one, jnp.bfloat16) for one in shapes],
-        in_specs=[SMEM] + [HBM] * 4,
-        out_specs=[VMEM] * len(shapes),
-        scratch_shapes=[pltpu.SemaphoreType.DMA((4 + groups,))],
+def join_kernel(w_key, w_value, pair, sems):
+    copy_all(
+        [(w_key, pair.at[:, :HEAD_DIM]), (w_value, pair.at[:, HEAD_DIM:])], sems
+    )
+
+
+def join(w_key, w_value):
+    shape = (w_key.shape[0], 2 * HEAD_DIM)
+    return pl.pallas_call(
+        join_kernel,
+        out_shape=jax.ShapeDtypeStruct(shape, jnp.bfloat16),
+        in_specs=[HBM] * 2,
+        out_specs=VMEM,
+        scratch_shapes=[pltpu.SemaphoreType.DMA((2,))],
         cost_estimate=estimate(1),
         name="prep",
-    )(place, w_key, w_value, w_query, w_out)
+    )(w_key, w_value)
+
+
+def halves_kernel(value, *parts):
+    width = parts[0].shape[1]
+    for index, part in enumerate(parts):
+        part[...] = value[:, index * width : (index + 1) * width]
+
+
+def halves(value, groups):
+    shape = (value.shape[0], value.shape[1] // groups)
+    return pl.pallas_call(
+        halves_kernel,
+        out_shape=[jax.ShapeDtypeStruct(shape, jnp.bfloat16)] * groups,
+        in_specs=[VMEM],
+        out_specs=[VMEM] * groups,
+        compiler_params=GRANT,
+        cost_estimate=estimate(1),
+    )(value)
+
+
+def cut_kernel(place, own, got, near, far):
+    depth, columns = own.shape[0], near.shape[1]
+    for side, target in ((place[0], near), (1 - place[0], far)):
+        span = pl.ds(pl.multiple_of(side * columns, 128), columns)
+        target[:depth] = own[:, span]
+        target[depth:] = got[:, span]
+
+
+def cut(place, own, got):
+    shape = jax.ShapeDtypeStruct((2 * own.shape[0], own.shape[1] // 2), jnp.bfloat16)
+    return pl.pallas_call(
+        cut_kernel,
+        out_shape=(shape, shape),
+        in_specs=[SMEM, VMEM, VMEM],
+        out_specs=(VMEM, VMEM),
+        compiler_params=GRANT,
+        cost_estimate=estimate(1),
+        name="cut",
+    )(place, own, got)
 
 
 def norm_kernel(table, hidden, gain, mine, other):
@@ -183,7 +212,7 @@
     )(table, hidden, gain)
 
 
-def project_kernel(start, count, mine, other, *refs):
+def project_kernel(start, count, group, mine, other, *refs):
     weights = refs[:count]
     keep, send = refs[-2:]
     carried = refs[count:-2]
@@ -192,17 +221,19 @@
     ):
         total = None if old is None else old[...]
         for slot in range(count):
-            term = dot(source[start + slot], weights[slot][...])
+            columns = target.shape[1]
+            at = group * columns if weights[slot].shape[1] > columns else 0
+            term = dot(source[start + slot], weights[slot][:, at : at + columns])
             total = term if total is None else total + term
         target[...] = total
 
 
-def project(mine, other, weights, start, carried):
+def project(mine, other, weights, columns, group, start, carried):
     count = len(weights)
-    shape = (mine.shape[1], weights[0].shape[1])
+    shape = (mine.shape[1], columns)
     shape = jax.ShapeDtypeStruct(shape, jnp.float32)
     return pl.pallas_call(
-        functools.partial(project_kernel, start, count),
+        functools.partial(project_kernel, start, count, group),
         out_shape=(shape, shape),
         in_specs=[VMEM] * (2 + count + len(carried)),
         out_specs=(VMEM, VMEM),
@@ -259,26 +290,19 @@
 
 def attend_kernel(count, offset, table, query, *refs):
     sources = refs[:count]
-    out, pairs, sems, even, odd, high, weight, mixture = refs[count:]
+    out, pairs, even, odd, high, weight, mixture = refs[count:]
     rows = sources[0].shape[0]
     lanes = query.shape[1]
     shard = table[0]
     factor = HEAD_DIM ** (-0.5) * LOG2E
 
-    def copy(slot, at):
-        pltpu.make_async_copy(sources[slot], pairs.at[at], sems.at[at]).start()
-
-    def wait(at):
-        pltpu.make_async_copy(pairs.at[at], pairs.at[at], sems.at[at]).wait()
-
-    copy(0, 0)
     needed = jnp.int32(0)
     for slot in range(1, count):
         seen = table[offset + slot] < shard
 
         @pl.when(seen)
         def _(slot=slot, needed=needed):
-            copy(slot, needed + 1)
+            pairs[pl.ds(needed, 1)] = sources[slot][...][None]
 
         needed = needed + seen.astype(jnp.int32)
 
@@ -303,38 +327,27 @@
         weight[...] = added
         mixture[...] = mixed
 
-    wait(0)
-    scores = dot(keys_of(0, 1), query[...])
+    scores = dot(sources[0][:, :HEAD_DIM], query[...])
     row = lax.broadcasted_iota(jnp.int32, scores.shape, 0)
     lane = lax.rem(lax.broadcasted_iota(jnp.int32, (1, lanes), 1), rows)
-    update(jnp.where(row <= lane, scores, -jnp.inf), values_of(0, 1), True)
+    update(jnp.where(row <= lane, scores, -jnp.inf), sources[0][:, HEAD_DIM:].T, True)
 
     single = lax.rem(needed, 2)
 
     @pl.when(single == 1)
     def _():
-        wait(1)
-        update(dot(keys_of(1, 1), query[...]), values_of(1, 1), False)
-
-    begin = 1 + single
+        update(dot(keys_of(0, 1), query[...]), values_of(0, 1), False)
+
+    begin = single
     turns = needed // 2
 
-    def arrive(turn):
-        wait(begin + 2 * turn)
-        wait(begin + 2 * turn + 1)
-
     def step(turn, here, there):
-        @pl.when(turn + 1 < turns)
-        def _():
-            arrive(turn + 1)
-
         at = begin + 2 * jnp.minimum(turn + 1, turns - 1)
         there[...] = dot(keys_of(at, 2), query[...])
         update(here[...], values_of(begin + 2 * turn, 2), False)
 
     @pl.when(turns > 0)
     def _():
-        arrive(0)
         even[...] = dot(keys_of(begin, 2), query[...])
 
         @pl.loop(0, (turns + 1) // 2)
@@ -360,11 +373,10 @@
     return pl.pallas_call(
         functools.partial(attend_kernel, count, offset),
         out_shape=jax.ShapeDtypeStruct(shape, jnp.bfloat16),
-        in_specs=[SMEM, VMEM] + [HBM] * count,
+        in_specs=[SMEM, VMEM] + [VMEM] * count,
         out_specs=VMEM,
         scratch_shapes=[
             pltpu.VMEM((count, rows, 2 * HEAD_DIM), jnp.bfloat16),
-            pltpu.SemaphoreType.DMA((count,)),
             pltpu.VMEM((2 * rows, lanes), jnp.float32),
             pltpu.VMEM((2 * rows, lanes), jnp.float32),
             pltpu.VMEM((1, lanes), jnp.float32),
@@ -376,66 +388,42 @@
     )(table, query, *sources)
 
 
-def out_kernel(pieces, groups, place, *refs):
+def out_kernel(pieces, groups, share, place, *refs):
     weights = refs[4 * groups : 4 * groups + pieces]
-    keep, keep_other, send, send_other, source, block, sems, weight_sems = refs[-8:]
-    rows = refs[0].shape[0] // 2
-    width = refs[0].shape[1]
+    targets, source = refs[4 * groups + pieces : -1], refs[-1]
+    rows, width = refs[0].shape[0] // 2, refs[0].shape[1]
     depth = width * groups
-    half = place[0]
-    near = pl.ds(pl.multiple_of(half * rows, 16), rows)
-    far = pl.ds(pl.multiple_of((1 - half) * rows, 16), rows)
-    copies = []
+    near = pl.ds(pl.multiple_of(place[0] * rows, 16), rows)
+    far = pl.ds(pl.multiple_of((1 - place[0]) * rows, 16), rows)
     for side in range(2):
         for index in range(groups):
             own, other = refs[side * groups + index], refs[(2 + side) * groups + index]
+            columns = slice(index * width, (index + 1) * width)
             for part, (ref, span) in enumerate(
-                ((own, near), (other, near), (own, far), (other, far))
+                ((own, near), (other, near), (own, far), (other, far))[: 2 * share]
             ):
-                place_at = (side, pl.ds(part * rows, rows), pl.ds(index * width, width))
-                copies.append(
-                    pltpu.make_async_copy(
-                        ref.at[span], source.at[place_at], sems.at[side, index, part]
-                    )
-                )
-    for copy in copies:
-        copy.start()
+                source[side, part * rows : (part + 1) * rows, columns] = ref[span, :]
     for piece in range(pieces):
-        pltpu.make_async_copy(
-            weights[piece], block.at[piece], weight_sems.at[piece]
-        ).start()
-    for copy in copies:
-        copy.wait()
-
-    @pl.loop(0, pieces)
-    def _(piece):
-        pltpu.make_async_copy(
-            block.at[piece], block.at[piece], weight_sems.at[piece]
-        ).wait()
-        one = dot(source[0], block[piece, :depth]).astype(jnp.bfloat16)
-        two = dot(source[1], block[piece, depth:]).astype(jnp.bfloat16)
+        block = weights[piece]
+        one = dot(source[0], block[:depth]).astype(jnp.bfloat16)
+        two = dot(source[1], block[depth:]).astype(jnp.bfloat16)
         value = (one.astype(jnp.float32) + two.astype(jnp.float32)).astype(jnp.bfloat16)
-        for part, target in enumerate((keep, keep_other, send, send_other)):
+        for part, target in enumerate(targets):
             target[piece] = value[part * rows : (part + 1) * rows]
 
 
-def project_out(place, attended, weights):
+def project_out(place, attended, weights, share):
     pieces = len(weights)
     groups = len(attended) // 4
     rows, depth = attended[0].shape[0], weights[0].shape[0] // 2
     columns = weights[0].shape[1]
     shape = jax.ShapeDtypeStruct((pieces, rows // 2, columns), jnp.bfloat16)
     return pl.pallas_call(
-        functools.partial(out_kernel, pieces, groups),
-        out_shape=(shape,) * 4,
-        in_specs=[SMEM] + [HBM] * (4 * groups + pieces),
-        out_specs=(VMEM,) * 4,
-        scratch_shapes=[
-            pltpu.VMEM((2, 2 * rows, depth), jnp.bfloat16),
-            pltpu.VMEM((pieces, 2 * depth, columns), jnp.bfloat16),
-            pltpu.SemaphoreType.DMA((2, groups, 4)),
-            pltpu.SemaphoreType.DMA((pieces,)),
-        ],
+        functools.partial(out_kernel, pieces, groups, share),
+        out_shape=(shape,) * (2 * share),
+        in_specs=[SMEM] + [VMEM] * (4 * groups + pieces),
+        out_specs=(VMEM,) * (2 * share),
+        scratch_shapes=[pltpu.VMEM((2, share * rows, depth), jnp.bfloat16)],
         compiler_params=GRANT,
         cost_estimate=estimate(3),
     )(place, *attended, *weights)
@@ -498,13 +486,16 @@
     table = jnp.stack(slot_shards(seq_size, shard) + slot_shards(seq_size, shard, -1))
     place = jnp.reshape(side, (1,)).astype(jnp.int32)
 
-    w_kv, *w_queries, near, far = prepare(place, w_key, w_value, w_query, w_out, groups)
+    q_first = pass_on(w_query, seq_size, 1)
+    w_query_other = swap_core(w_query, seq_size)
+    q_second = pass_on(w_query_other, seq_size, 1)
+    q_weights = []
+    for first, second in zip(halves(q_first, groups), halves(q_second, groups)):
+        ring = ring_gather(first, second, seq_size, begin=2)
+        q_weights.append([w_query, q_first, q_second] + ring[2:])
+    w_kv = join(w_key, w_value)
     w_kv_other = swap_core(w_kv, seq_size)
     kv_weights = ring_gather(w_kv, w_kv_other, seq_size)
-    q_weights = []
-    for weight in w_queries:
-        weight_other = swap_core(weight, seq_size)
-        q_weights.append(ring_gather(weight, weight_other, seq_size))
     mine, for_other = norm(table, hidden, norm_gain.reshape(1, width), slots, depth)
 
     positions = shard * rows + jnp.arange(rows, dtype=jnp.int32)
@@ -522,7 +513,7 @@
     )
     other = swap_core(for_other, seq_size)
 
-    keep, send = project(mine, other, kv_weights, 0, ())
+    keep, send = project(mine, other, kv_weights, 2 * HEAD_DIM, 0, 0, ())
     got = swap_core(send, seq_size)
     own_kv = keys_values(keep, got, bias_kv, cosine, sine)
     other_kv = swap_core(own_kv, seq_size)
@@ -537,7 +528,10 @@
         sums = ()
         start = 0
         for count in (slots - 3, 3):
-            sums = project(mine, other, weights[start : start + count], start, sums)
+            sums = project(
+                mine, other, weights[start : start + count], columns, index, start,
+                sums,
+            )
             start += count
         keep, send = sums
         got = swap_core(send, seq_size)
@@ -545,8 +539,8 @@
         query = queries(keep, got, bias, cosine, sine)
         attended.append(attend(table, query, tokens, 2 * slots))
 
-    far = swap_head(far)
-    piece = jnp.concatenate([near, far])
+    w_out_across = swap_head(w_out)
+    piece, rest = cut(place, w_out, w_out_across)
     piece_other = swap_core(piece, seq_size)
     out_weights = ring_gather(piece, piece_other, seq_size)
 
@@ -556,11 +550,14 @@
         attended_other.append(swap_core(one, seq_size))
         across_other.append(swap_core(across[-1], seq_size))
     operands = attended + across + attended_other + across_other
-    whole = None
-    start = 0
-    for count in (slots - 5, 2, 2, 1):
+    keep, keep_other = project_out(place, operands, (piece, rest), 1)
+    theirs = swap_core(keep_other, seq_size)
+    parts = (keep[:1], keep[1:], theirs[:1], theirs[1:])
+    whole = place_part(table, place, parts, 0, slots, w_out.shape[1], None)
+    start = 1
+    for count in (slots - 6, 2, 2, 1):
         keep, keep_other, send, send_other = project_out(
-            place, operands, out_weights[start : start + count]
+            place, operands, out_weights[start : start + count], 2
         )
         got = swap_head(send)
         got_other = swap_both(send_other, seq_size)

time: 174 us -> 163 us (0.937)
  the two profiles are of different devices: /device:TPU:26 before, /device:TPU:27 now
where the time goes in v2:
time: 163 us
  waiting for transfers between devices  74.1 us (45%)
  Pallas kernels  40.7 us (25%)
  starting transfers between devices  37.2 us (23%)
  local copies, waits for them, and re-layouts  8.08 us (5%)
  other arithmetic  2.11 us (1%)
    ppermute x33, waiting for transfers between devices, pass_on(): return lax.ppermute(value, 'seq', ring_perm(seq_size, turn))  62.4 us
    ppermute x24, starting transfers between devices, swap_core(): return lax.ppermute(value, 'seq', [(s, s ^ 1) for s in range(seq_size)])  18.3 us
    pallas_call x2, Pallas kernels, attend(): pl.pallas_call(functools.partial(attend_kernel, count, offset), out_shape...  12.6 us
    ppermute x33, starting transfers between devices, pass_on(): return lax.ppermute(value, 'seq', ring_perm(seq_size, turn))  8.25 us
    pallas_call x5, Pallas kernels, project(): pl.pallas_call(functools.partial(project_kernel, start, count, group), ou...  8.23 us
    unnamed x26, local copies, waits for them, and re-layouts  7.21 us
    pallas_call x5, Pallas kernels, place_part(): pl.pallas_call(functools.partial(place_kernel, start, slots, width), out_...  6.82 us
    ppermute x7, starting transfers between devices, swap_head(): return lax.ppermute(value, 'head', [(0, 1), (1, 0)])  5.55 us
  transfers between devices with their start and end apart: 68, of which 25 were waited for; matrix products, arithmetic and copies ran while one was open for 0% of the time, Pallas kernels for 21%

profile of v2, /device:TPU:27, one launch (start us, length us, event | category | flops | bytes accessed | tf_op | source)
XLA Modules:
  0.0 162.8 jit_solution(14162206385676985566)
XLA Ops:
  2.9 2.3 %copy-done = bf16[288,8192]{1,0:T(8,128)(2,1)S(1)} copy-done((bf16[288,8192]{1,0:T(8,128)(2,1)S(1)}, bf16[288,8192]{1,0:T(8,128)(2,1)}, u32[]{:S(2)}) %copy-start) | copy-done | bytes 4718616
  5.2 4.8 %norm.1 = (bf16[8,288,512]{2,1,0:T(8,128)(2,1)S(1)}, bf16[8,288,512]{2,1,0:T(8,128)(2,1)}) custom-call(s32[32]{0:T(128)S(1)} %stack.125.table, bf16[288,8192]{1,0:T(8,128)(2,1)S(1)} %copy-done, bf16[1,8192]{1,0:T(2,128)(2,1)S(1)} %reshape.46.gain), custom_call_target="tpu_custom_call" | custom-call | flops 4000000000 | bytes 1000000 | tf_op jit(solution)/shard_map/norm/pallas_call | solution.py:204
  10.0 1.4 copy-done.11
  12.6 1.7 %prep.1.refs_0_ = bf16[512,256]{1,0:T(8,128)(2,1)} custom-call(bf16[512,128]{1,0:T(8,128)(2,1)} %w_key.1, bf16[512,128]{1,0:T(8,128)(2,1)} %w_value.1), custom_call_target="tpu_custom_call" | custom-call | flops 1000000000 | bytes 1000000 | tf_op jit(solution)/shard_map/prep/pallas_call | solution.py:123
  15.5 2.1 %collective-permute-done.4 = bf16[512,512]{1,0:T(8,128)(2,1)} collective-permute-done((bf16[512,512]{1,0:T(8,128)(2,1)}, bf16[512,512]{1,0:T(8,128)(2,1)}, u32[]{:S(2)}, u32[]{:S(2)}) %collective-permute-start.4) | collective-permute-done | bytes 524320 | tf_op jit(solution)/shard_map/ppermute | solution.py:75
  17.8 5.9 %collective-permute-done.10.refs_1_ = bf16[512,256]{1,0:T(8,128)(2,1)S(1)} collective-permute-done((bf16[512,256]{1,0:T(8,128)(2,1)}, bf16[512,256]{1,0:T(8,128)(2,1)S(1)}, u32[]{:S(2)}, u32[]{:S(2)}) %collective-permute-start.10) | collective-permute-done | bytes 262176 | tf_op jit(solution)/shard_map/ppermute | solution.py:88
  23.7 1.2 collective-permute-start.46
  25.4 1.8 %shard_map.91 = (bf16[512,256]{1,0:T(8,128)(2,1)S(1)}, bf16[512,256]{1,0:T(8,128)(2,1)}) custom-call(bf16[512,512]{1,0:T(8,128)(2,1)} %collective-permute-done.1.value.refs_1_), custom_call_target="tpu_custom_call" | custom-call | flops 1000000000 | bytes 1000000 | tf_op jit(solution)/shard_map/pallas_call | solution.py:142
  27.1 5.1 %collective-permute-done.13.refs_3_ = bf16[512,256]{1,0:T(8,128)(2,1)} collective-permute-done((bf16[512,256]{1,0:T(8,128)(2,1)S(1)}, bf16[512,256]{1,0:T(8,128)(2,1)}, u32[]{:S(2)}, u32[]{:S(2)}) %collective-permute-start.13) | collective-permute-done | bytes 262176 | tf_op jit(solution)/shard_map/ppermute | solution.py:88
  32.5 2.6 %collective-permute-done.12.refs_2_ = bf16[512,256]{1,0:T(8,128)(2,1)} collective-permute-done((bf16[512,256]{1,0:T(8,128)(2,1)S(1)}, bf16[512,256]{1,0:T(8,128)(2,1)}, u32[]{:S(2)}, u32[]{:S(2)}) %collective-permute-start.12) | collective-permute-done | bytes 262176 | tf_op jit(solution)/shard_map/ppermute | solution.py:88
  37.9 1.1 copy-done.5
  40.9 2.1 %collective-permute-start.54 = (bf16[1024,256]{1,0:T(8,128)(2,1)S(1)}, bf16[1024,256]{1,0:T(8,128)(2,1)S(1)}, u32[]{:S(2)}, u32[]{:S(2)}) collective-permute-start(bf16[1024,256]{1,0:T(8,128)(2,1)S(1)} %get-tuple-element.67.refs_8_), channel_id=1, source_target_pairs={{0,2},{2,0},{4,6},{6,4},{8,10},{10,8},{12,14},{14,12},{16,18},{18,... | collective-permute-start | bytes 1572872 | tf_op jit(solution)/shard_map/ppermute | solution.py:75
  43.9 2.6 %collective-permute-done.36.refs_4_ = bf16[512,256]{1,0:T(8,128)(2,1)} collective-permute-done((bf16[512,256]{1,0:T(8,128)(2,1)}, bf16[512,256]{1,0:T(8,128)(2,1)}, u32[]{:S(2)}, u32[]{:S(2)}) %collective-permute-start.36) | collective-permute-done | bytes 262176 | tf_op jit(solution)/shard_map/ppermute | solution.py:88
  46.9 2.3 %shard_map.98 = (f32[288,256]{1,0:T(8,128)S(1)}, f32[288,256]{1,0:T(8,128)S(1)}) custom-call(bf16[8,288,512]{2,1,0:T(8,128)(2,1)S(1)} %copy-done.12, bf16[8,288,512]{2,1,0:T(8,128)(2,1)S(1)} %collective-permute-done.other, bf16[512,512]{1,0:T(8,128)(2,1)} %refs_0_.3, bf16[512,512]{1,0:T(8,128)(2,1)} %collective-permute-done.1.value.refs_1_, ...), custom_call_target="tpu_custom_call" | custom-call | flops 4000000000 | bytes 1000000 | tf_op jit(solution)/shard_map/pallas_call | solution.py:235
  50.1 1.9 %collective-permute-done.35.refs_0_ = bf16[512,256]{1,0:T(8,128)(2,1)S(1)} collective-permute-done((bf16[512,256]{1,0:T(8,128)(2,1)}, bf16[512,256]{1,0:T(8,128)(2,1)S(1)}, u32[]{:S(2)}, u32[]{:S(2)}) %collective-permute-start.35) | collective-permute-done | bytes 262176 | tf_op jit(solution)/shard_map/ppermute | solution.py:88
  52.3 2.6 %collective-permute-done.17.refs_7_ = bf16[512,256]{1,0:T(8,128)(2,1)S(1)} collective-permute-done((bf16[512,256]{1,0:T(8,128)(2,1)}, bf16[512,256]{1,0:T(8,128)(2,1)S(1)}, u32[]{:S(2)}, u32[]{:S(2)}) %collective-permute-start.17) | collective-permute-done | bytes 262176 | tf_op jit(solution)/shard_map/ppermute | solution.py:88
  55.1 2.5 %collective-permute-done.16.refs_6_ = bf16[512,256]{1,0:T(8,128)(2,1)S(1)} collective-permute-done((bf16[512,256]{1,0:T(8,128)(2,1)}, bf16[512,256]{1,0:T(8,128)(2,1)S(1)}, u32[]{:S(2)}, u32[]{:S(2)}) %collective-permute-start.16) | collective-permute-done | bytes 262176 | tf_op jit(solution)/shard_map/ppermute | solution.py:88
  57.9 2.6 %shard_map.96 = (f32[288,256]{1,0:T(8,128)S(1)}, f32[288,256]{1,0:T(8,128)S(1)}) custom-call(bf16[8,288,512]{2,1,0:T(8,128)(2,1)S(1)} %copy-done.12, bf16[8,288,512]{2,1,0:T(8,128)(2,1)S(1)} %collective-permute-done.other, bf16[512,256]{1,0:T(8,128)(2,1)S(1)} %copy-done.6, bf16[512,256]{1,0:T(8,128)(2,1)S(1)} %collective-permute-done.10.refs_1_, ...), custom_call_target="tpu_custom_call" | custom-call | flops 4000000000 | bytes 1000000 | tf_op jit(solution)/shard_map/pallas_call | solution.py:235
  60.4 5.6 %collective-permute-done.3.refs_0_ = bf16[512,256]{1,0:T(8,128)(2,1)S(1)} collective-permute-done((bf16[512,256]{1,0:T(8,128)(2,1)S(1)}, bf16[512,256]{1,0:T(8,128)(2,1)S(1)}, u32[]{:S(2)}, u32[]{:S(2)}) %collective-permute-start.3) | collective-permute-done | bytes 262176 | tf_op jit(solution)/shard_map/ppermute | solution.py:88
  66.3 2.6 %collective-permute-done.6.refs_4_ = bf16[512,256]{1,0:T(8,128)(2,1)S(1)} collective-permute-done((bf16[512,256]{1,0:T(8,128)(2,1)S(1)}, bf16[512,256]{1,0:T(8,128)(2,1)S(1)}, u32[]{:S(2)}, u32[]{:S(2)}) %collective-permute-start.6) | collective-permute-done | bytes 262176 | tf_op jit(solution)/shard_map/ppermute | solution.py:88
  68.9 2.1 %collective-permute-start.18 = (f32[288,256]{1,0:T(8,128)S(1)}, f32[288,256]{1,0:T(8,128)S(1)}, u32[]{:S(2)}, u32[]{:S(2)}) collective-permute-start(f32[288,256]{1,0:T(8,128)S(1)} %get-tuple-element.59), channel_id=1, source_target_pairs={{0,2},{2,0},{4,6},{6,4},{8,10},{10,8},{12,14},{14,12},{16,18},{18,... | collective-permute-start | bytes 884744 | tf_op jit(solution)/shard_map/ppermute | solution.py:75
  71.0 2.1 %shard_map.93 = (f32[288,256]{1,0:T(8,128)S(1)}, f32[288,256]{1,0:T(8,128)S(1)}) custom-call(bf16[8,288,512]{2,1,0:T(8,128)(2,1)S(1)} %copy-done.12, bf16[8,288,512]{2,1,0:T(8,128)(2,1)S(1)} %collective-permute-done.other, bf16[512,512]{1,0:T(8,128)(2,1)} %refs_0_.3, bf16[512,512]{1,0:T(8,128)(2,1)} %collective-permute-done.1.value.refs_1_, ...), custom_call_target="tpu_custom_call" | custom-call | flops 4000000000 | bytes 1000000 | tf_op jit(solution)/shard_map/pallas_call | solution.py:235
  76.1 2.6 %collective-permute-done.8.refs_2_ = bf16[512,256]{1,0:T(8,128)(2,1)S(1)} collective-permute-done((bf16[512,256]{1,0:T(8,128)(2,1)S(1)}, bf16[512,256]{1,0:T(8,128)(2,1)S(1)}, u32[]{:S(2)}, u32[]{:S(2)}) %collective-permute-start.8) | collective-permute-done | bytes 262176 | tf_op jit(solution)/shard_map/ppermute | solution.py:88
  79.0 9.8 %collective-permute-done.7.refs_1_ = bf16[512,256]{1,0:T(8,128)(2,1)S(1)} collective-permute-done((bf16[512,256]{1,0:T(8,128)(2,1)S(1)}, bf16[512,256]{1,0:T(8,128)(2,1)S(1)}, u32[]{:S(2)}, u32[]{:S(2)}) %collective-permute-start.7) | collective-permute-done | bytes 262176 | tf_op jit(solution)/shard_map/ppermute | solution.py:88
  91.3 4.2 %collective-permute-done.21.refs_2_ = bf16[288,256]{1,0:T(8,128)(2,1)S(1)} collective-permute-done((bf16[288,256]{1,0:T(8,128)(2,1)S(1)}, bf16[288,256]{1,0:T(8,128)(2,1)S(1)}, u32[]{:S(2)}, u32[]{:S(2)}) %collective-permute-start.21) | collective-permute-done | bytes 147488 | tf_op jit(solution)/shard_map/ppermute | solution.py:88
  95.6 2.0 %collective-permute-done.22.refs_3_ = bf16[288,256]{1,0:T(8,128)(2,1)S(1)} collective-permute-done((bf16[288,256]{1,0:T(8,128)(2,1)S(1)}, bf16[288,256]{1,0:T(8,128)(2,1)S(1)}, u32[]{:S(2)}, u32[]{:S(2)}) %collective-permute-start.22) | collective-permute-done | bytes 147488 | tf_op jit(solution)/shard_map/ppermute | solution.py:88
  98.5 1.2 collective-permute-done.23.refs_4_
  99.9 2.0 %collective-permute-done.24.refs_5_ = bf16[288,256]{1,0:T(8,128)(2,1)S(1)} collective-permute-done((bf16[288,256]{1,0:T(8,128)(2,1)S(1)}, bf16[288,256]{1,0:T(8,128)(2,1)S(1)}, u32[]{:S(2)}, u32[]{:S(2)}) %collective-permute-start.24) | collective-permute-done | bytes 147488 | tf_op jit(solution)/shard_map/ppermute | solution.py:88
  102.4 1.5 collective-permute-start.29
  104.4 2.2 %collective-permute-start.32 = (bf16[288,256]{1,0:T(8,128)(2,1)S(1)}, bf16[288,256]{1,0:T(8,128)(2,1)S(1)}, u32[]{:S(2)}, u32[]{:S(2)}) collective-permute-start(bf16[288,256]{1,0:T(8,128)(2,1)S(1)} %collective-permute-done.25.refs_6_), channel_id=1, source_target_pairs={{0,2},{2,0},{4,6},{6,4},{8,10},{10,8},{12,14},{14,12},{16,18},{18,... | collective-permute-start | bytes 442376 | tf_op jit(solution)/shard_map/ppermute | solution.py:75
  106.6 1.6 collective-permute-start.33
  109.2 6.2 %shard_map.101.refs_1_ = bf16[288,256]{1,0:T(8,128)(2,1)S(1)} custom-call(s32[32]{0:T(128)S(1)} %stack.125.table, bf16[128,576]{1,0:T(8,128)(2,1)S(1)} %shard_map.100.query, bf16[288,256]{1,0:T(8,128)(2,1)S(1)} %kv.1.refs_0_, bf16[288,256]{1,0:T(8,128)(2,1)S(1)} %collective-permute-done.19.refs_1_, bf16[288,256]{1,0:T(8,128)(2,1)S(1)} %collective-permute-done.21.refs_2_, ...), custom_call_target="tpu_custom_call" | custom-call | flops 8000000000 | bytes 1000000 | tf_op jit(solution)/shard_map/pallas_call | solution.py:373
  115.4 1.3 collective-permute-start.41
  116.7 6.4 %shard_map.97.refs_0_ = bf16[288,256]{1,0:T(8,128)(2,1)S(1)} custom-call(s32[32]{0:T(128)S(1)} %stack.125.table, bf16[128,576]{1,0:T(8,128)(2,1)S(1)} %shard_map.95.query, bf16[288,256]{1,0:T(8,128)(2,1)S(1)} %kv.1.refs_0_, bf16[288,256]{1,0:T(8,128)(2,1)S(1)} %collective-permute-done.19.refs_1_, bf16[288,256]{1,0:T(8,128)(2,1)S(1)} %collective-permute-done.21.refs_2_, ...), custom_call_target="tpu_custom_call" | custom-call | flops 8000000000 | bytes 1000000 | tf_op jit(solution)/shard_map/pallas_call | solution.py:373
  124.0 4.8 %collective-permute-done.40.refs_2_ = bf16[288,256]{1,0:T(8,128)(2,1)S(1)} collective-permute-done((bf16[288,256]{1,0:T(8,128)(2,1)S(1)}, bf16[288,256]{1,0:T(8,128)(2,1)S(1)}, u32[]{:S(2)}, u32[]{:S(2)}) %collective-permute-start.40) | collective-permute-done | bytes 147488 | tf_op jit(solution)/shard_map/ppermute | solution.py:79
  133.4 4.1 %collective-permute-done.57.refs_9_ = bf16[1024,256]{1,0:T(8,128)(2,1)S(1)} collective-permute-done((bf16[1024,256]{1,0:T(8,128)(2,1)S(1)}, bf16[1024,256]{1,0:T(8,128)(2,1)S(1)}, u32[]{:S(2)}, u32[]{:S(2)}) %collective-permute-start.57) | collective-permute-done | bytes 524320 | tf_op jit(solution)/shard_map/ppermute | solution.py:88
  139.4 3.8 %collective-permute-done.50.refs_8_ = bf16[1024,256]{1,0:T(8,128)(2,1)S(1)} collective-permute-done((bf16[1024,256]{1,0:T(8,128)(2,1)S(1)}, bf16[1024,256]{1,0:T(8,128)(2,1)S(1)}, u32[]{:S(2)}, u32[]{:S(2)}) %collective-permute-start.50) | collective-permute-done | bytes 524320 | tf_op jit(solution)/shard_map/ppermute | solution.py:88
  143.9 1.3 collective-permute-start.62
  145.2 1.2 collective-permute-start.63
  146.4 1.3 shard_map.107.refs_4_
  148.8 1.2 collective-permute-start.60
  150.0 1.4 shard_map.108.refs_4_
  151.4 1.9 %collective-permute-start.51 = (bf16[1,144,256]{2,1,0:T(8,128)(2,1)S(1)}, bf16[1,144,256]{2,1,0:T(8,128)(2,1)S(1)}, u32[]{:S(2)}, u32[]{:S(2)}) collective-permute-start(bf16[1,144,256]{2,1,0:T(8,128)(2,1)S(1)} %get-tuple-element.69), channel_id=1, source_target_pairs={{0,1},{1,0},{2,3},{3,2},{4,5},{5,4},{6,7},{7,6},{8,9},{9,8},{10,11... | collective-permute-start | bytes 221192 | tf_op jit(solution)/shard_map/ppermute | solution.py:79
  153.4 1.4 shard_map.109.refs_4_
  154.8 1.6 collective-permute-start.53
  156.4 2.6 %collective-permute-done.60.refs_3_ = bf16[2,144,256]{2,1,0:T(8,128)(2,1)S(1)} collective-permute-done((bf16[2,144,256]{2,1,0:T(8,128)(2,1)S(1)}, bf16[2,144,256]{2,1,0:T(8,128)(2,1)S(1)}, u32[]{:S(2)}, u32[]{:S(2)}) %collective-permute-start.60) | collective-permute-done | bytes 147488 | tf_op jit(solution)/shard_map/ppermute | solution.py:84
  159.0 1.4 shard_map.110.refs_4_
  161.4 1.3 shard_map.111
  (150 shorter events, 32.9 us)
Async XLA Ops:
  11.5 35.2 %collective-permute-start = (bf16[8,288,512]{2,1,0:T(8,128)(2,1)}, bf16[8,288,512]{2,1,0:T(8,128)(2,1)S(1)}, u32[]{:S(2)}, u32[]{:S(2)}) collective-permute-start(bf16[8,288,512]{2,1,0:T(8,128)(2,1)} %get-tuple-element.48), channel_id=1, source_target_pairs={{0,2},{2,0},{4,6},{6,4},{8,10},{10,8},{12,14},{14,12},{16,18},{18,... | collective-permute-start | bytes 7077896 | tf_op jit(solution)/shard_map/ppermute | solution.py:75
  12.3 12.9 %collective-permute-start.1 = (bf16[512,512]{1,0:T(8,128)(2,1)}, bf16[512,512]{1,0:T(8,128)(2,1)}, u32[]{:S(2)}, u32[]{:S(2)}) collective-permute-start(bf16[512,512]{1,0:T(8,128)(2,1)} %refs_0_.3), channel_id=1, source_target_pairs={{0,8},{2,6},{8,16},{10,2},{16,24},{18,10},{24,28},{26,18},{28,20},... | collective-permute-start | bytes 1572872 | tf_op jit(solution)/shard_map/ppermute | solution.py:88
  14.3 9.4 %collective-permute-start.10 = (bf16[512,256]{1,0:T(8,128)(2,1)}, bf16[512,256]{1,0:T(8,128)(2,1)S(1)}, u32[]{:S(2)}, u32[]{:S(2)}) collective-permute-start(bf16[512,256]{1,0:T(8,128)(2,1)} %prep.1.refs_0_), channel_id=1, source_target_pairs={{0,8},{2,6},{8,16},{10,2},{16,24},{18,10},{24,28},{26,18},{28,20},... | collective-permute-start | bytes 786440 | tf_op jit(solution)/shard_map/ppermute | solution.py:88
  14.5 10.4 %collective-permute-start.11 = (bf16[512,256]{1,0:T(8,128)(2,1)}, bf16[512,256]{1,0:T(8,128)(2,1)S(1)}, u32[]{:S(2)}, u32[]{:S(2)}) collective-permute-start(bf16[512,256]{1,0:T(8,128)(2,1)} %prep.1.refs_0_), channel_id=1, source_target_pairs={{0,2},{2,0},{4,6},{6,4},{8,10},{10,8},{12,14},{14,12},{16,18},{18,... | collective-permute-start | bytes 786440 | tf_op jit(solution)/shard_map/ppermute | solution.py:75
  17.5 17.8 %collective-permute-start.5 = (bf16[512,512]{1,0:T(8,128)(2,1)}, bf16[512,512]{1,0:T(8,128)(2,1)S(1)}, u32[]{:S(2)}, u32[]{:S(2)}) collective-permute-start(bf16[512,512]{1,0:T(8,128)(2,1)} %collective-permute-done.4), channel_id=1, source_target_pairs={{0,8},{2,6},{8,16},{10,2},{16,24},{18,10},{24,28},{26,18},{28,20},... | collective-permute-start | bytes 1572872 | tf_op jit(solution)/shard_map/ppermute | solution.py:88
  23.7 13.3 %collective-permute-start.46 = (bf16[512,512]{1,0:T(8,128)(2,1)S(1)}, bf16[512,512]{1,0:T(8,128)(2,1)S(1)}, u32[]{:S(2)}, u32[]{:S(2)}) collective-permute-start(bf16[512,512]{1,0:T(8,128)(2,1)S(1)} %copy-done.1), channel_id=1, source_target_pairs={{0,1},{1,0},{2,3},{3,2},{4,5},{5,4},{6,7},{7,6},{8,9},{9,8},{10,11... | collective-permute-start | bytes 1572872 | tf_op jit(solution)/shard_map/ppermute | solution.py:79
  24.9 7.3 %collective-permute-start.13 = (bf16[512,256]{1,0:T(8,128)(2,1)S(1)}, bf16[512,256]{1,0:T(8,128)(2,1)}, u32[]{:S(2)}, u32[]{:S(2)}) collective-permute-start(bf16[512,256]{1,0:T(8,128)(2,1)S(1)} %collective-permute-done.10.refs_1_), channel_id=1, source_target_pairs={{0,8},{2,6},{8,16},{10,2},{16,24},{18,10},{24,28},{26,18},{28,20},... | collective-permute-start | bytes 786440 | tf_op jit(solution)/shard_map/ppermute | solution.py:88
  25.2 9.8 %collective-permute-start.12 = (bf16[512,256]{1,0:T(8,128)(2,1)S(1)}, bf16[512,256]{1,0:T(8,128)(2,1)}, u32[]{:S(2)}, u32[]{:S(2)}) collective-permute-start(bf16[512,256]{1,0:T(8,128)(2,1)S(1)} %collective-permute-done.11), channel_id=1, source_target_pairs={{0,8},{2,6},{8,16},{10,2},{16,24},{18,10},{24,28},{26,18},{28,20},... | collective-permute-start | bytes 786440 | tf_op jit(solution)/shard_map/ppermute | solution.py:88
  32.2 6.9 %collective-permute-start.34 = (bf16[512,256]{1,0:T(8,128)(2,1)}, bf16[512,256]{1,0:T(8,128)(2,1)}, u32[]{:S(2)}, u32[]{:S(2)}) collective-permute-start(bf16[512,256]{1,0:T(8,128)(2,1)} %get-tuple-element.61), channel_id=1, source_target_pairs={{0,8},{2,6},{8,16},{10,2},{16,24},{18,10},{24,28},{26,18},{28,20},... | collective-permute-start | bytes 786440 | tf_op jit(solution)/shard_map/ppermute | solution.py:88
  35.3 8.4 %collective-permute-start.14 = (bf16[512,256]{1,0:T(8,128)(2,1)}, bf16[512,256]{1,0:T(8,128)(2,1)}, u32[]{:S(2)}, u32[]{:S(2)}) collective-permute-start(bf16[512,256]{1,0:T(8,128)(2,1)} %collective-permute-done.12.refs_2_), channel_id=1, source_target_pairs={{0,8},{2,6},{8,16},{10,2},{16,24},{18,10},{24,28},{26,18},{28,20},... | collective-permute-start | bytes 786440 | tf_op jit(solution)/shard_map/ppermute | solution.py:88
  37.8 8.7 %collective-permute-start.36 = (bf16[512,256]{1,0:T(8,128)(2,1)}, bf16[512,256]{1,0:T(8,128)(2,1)}, u32[]{:S(2)}, u32[]{:S(2)}) collective-permute-start(bf16[512,256]{1,0:T(8,128)(2,1)} %get-tuple-element.62), channel_id=1, source_target_pairs={{0,8},{2,6},{8,16},{10,2},{16,24},{18,10},{24,28},{26,18},{28,20},... | collective-permute-start | bytes 786440 | tf_op jit(solution)/shard_map/ppermute | solution.py:88
  40.0 9.3 %collective-permute-start.2 = (bf16[512,256]{1,0:T(8,128)(2,1)S(1)}, bf16[512,256]{1,0:T(8,128)(2,1)S(1)}, u32[]{:S(2)}, u32[]{:S(2)}) collective-permute-start(bf16[512,256]{1,0:T(8,128)(2,1)S(1)} %copy-done.10), channel_id=1, source_target_pairs={{0,8},{2,6},{8,16},{10,2},{16,24},{18,10},{24,28},{26,18},{28,20},... | collective-permute-start | bytes 786440 | tf_op jit(solution)/shard_map/ppermute | solution.py:88
  40.9 32.2 %collective-permute-start.54 = (bf16[1024,256]{1,0:T(8,128)(2,1)S(1)}, bf16[1024,256]{1,0:T(8,128)(2,1)S(1)}, u32[]{:S(2)}, u32[]{:S(2)}) collective-permute-start(bf16[1024,256]{1,0:T(8,128)(2,1)S(1)} %get-tuple-element.67.refs_8_), channel_id=1, source_target_pairs={{0,2},{2,0},{4,6},{6,4},{8,10},{10,8},{12,14},{14,12},{16,18},{18,... | collective-permute-start | bytes 1572872 | tf_op jit(solution)/shard_map/ppermute | solution.py:75
  43.7 8.3 %collective-permute-start.35 = (bf16[512,256]{1,0:T(8,128)(2,1)}, bf16[512,256]{1,0:T(8,128)(2,1)S(1)}, u32[]{:S(2)}, u32[]{:S(2)}) collective-permute-start(bf16[512,256]{1,0:T(8,128)(2,1)} %collective-permute-done.34.refs_3_), channel_id=1, source_target_pairs={{0,8},{2,6},{8,16},{10,2},{16,24},{18,10},{24,28},{26,18},{28,20},... | collective-permute-start | bytes 786440 | tf_op jit(solution)/shard_map/ppermute | solution.py:88
  46.5 8.3 %collective-permute-start.17 = (bf16[512,256]{1,0:T(8,128)(2,1)}, bf16[512,256]{1,0:T(8,128)(2,1)S(1)}, u32[]{:S(2)}, u32[]{:S(2)}) collective-permute-start(bf16[512,256]{1,0:T(8,128)(2,1)} %collective-permute-done.15.refs_5_), channel_id=1, source_target_pairs={{0,8},{2,6},{8,16},{10,2},{16,24},{18,10},{24,28},{26,18},{28,20},... | collective-permute-start | bytes 786440 | tf_op jit(solution)/shard_map/ppermute | solution.py:88
  46.7 10.9 %collective-permute-start.16 = (bf16[512,256]{1,0:T(8,128)(2,1)}, bf16[512,256]{1,0:T(8,128)(2,1)S(1)}, u32[]{:S(2)}, u32[]{:S(2)}) collective-permute-start(bf16[512,256]{1,0:T(8,128)(2,1)} %collective-permute-done.14.refs_4_), channel_id=1, source_target_pairs={{0,8},{2,6},{8,16},{10,2},{16,24},{18,10},{24,28},{26,18},{28,20},... | collective-permute-start | bytes 786440 | tf_op jit(solution)/shard_map/ppermute | solution.py:88
  49.3 24.5 %collective-permute-start.47 = (bf16[1024,256]{1,0:T(8,128)(2,1)S(1)}, bf16[1024,256]{1,0:T(8,128)(2,1)S(1)}, u32[]{:S(2)}, u32[]{:S(2)}) collective-permute-start(bf16[1024,256]{1,0:T(8,128)(2,1)S(1)} %get-tuple-element.67.refs_8_), channel_id=1, source_target_pairs={{0,8},{2,6},{8,16},{10,2},{16,24},{18,10},{24,28},{26,18},{28,20},... | collective-permute-start | bytes 1572872 | tf_op jit(solution)/shard_map/ppermute | solution.py:88
  52.0 14.0 %collective-permute-start.3 = (bf16[512,256]{1,0:T(8,128)(2,1)S(1)}, bf16[512,256]{1,0:T(8,128)(2,1)S(1)}, u32[]{:S(2)}, u32[]{:S(2)}) collective-permute-start(bf16[512,256]{1,0:T(8,128)(2,1)S(1)} %collective-permute-done.2.refs_3_), channel_id=1, source_target_pairs={{0,8},{2,6},{8,16},{10,2},{16,24},{18,10},{24,28},{26,18},{28,20},... | collective-permute-start | bytes 786440 | tf_op jit(solution)/shard_map/ppermute | solution.py:88
  54.8 14.0 %collective-permute-start.6 = (bf16[512,256]{1,0:T(8,128)(2,1)S(1)}, bf16[512,256]{1,0:T(8,128)(2,1)S(1)}, u32[]{:S(2)}, u32[]{:S(2)}) collective-permute-start(bf16[512,256]{1,0:T(8,128)(2,1)S(1)} %copy-done.8), channel_id=1, source_target_pairs={{0,8},{2,6},{8,16},{10,2},{16,24},{18,10},{24,28},{26,18},{28,20},... | collective-permute-start | bytes 786440 | tf_op jit(solution)/shard_map/ppermute | solution.py:88
  57.6 16.7 %collective-permute-start.38 = (bf16[512,256]{1,0:T(8,128)(2,1)S(1)}, bf16[512,256]{1,0:T(8,128)(2,1)S(1)}, u32[]{:S(2)}, u32[]{:S(2)}) collective-permute-start(bf16[512,256]{1,0:T(8,128)(2,1)S(1)} %collective-permute-done.35.refs_0_), channel_id=1, source_target_pairs={{0,8},{2,6},{8,16},{10,2},{16,24},{18,10},{24,28},{26,18},{28,20},... | collective-permute-start | bytes 786440 | tf_op jit(solution)/shard_map/ppermute | solution.py:88
  66.0 8.7 %collective-permute-start.37 = (bf16[512,256]{1,0:T(8,128)(2,1)}, bf16[512,256]{1,0:T(8,128)(2,1)S(1)}, u32[]{:S(2)}, u32[]{:S(2)}) collective-permute-start(bf16[512,256]{1,0:T(8,128)(2,1)} %collective-permute-done.36.refs_4_), channel_id=1, source_target_pairs={{0,8},{2,6},{8,16},{10,2},{16,24},{18,10},{24,28},{26,18},{28,20},... | collective-permute-start | bytes 786440 | tf_op jit(solution)/shard_map/ppermute | solution.py:88
  73.4 17.1 %collective-permute-start.55 = (bf16[1024,256]{1,0:T(8,128)(2,1)S(1)}, bf16[1024,256]{1,0:T(8,128)(2,1)S(1)}, u32[]{:S(2)}, u32[]{:S(2)}) collective-permute-start(bf16[1024,256]{1,0:T(8,128)(2,1)S(1)} %collective-permute-done.54), channel_id=1, source_target_pairs={{0,8},{2,6},{8,16},{10,2},{16,24},{18,10},{24,28},{26,18},{28,20},... | collective-permute-start | bytes 1572872 | tf_op jit(solution)/shard_map/ppermute | solution.py:88
  73.8 14.9 %collective-permute-start.7 = (bf16[512,256]{1,0:T(8,128)(2,1)S(1)}, bf16[512,256]{1,0:T(8,128)(2,1)S(1)}, u32[]{:S(2)}, u32[]{:S(2)}) collective-permute-start(bf16[512,256]{1,0:T(8,128)(2,1)S(1)} %collective-permute-done.6.refs_4_), channel_id=1, source_target_pairs={{0,8},{2,6},{8,16},{10,2},{16,24},{18,10},{24,28},{26,18},{28,20},... | collective-permute-start | bytes 786440 | tf_op jit(solution)/shard_map/ppermute | solution.py:88
  74.4 15.2 %collective-permute-start.20 = (bf16[288,256]{1,0:T(8,128)(2,1)S(1)}, bf16[288,256]{1,0:T(8,128)(2,1)S(1)}, u32[]{:S(2)}, u32[]{:S(2)}) collective-permute-start(bf16[288,256]{1,0:T(8,128)(2,1)S(1)} %kv.1.refs_0_), channel_id=1, source_target_pairs={{0,2},{2,0},{4,6},{6,4},{8,10},{10,8},{12,14},{14,12},{16,18},{18,... | collective-permute-start | bytes 442376 | tf_op jit(solution)/shard_map/ppermute | solution.py:75
  74.8 15.0 %collective-permute-start.19 = (bf16[288,256]{1,0:T(8,128)(2,1)S(1)}, bf16[288,256]{1,0:T(8,128)(2,1)S(1)}, u32[]{:S(2)}, u32[]{:S(2)}) collective-permute-start(bf16[288,256]{1,0:T(8,128)(2,1)S(1)} %kv.1.refs_0_), channel_id=1, source_target_pairs={{0,4},{2,10},{8,0},{10,18},{16,8},{18,26},{24,16},{26,30},{28,24},... | collective-permute-start | bytes 442376 | tf_op jit(solution)/shard_map/ppermute | solution.py:88
  78.7 19.1 %collective-permute-start.48 = (bf16[1024,256]{1,0:T(8,128)(2,1)S(1)}, bf16[1024,256]{1,0:T(8,128)(2,1)S(1)}, u32[]{:S(2)}, u32[]{:S(2)}) collective-permute-start(bf16[1024,256]{1,0:T(8,128)(2,1)S(1)} %collective-permute-done.47.refs_8_), channel_id=1, source_target_pairs={{0,8},{2,6},{8,16},{10,2},{16,24},{18,10},{24,28},{26,18},{28,20},... | collective-permute-start | bytes 1572872 | tf_op jit(solution)/shard_map/ppermute | solution.py:88
  88.7 9.7 %collective-permute-start.39 = (f32[288,256]{1,0:T(8,128)S(1)}, f32[288,256]{1,0:T(8,128)S(1)}, u32[]{:S(2)}, u32[]{:S(2)}) collective-permute-start(f32[288,256]{1,0:T(8,128)S(1)} %get-tuple-element.66), channel_id=1, source_target_pairs={{0,2},{2,0},{4,6},{6,4},{8,10},{10,8},{12,14},{14,12},{16,18},{18,... | collective-permute-start | bytes 884744 | tf_op jit(solution)/shard_map/ppermute | solution.py:75
  89.7 7.9 %collective-permute-start.22 = (bf16[288,256]{1,0:T(8,128)(2,1)S(1)}, bf16[288,256]{1,0:T(8,128)(2,1)S(1)}, u32[]{:S(2)}, u32[]{:S(2)}) collective-permute-start(bf16[288,256]{1,0:T(8,128)(2,1)S(1)} %collective-permute-done.19.refs_1_), channel_id=1, source_target_pairs={{0,4},{2,10},{8,0},{10,18},{16,8},{18,26},{24,16},{26,30},{28,24},... | collective-permute-start | bytes 442376 | tf_op jit(solution)/shard_map/ppermute | solution.py:88
  90.5 11.8 %collective-permute-start.9 = (f32[288,256]{1,0:T(8,128)S(1)}, f32[288,256]{1,0:T(8,128)S(1)}, u32[]{:S(2)}, u32[]{:S(2)}) collective-permute-start(f32[288,256]{1,0:T(8,128)S(1)} %get-tuple-element.54), channel_id=1, source_target_pairs={{0,2},{2,0},{4,6},{6,4},{8,10},{10,8},{12,14},{14,12},{16,18},{18,... | collective-permute-start | bytes 884744 | tf_op jit(solution)/shard_map/ppermute | solution.py:75
  97.8 6.1 %collective-permute-start.27 = (bf16[288,256]{1,0:T(8,128)(2,1)S(1)}, bf16[288,256]{1,0:T(8,128)(2,1)S(1)}, u32[]{:S(2)}, u32[]{:S(2)}) collective-permute-start(bf16[288,256]{1,0:T(8,128)(2,1)S(1)} %collective-permute-done.19.refs_1_), channel_id=1, source_target_pairs={{0,2},{2,0},{4,6},{6,4},{8,10},{10,8},{12,14},{14,12},{16,18},{18,... | collective-permute-start | bytes 442376 | tf_op jit(solution)/shard_map/ppermute | solution.py:75
  102.4 6.0 %collective-permute-start.29 = (bf16[288,256]{1,0:T(8,128)(2,1)S(1)}, bf16[288,256]{1,0:T(8,128)(2,1)S(1)}, u32[]{:S(2)}, u32[]{:S(2)}) collective-permute-start(bf16[288,256]{1,0:T(8,128)(2,1)S(1)} %collective-permute-done.22.refs_3_), channel_id=1, source_target_pairs={{0,2},{2,0},{4,6},{6,4},{8,10},{10,8},{12,14},{14,12},{16,18},{18,... | collective-permute-start | bytes 442376 | tf_op jit(solution)/shard_map/ppermute | solution.py:75
  108.4 15.0 %collective-permute-start.56 = (bf16[1024,256]{1,0:T(8,128)(2,1)S(1)}, bf16[1024,256]{1,0:T(8,128)(2,1)S(1)}, u32[]{:S(2)}, u32[]{:S(2)}) collective-permute-start(bf16[1024,256]{1,0:T(8,128)(2,1)S(1)} %collective-permute-done.55.refs_9_), channel_id=1, source_target_pairs={{0,8},{2,6},{8,16},{10,2},{16,24},{18,10},{24,28},{26,18},{28,20},... | collective-permute-start | bytes 1572872 | tf_op jit(solution)/shard_map/ppermute | solution.py:88
  108.7 20.5 %collective-permute-start.49 = (bf16[1024,256]{1,0:T(8,128)(2,1)S(1)}, bf16[1024,256]{1,0:T(8,128)(2,1)S(1)}, u32[]{:S(2)}, u32[]{:S(2)}) collective-permute-start(bf16[1024,256]{1,0:T(8,128)(2,1)S(1)} %collective-permute-done.48.refs_8_), channel_id=1, source_target_pairs={{0,8},{2,6},{8,16},{10,2},{16,24},{18,10},{24,28},{26,18},{28,20},... | collective-permute-start | bytes 1572872 | tf_op jit(solution)/shard_map/ppermute | solution.py:88
  115.4 8.5 %collective-permute-start.41 = (bf16[288,256]{1,0:T(8,128)(2,1)S(1)}, bf16[288,256]{1,0:T(8,128)(2,1)S(1)}, u32[]{:S(2)}, u32[]{:S(2)}) collective-permute-start(bf16[288,256]{1,0:T(8,128)(2,1)S(1)} %shard_map.101.refs_1_), channel_id=1, source_target_pairs={{0,1},{1,0},{2,3},{3,2},{4,5},{5,4},{6,7},{7,6},{8,9},{9,8},{10,11... | collective-permute-start | bytes 442376 | tf_op jit(solution)/shard_map/ppermute | solution.py:79
  129.2 8.3 %collective-permute-start.57 = (bf16[1024,256]{1,0:T(8,128)(2,1)S(1)}, bf16[1024,256]{1,0:T(8,128)(2,1)S(1)}, u32[]{:S(2)}, u32[]{:S(2)}) collective-permute-start(bf16[1024,256]{1,0:T(8,128)(2,1)S(1)} %collective-permute-done.56.refs_9_), channel_id=1, source_target_pairs={{0,8},{2,6},{8,16},{10,2},{16,24},{18,10},{24,28},{26,18},{28,20},... | collective-permute-start | bytes 1572872 | tf_op jit(solution)/shard_map/ppermute | solution.py:88
  129.2 13.9 %collective-permute-start.50 = (bf16[1024,256]{1,0:T(8,128)(2,1)S(1)}, bf16[1024,256]{1,0:T(8,128)(2,1)S(1)}, u32[]{:S(2)}, u32[]{:S(2)}) collective-permute-start(bf16[1024,256]{1,0:T(8,128)(2,1)S(1)} %collective-permute-done.49.refs_8_), channel_id=1, source_target_pairs={{0,8},{2,6},{8,16},{10,2},{16,24},{18,10},{24,28},{26,18},{28,20},... | collective-permute-start | bytes 1572872 | tf_op jit(solution)/shard_map/ppermute | solution.py:88
  130.7 13.2 %collective-permute-start.67 = (bf16[2,144,256]{2,1,0:T(8,128)(2,1)S(1)}, bf16[2,144,256]{2,1,0:T(8,128)(2,1)S(1)}, u32[]{:S(2)}, u32[]{:S(2)}) collective-permute-start(bf16[2,144,256]{2,1,0:T(8,128)(2,1)S(1)} %get-tuple-element.86), channel_id=1, source_target_pairs={{0,2},{2,0},{4,6},{6,4},{8,10},{10,8},{12,14},{14,12},{16,18},{18,... | collective-permute-start | bytes 442376 | tf_op jit(solution)/shard_map/ppermute | solution.py:75
  131.9 13.3 %collective-permute-start.64 = (bf16[2,144,256]{2,1,0:T(8,128)(2,1)S(1)}, bf16[2,144,256]{2,1,0:T(8,128)(2,1)S(1)}, u32[]{:S(2)}, u32[]{:S(2)}) collective-permute-start(bf16[2,144,256]{2,1,0:T(8,128)(2,1)S(1)} %get-tuple-element.81), channel_id=1, source_target_pairs={{0,1},{1,0},{2,3},{3,2},{4,5},{5,4},{6,7},{7,6},{8,9},{9,8},{10,11... | collective-permute-start | bytes 442376 | tf_op jit(solution)/shard_map/ppermute | solution.py:79
  132.2 15.5 %collective-permute-start.65 = (bf16[2,144,256]{2,1,0:T(8,128)(2,1)S(1)}, bf16[2,144,256]{2,1,0:T(8,128)(2,1)S(1)}, u32[]{:S(2)}, u32[]{:S(2)}) collective-permute-start(bf16[2,144,256]{2,1,0:T(8,128)(2,1)S(1)} %get-tuple-element.82), channel_id=1, source_target_pairs={{0,2},{2,0},{4,6},{6,4},{8,10},{10,8},{12,14},{14,12},{16,18},{18,... | collective-permute-start | bytes 442376 | tf_op jit(solution)/shard_map/ppermute | solution.py:75
  137.5 10.5 %collective-permute-start.66 = (bf16[2,144,256]{2,1,0:T(8,128)(2,1)S(1)}, bf16[2,144,256]{2,1,0:T(8,128)(2,1)S(1)}, u32[]{:S(2)}, u32[]{:S(2)}) collective-permute-start(bf16[2,144,256]{2,1,0:T(8,128)(2,1)S(1)} %get-tuple-element.83), channel_id=1, source_target_pairs={{0,3},{1,2},{2,1},{3,0},{4,7},{5,6},{6,5},{7,4},{8,11},{9,10},{10,... | collective-permute-start | bytes 442376 | tf_op jit(solution)/shard_map/ppermute | solution.py:84
  143.9 7.6 %collective-permute-start.62 = (bf16[2,144,256]{2,1,0:T(8,128)(2,1)S(1)}, bf16[2,144,256]{2,1,0:T(8,128)(2,1)S(1)}, u32[]{:S(2)}, u32[]{:S(2)}) collective-permute-start(bf16[2,144,256]{2,1,0:T(8,128)(2,1)S(1)} %get-tuple-element.78), channel_id=1, source_target_pairs={{0,2},{2,0},{4,6},{6,4},{8,10},{10,8},{12,14},{14,12},{16,18},{18,... | collective-permute-start | bytes 442376 | tf_op jit(solution)/shard_map/ppermute | solution.py:75
  145.2 8.2 %collective-permute-start.63 = (bf16[2,144,256]{2,1,0:T(8,128)(2,1)S(1)}, bf16[2,144,256]{2,1,0:T(8,128)(2,1)S(1)}, u32[]{:S(2)}, u32[]{:S(2)}) collective-permute-start(bf16[2,144,256]{2,1,0:T(8,128)(2,1)S(1)} %get-tuple-element.79), channel_id=1, source_target_pairs={{0,3},{1,2},{2,1},{3,0},{4,7},{5,6},{6,5},{7,4},{8,11},{9,10},{10,... | collective-permute-start | bytes 442376 | tf_op jit(solution)/shard_map/ppermute | solution.py:84
  147.7 7.1 %collective-permute-start.58 = (bf16[2,144,256]{2,1,0:T(8,128)(2,1)S(1)}, bf16[2,144,256]{2,1,0:T(8,128)(2,1)S(1)}, u32[]{:S(2)}, u32[]{:S(2)}) collective-permute-start(bf16[2,144,256]{2,1,0:T(8,128)(2,1)S(1)} %get-tuple-element.73), channel_id=1, source_target_pairs={{0,1},{1,0},{2,3},{3,2},{4,5},{5,4},{6,7},{7,6},{8,9},{9,8},{10,11... | collective-permute-start | bytes 442376 | tf_op jit(solution)/shard_map/ppermute | solution.py:79
  148.0 8.4 %collective-permute-start.59 = (bf16[2,144,256]{2,1,0:T(8,128)(2,1)S(1)}, bf16[2,144,256]{2,1,0:T(8,128)(2,1)S(1)}, u32[]{:S(2)}, u32[]{:S(2)}) collective-permute-start(bf16[2,144,256]{2,1,0:T(8,128)(2,1)S(1)} %get-tuple-element.74), channel_id=1, source_target_pairs={{0,2},{2,0},{4,6},{6,4},{8,10},{10,8},{12,14},{14,12},{16,18},{18,... | collective-permute-start | bytes 442376 | tf_op jit(solution)/shard_map/ppermute | solution.py:75
  148.8 10.2 %collective-permute-start.60 = (bf16[2,144,256]{2,1,0:T(8,128)(2,1)S(1)}, bf16[2,144,256]{2,1,0:T(8,128)(2,1)S(1)}, u32[]{:S(2)}, u32[]{:S(2)}) collective-permute-start(bf16[2,144,256]{2,1,0:T(8,128)(2,1)S(1)} %get-tuple-element.75), channel_id=1, source_target_pairs={{0,3},{1,2},{2,1},{3,0},{4,7},{5,6},{6,5},{7,4},{8,11},{9,10},{10,... | collective-permute-start | bytes 442376 | tf_op jit(solution)/shard_map/ppermute | solution.py:84
  151.4 9.0 %collective-permute-start.51 = (bf16[1,144,256]{2,1,0:T(8,128)(2,1)S(1)}, bf16[1,144,256]{2,1,0:T(8,128)(2,1)S(1)}, u32[]{:S(2)}, u32[]{:S(2)}) collective-permute-start(bf16[1,144,256]{2,1,0:T(8,128)(2,1)S(1)} %get-tuple-element.69), channel_id=1, source_target_pairs={{0,1},{1,0},{2,3},{3,2},{4,5},{5,4},{6,7},{7,6},{8,9},{9,8},{10,11... | collective-permute-start | bytes 221192 | tf_op jit(solution)/shard_map/ppermute | solution.py:79
  153.4 7.0 %collective-permute-start.52 = (bf16[1,144,256]{2,1,0:T(8,128)(2,1)S(1)}, bf16[1,144,256]{2,1,0:T(8,128)(2,1)S(1)}, u32[]{:S(2)}, u32[]{:S(2)}) collective-permute-start(bf16[1,144,256]{2,1,0:T(8,128)(2,1)S(1)} %get-tuple-element.70), channel_id=1, source_target_pairs={{0,2},{2,0},{4,6},{6,4},{8,10},{10,8},{12,14},{14,12},{16,18},{18,... | collective-permute-start | bytes 221192 | tf_op jit(solution)/shard_map/ppermute | solution.py:75
  154.8 6.5 %collective-permute-start.53 = (bf16[1,144,256]{2,1,0:T(8,128)(2,1)S(1)}, bf16[1,144,256]{2,1,0:T(8,128)(2,1)S(1)}, u32[]{:S(2)}, u32[]{:S(2)}) collective-permute-start(bf16[1,144,256]{2,1,0:T(8,128)(2,1)S(1)} %get-tuple-element.71), channel_id=1, source_target_pairs={{0,3},{1,2},{2,1},{3,0},{4,7},{5,6},{6,5},{7,4},{8,11},{9,10},{10,... | collective-permute-start | bytes 221192 | tf_op jit(solution)/shard_map/ppermute | solution.py:84
  (33 other events, 164.9 us)

commit v3 on v2

--- a/solution.py
+++ b/solution.py
@@ -552,10 +552,10 @@
     operands = attended + across + attended_other + across_other
     keep, keep_other = project_out(place, operands, (piece, rest), 1)
     theirs = swap_core(keep_other, seq_size)
-    parts = (keep[:1], keep[1:], theirs[:1], theirs[1:])
-    whole = place_part(table, place, parts, 0, slots, w_out.shape[1], None)
+    own_parts = (keep[:1], keep[1:], theirs[:1], theirs[1:])
+    whole = None
     start = 1
-    for count in (slots - 6, 2, 2, 1):
+    for index, count in enumerate((slots - 6, 2, 2, 1)):
         keep, keep_other, send, send_other = project_out(
             place, operands, out_weights[start : start + count], 2
         )
@@ -566,6 +566,8 @@
             table, place, (keep, got, kept_other, got_other), start, slots,
             w_out.shape[1], whole,
         )
+        if index == 0:
+            whole = place_part(table, place, own_parts, 0, slots, w_out.shape[1], whole)
         start += count
     return whole
 

time: 163 us -> 163 us (level)
  no operation moved by 1% of the time
where the time goes in v3:
time: 163 us
  waiting for transfers between devices  73.2 us (45%)
  Pallas kernels  40.7 us (25%)
  starting transfers between devices  38.1 us (23%)
  local copies, waits for them, and re-layouts  8.08 us (5%)
  other arithmetic  2.11 us (1%)
    ppermute x33, waiting for transfers between devices, pass_on(): return lax.ppermute(value, 'seq', ring_perm(seq_size, turn))  61.6 us
    ppermute x24, starting transfers between devices, swap_core(): return lax.ppermute(value, 'seq', [(s, s ^ 1) for s in range(seq_size)])  19.1 us
    pallas_call x2, Pallas kernels, attend(): pl.pallas_call(functools.partial(attend_kernel, count, offset), out_shape...  12.6 us
    ppermute x33, starting transfers between devices, pass_on(): return lax.ppermute(value, 'seq', ring_perm(seq_size, turn))  8.25 us
    pallas_call x5, Pallas kernels, project(): pl.pallas_call(functools.partial(project_kernel, start, count, group), ou...  8.23 us
    unnamed x26, local copies, waits for them, and re-layouts  7.21 us
    pallas_call x5, Pallas kernels, place_part(): pl.pallas_call(functools.partial(place_kernel, start, slots, width), out_...  6.82 us
    ppermute x7, starting transfers between devices, swap_head(): return lax.ppermute(value, 'head', [(0, 1), (1, 0)])  5.41 us
  transfers between devices with their start and end apart: 68, of which 25 were waited for; matrix products, arithmetic and copies ran while one was open for 0% of the time, Pallas kernels for 21%

profile of v3, /device:TPU:27, one launch (start us, length us, event | category | flops | bytes accessed | tf_op | source)
XLA Modules:
  0.0 162.8 jit_solution(5527466614092331261)
XLA Ops:
  2.9 2.3 %copy-done = bf16[288,8192]{1,0:T(8,128)(2,1)S(1)} copy-done((bf16[288,8192]{1,0:T(8,128)(2,1)S(1)}, bf16[288,8192]{1,0:T(8,128)(2,1)}, u32[]{:S(2)}) %copy-start) | copy-done | bytes 4718616
  5.2 4.8 %norm.1 = (bf16[8,288,512]{2,1,0:T(8,128)(2,1)S(1)}, bf16[8,288,512]{2,1,0:T(8,128)(2,1)}) custom-call(s32[32]{0:T(128)S(1)} %stack.125.table, bf16[288,8192]{1,0:T(8,128)(2,1)S(1)} %copy-done, bf16[1,8192]{1,0:T(2,128)(2,1)S(1)} %reshape.46.gain), custom_call_target="tpu_custom_call" | custom-call | flops 4000000000 | bytes 1000000 | tf_op jit(solution)/shard_map/norm/pallas_call | solution.py:204
  10.0 1.4 copy-done.11
  12.6 1.7 %prep.1.refs_0_ = bf16[512,256]{1,0:T(8,128)(2,1)} custom-call(bf16[512,128]{1,0:T(8,128)(2,1)} %w_key.1, bf16[512,128]{1,0:T(8,128)(2,1)} %w_value.1), custom_call_target="tpu_custom_call" | custom-call | flops 1000000000 | bytes 1000000 | tf_op jit(solution)/shard_map/prep/pallas_call | solution.py:123
  15.5 2.1 %collective-permute-done.4 = bf16[512,512]{1,0:T(8,128)(2,1)} collective-permute-done((bf16[512,512]{1,0:T(8,128)(2,1)}, bf16[512,512]{1,0:T(8,128)(2,1)}, u32[]{:S(2)}, u32[]{:S(2)}) %collective-permute-start.4) | collective-permute-done | bytes 524320 | tf_op jit(solution)/shard_map/ppermute | solution.py:75
  17.8 5.9 %collective-permute-done.10.refs_1_ = bf16[512,256]{1,0:T(8,128)(2,1)S(1)} collective-permute-done((bf16[512,256]{1,0:T(8,128)(2,1)}, bf16[512,256]{1,0:T(8,128)(2,1)S(1)}, u32[]{:S(2)}, u32[]{:S(2)}) %collective-permute-start.10) | collective-permute-done | bytes 262176 | tf_op jit(solution)/shard_map/ppermute | solution.py:88
  23.7 1.2 collective-permute-start.46
  25.4 1.8 %shard_map.91 = (bf16[512,256]{1,0:T(8,128)(2,1)S(1)}, bf16[512,256]{1,0:T(8,128)(2,1)}) custom-call(bf16[512,512]{1,0:T(8,128)(2,1)} %collective-permute-done.1.value.refs_1_), custom_call_target="tpu_custom_call" | custom-call | flops 1000000000 | bytes 1000000 | tf_op jit(solution)/shard_map/pallas_call | solution.py:142
  27.1 5.1 %collective-permute-done.13.refs_3_ = bf16[512,256]{1,0:T(8,128)(2,1)} collective-permute-done((bf16[512,256]{1,0:T(8,128)(2,1)S(1)}, bf16[512,256]{1,0:T(8,128)(2,1)}, u32[]{:S(2)}, u32[]{:S(2)}) %collective-permute-start.13) | collective-permute-done | bytes 262176 | tf_op jit(solution)/shard_map/ppermute | solution.py:88
  32.5 2.6 %collective-permute-done.12.refs_2_ = bf16[512,256]{1,0:T(8,128)(2,1)} collective-permute-done((bf16[512,256]{1,0:T(8,128)(2,1)S(1)}, bf16[512,256]{1,0:T(8,128)(2,1)}, u32[]{:S(2)}, u32[]{:S(2)}) %collective-permute-start.12) | collective-permute-done | bytes 262176 | tf_op jit(solution)/shard_map/ppermute | solution.py:88
  40.9 2.1 %collective-permute-start.54 = (bf16[1024,256]{1,0:T(8,128)(2,1)S(1)}, bf16[1024,256]{1,0:T(8,128)(2,1)S(1)}, u32[]{:S(2)}, u32[]{:S(2)}) collective-permute-start(bf16[1024,256]{1,0:T(8,128)(2,1)S(1)} %get-tuple-element.67.refs_8_), channel_id=1, source_target_pairs={{0,2},{2,0},{4,6},{6,4},{8,10},{10,8},{12,14},{14,12},{16,18},{18,... | collective-permute-start | bytes 1572872 | tf_op jit(solution)/shard_map/ppermute | solution.py:75
  43.9 2.6 %collective-permute-done.36.refs_4_ = bf16[512,256]{1,0:T(8,128)(2,1)} collective-permute-done((bf16[512,256]{1,0:T(8,128)(2,1)}, bf16[512,256]{1,0:T(8,128)(2,1)}, u32[]{:S(2)}, u32[]{:S(2)}) %collective-permute-start.36) | collective-permute-done | bytes 262176 | tf_op jit(solution)/shard_map/ppermute | solution.py:88
  46.9 2.3 %shard_map.98 = (f32[288,256]{1,0:T(8,128)S(1)}, f32[288,256]{1,0:T(8,128)S(1)}) custom-call(bf16[8,288,512]{2,1,0:T(8,128)(2,1)S(1)} %copy-done.12, bf16[8,288,512]{2,1,0:T(8,128)(2,1)S(1)} %collective-permute-done.other, bf16[512,512]{1,0:T(8,128)(2,1)} %refs_0_.3, bf16[512,512]{1,0:T(8,128)(2,1)} %collective-permute-done.1.value.refs_1_, ...), custom_call_target="tpu_custom_call" | custom-call | flops 4000000000 | bytes 1000000 | tf_op jit(solution)/shard_map/pallas_call | solution.py:235
  50.1 1.9 %collective-permute-done.35.refs_0_ = bf16[512,256]{1,0:T(8,128)(2,1)S(1)} collective-permute-done((bf16[512,256]{1,0:T(8,128)(2,1)}, bf16[512,256]{1,0:T(8,128)(2,1)S(1)}, u32[]{:S(2)}, u32[]{:S(2)}) %collective-permute-start.35) | collective-permute-done | bytes 262176 | tf_op jit(solution)/shard_map/ppermute | solution.py:88
  52.3 2.6 %collective-permute-done.17.refs_7_ = bf16[512,256]{1,0:T(8,128)(2,1)S(1)} collective-permute-done((bf16[512,256]{1,0:T(8,128)(2,1)}, bf16[512,256]{1,0:T(8,128)(2,1)S(1)}, u32[]{:S(2)}, u32[]{:S(2)}) %collective-permute-start.17) | collective-permute-done | bytes 262176 | tf_op jit(solution)/shard_map/ppermute | solution.py:88
  55.1 2.5 %collective-permute-done.16.refs_6_ = bf16[512,256]{1,0:T(8,128)(2,1)S(1)} collective-permute-done((bf16[512,256]{1,0:T(8,128)(2,1)}, bf16[512,256]{1,0:T(8,128)(2,1)S(1)}, u32[]{:S(2)}, u32[]{:S(2)}) %collective-permute-start.16) | collective-permute-done | bytes 262176 | tf_op jit(solution)/shard_map/ppermute | solution.py:88
  57.9 2.6 %shard_map.96 = (f32[288,256]{1,0:T(8,128)S(1)}, f32[288,256]{1,0:T(8,128)S(1)}) custom-call(bf16[8,288,512]{2,1,0:T(8,128)(2,1)S(1)} %copy-done.12, bf16[8,288,512]{2,1,0:T(8,128)(2,1)S(1)} %collective-permute-done.other, bf16[512,256]{1,0:T(8,128)(2,1)S(1)} %copy-done.6, bf16[512,256]{1,0:T(8,128)(2,1)S(1)} %collective-permute-done.10.refs_1_, ...), custom_call_target="tpu_custom_call" | custom-call | flops 4000000000 | bytes 1000000 | tf_op jit(solution)/shard_map/pallas_call | solution.py:235
  60.4 5.6 %collective-permute-done.3.refs_0_ = bf16[512,256]{1,0:T(8,128)(2,1)S(1)} collective-permute-done((bf16[512,256]{1,0:T(8,128)(2,1)S(1)}, bf16[512,256]{1,0:T(8,128)(2,1)S(1)}, u32[]{:S(2)}, u32[]{:S(2)}) %collective-permute-start.3) | collective-permute-done | bytes 262176 | tf_op jit(solution)/shard_map/ppermute | solution.py:88
  66.3 2.6 %collective-permute-done.6.refs_4_ = bf16[512,256]{1,0:T(8,128)(2,1)S(1)} collective-permute-done((bf16[512,256]{1,0:T(8,128)(2,1)S(1)}, bf16[512,256]{1,0:T(8,128)(2,1)S(1)}, u32[]{:S(2)}, u32[]{:S(2)}) %collective-permute-start.6) | collective-permute-done | bytes 262176 | tf_op jit(solution)/shard_map/ppermute | solution.py:88
  68.9 2.1 %collective-permute-start.18 = (f32[288,256]{1,0:T(8,128)S(1)}, f32[288,256]{1,0:T(8,128)S(1)}, u32[]{:S(2)}, u32[]{:S(2)}) collective-permute-start(f32[288,256]{1,0:T(8,128)S(1)} %get-tuple-element.59), channel_id=1, source_target_pairs={{0,2},{2,0},{4,6},{6,4},{8,10},{10,8},{12,14},{14,12},{16,18},{18,... | collective-permute-start | bytes 884744 | tf_op jit(solution)/shard_map/ppermute | solution.py:75
  71.0 2.1 %shard_map.93 = (f32[288,256]{1,0:T(8,128)S(1)}, f32[288,256]{1,0:T(8,128)S(1)}) custom-call(bf16[8,288,512]{2,1,0:T(8,128)(2,1)S(1)} %copy-done.12, bf16[8,288,512]{2,1,0:T(8,128)(2,1)S(1)} %collective-permute-done.other, bf16[512,512]{1,0:T(8,128)(2,1)} %refs_0_.3, bf16[512,512]{1,0:T(8,128)(2,1)} %collective-permute-done.1.value.refs_1_, ...), custom_call_target="tpu_custom_call" | custom-call | flops 4000000000 | bytes 1000000 | tf_op jit(solution)/shard_map/pallas_call | solution.py:235
  76.1 2.6 %collective-permute-done.8.refs_2_ = bf16[512,256]{1,0:T(8,128)(2,1)S(1)} collective-permute-done((bf16[512,256]{1,0:T(8,128)(2,1)S(1)}, bf16[512,256]{1,0:T(8,128)(2,1)S(1)}, u32[]{:S(2)}, u32[]{:S(2)}) %collective-permute-start.8) | collective-permute-done | bytes 262176 | tf_op jit(solution)/shard_map/ppermute | solution.py:88
  79.0 9.8 %collective-permute-done.7.refs_1_ = bf16[512,256]{1,0:T(8,128)(2,1)S(1)} collective-permute-done((bf16[512,256]{1,0:T(8,128)(2,1)S(1)}, bf16[512,256]{1,0:T(8,128)(2,1)S(1)}, u32[]{:S(2)}, u32[]{:S(2)}) %collective-permute-start.7) | collective-permute-done | bytes 262176 | tf_op jit(solution)/shard_map/ppermute | solution.py:88
  91.3 4.2 %collective-permute-done.21.refs_2_ = bf16[288,256]{1,0:T(8,128)(2,1)S(1)} collective-permute-done((bf16[288,256]{1,0:T(8,128)(2,1)S(1)}, bf16[288,256]{1,0:T(8,128)(2,1)S(1)}, u32[]{:S(2)}, u32[]{:S(2)}) %collective-permute-start.21) | collective-permute-done | bytes 147488 | tf_op jit(solution)/shard_map/ppermute | solution.py:88
  95.6 2.0 %collective-permute-done.22.refs_3_ = bf16[288,256]{1,0:T(8,128)(2,1)S(1)} collective-permute-done((bf16[288,256]{1,0:T(8,128)(2,1)S(1)}, bf16[288,256]{1,0:T(8,128)(2,1)S(1)}, u32[]{:S(2)}, u32[]{:S(2)}) %collective-permute-start.22) | collective-permute-done | bytes 147488 | tf_op jit(solution)/shard_map/ppermute | solution.py:88
  98.5 1.2 collective-permute-done.23.refs_4_
  99.9 2.0 %collective-permute-done.24.refs_5_ = bf16[288,256]{1,0:T(8,128)(2,1)S(1)} collective-permute-done((bf16[288,256]{1,0:T(8,128)(2,1)S(1)}, bf16[288,256]{1,0:T(8,128)(2,1)S(1)}, u32[]{:S(2)}, u32[]{:S(2)}) %collective-permute-start.24) | collective-permute-done | bytes 147488 | tf_op jit(solution)/shard_map/ppermute | solution.py:88
  102.4 1.5 collective-permute-start.29
  104.4 2.2 %collective-permute-start.32 = (bf16[288,256]{1,0:T(8,128)(2,1)S(1)}, bf16[288,256]{1,0:T(8,128)(2,1)S(1)}, u32[]{:S(2)}, u32[]{:S(2)}) collective-permute-start(bf16[288,256]{1,0:T(8,128)(2,1)S(1)} %collective-permute-done.25.refs_6_), channel_id=1, source_target_pairs={{0,2},{2,0},{4,6},{6,4},{8,10},{10,8},{12,14},{14,12},{16,18},{18,... | collective-permute-start | bytes 442376 | tf_op jit(solution)/shard_map/ppermute | solution.py:75
  106.6 1.6 collective-permute-start.33
  109.2 6.2 %shard_map.101.refs_1_ = bf16[288,256]{1,0:T(8,128)(2,1)S(1)} custom-call(s32[32]{0:T(128)S(1)} %stack.125.table, bf16[128,576]{1,0:T(8,128)(2,1)S(1)} %shard_map.100.query, bf16[288,256]{1,0:T(8,128)(2,1)S(1)} %kv.1.refs_0_, bf16[288,256]{1,0:T(8,128)(2,1)S(1)} %collective-permute-done.19.refs_1_, bf16[288,256]{1,0:T(8,128)(2,1)S(1)} %collective-permute-done.21.refs_2_, ...), custom_call_target="tpu_custom_call" | custom-call | flops 8000000000 | bytes 1000000 | tf_op jit(solution)/shard_map/pallas_call | solution.py:373
  115.4 1.3 collective-permute-start.41
  116.7 6.4 %shard_map.97.refs_0_ = bf16[288,256]{1,0:T(8,128)(2,1)S(1)} custom-call(s32[32]{0:T(128)S(1)} %stack.125.table, bf16[128,576]{1,0:T(8,128)(2,1)S(1)} %shard_map.95.query, bf16[288,256]{1,0:T(8,128)(2,1)S(1)} %kv.1.refs_0_, bf16[288,256]{1,0:T(8,128)(2,1)S(1)} %collective-permute-done.19.refs_1_, bf16[288,256]{1,0:T(8,128)(2,1)S(1)} %collective-permute-done.21.refs_2_, ...), custom_call_target="tpu_custom_call" | custom-call | flops 8000000000 | bytes 1000000 | tf_op jit(solution)/shard_map/pallas_call | solution.py:373
  124.0 4.8 %collective-permute-done.40.refs_2_ = bf16[288,256]{1,0:T(8,128)(2,1)S(1)} collective-permute-done((bf16[288,256]{1,0:T(8,128)(2,1)S(1)}, bf16[288,256]{1,0:T(8,128)(2,1)S(1)}, u32[]{:S(2)}, u32[]{:S(2)}) %collective-permute-start.40) | collective-permute-done | bytes 147488 | tf_op jit(solution)/shard_map/ppermute | solution.py:79
  131.9 1.1 collective-permute-start.67
  134.4 3.2 %collective-permute-done.57.refs_9_ = bf16[1024,256]{1,0:T(8,128)(2,1)S(1)} collective-permute-done((bf16[1024,256]{1,0:T(8,128)(2,1)S(1)}, bf16[1024,256]{1,0:T(8,128)(2,1)S(1)}, u32[]{:S(2)}, u32[]{:S(2)}) %collective-permute-start.57) | collective-permute-done | bytes 524320 | tf_op jit(solution)/shard_map/ppermute | solution.py:88
  139.3 3.9 %collective-permute-done.50.refs_8_ = bf16[1024,256]{1,0:T(8,128)(2,1)S(1)} collective-permute-done((bf16[1024,256]{1,0:T(8,128)(2,1)S(1)}, bf16[1024,256]{1,0:T(8,128)(2,1)S(1)}, u32[]{:S(2)}, u32[]{:S(2)}) %collective-permute-start.50) | collective-permute-done | bytes 524320 | tf_op jit(solution)/shard_map/ppermute | solution.py:88
  143.9 1.3 collective-permute-start.62
  145.2 1.2 collective-permute-start.63
  147.4 1.4 shard_map.107.refs_4_
  148.9 1.2 collective-permute-start.60
  150.1 1.3 shard_map.108.refs_4_
  151.4 1.9 %collective-permute-start.51 = (bf16[1,144,256]{2,1,0:T(8,128)(2,1)S(1)}, bf16[1,144,256]{2,1,0:T(8,128)(2,1)S(1)}, u32[]{:S(2)}, u32[]{:S(2)}) collective-permute-start(bf16[1,144,256]{2,1,0:T(8,128)(2,1)S(1)} %get-tuple-element.69), channel_id=1, source_target_pairs={{0,1},{1,0},{2,3},{3,2},{4,5},{5,4},{6,7},{7,6},{8,9},{9,8},{10,11... | collective-permute-start | bytes 221192 | tf_op jit(solution)/shard_map/ppermute | solution.py:79
  153.3 1.4 shard_map.109.refs_4_
  154.7 1.7 %collective-permute-start.53 = (bf16[1,144,256]{2,1,0:T(8,128)(2,1)S(1)}, bf16[1,144,256]{2,1,0:T(8,128)(2,1)S(1)}, u32[]{:S(2)}, u32[]{:S(2)}) collective-permute-start(bf16[1,144,256]{2,1,0:T(8,128)(2,1)S(1)} %get-tuple-element.71), channel_id=1, source_target_pairs={{0,3},{1,2},{2,1},{3,0},{4,7},{5,6},{6,5},{7,4},{8,11},{9,10},{10,... | collective-permute-start | bytes 221192 | tf_op jit(solution)/shard_map/ppermute | solution.py:84
  156.4 2.6 %collective-permute-done.60.refs_3_ = bf16[2,144,256]{2,1,0:T(8,128)(2,1)S(1)} collective-permute-done((bf16[2,144,256]{2,1,0:T(8,128)(2,1)S(1)}, bf16[2,144,256]{2,1,0:T(8,128)(2,1)S(1)}, u32[]{:S(2)}, u32[]{:S(2)}) %collective-permute-start.60) | collective-permute-done | bytes 147488 | tf_op jit(solution)/shard_map/ppermute | solution.py:84
  159.0 1.4 shard_map.110.refs_4_
  161.4 1.3 shard_map.111
  (150 shorter events, 33.6 us)
Async XLA Ops:
  11.5 35.2 %collective-permute-start = (bf16[8,288,512]{2,1,0:T(8,128)(2,1)}, bf16[8,288,512]{2,1,0:T(8,128)(2,1)S(1)}, u32[]{:S(2)}, u32[]{:S(2)}) collective-permute-start(bf16[8,288,512]{2,1,0:T(8,128)(2,1)} %get-tuple-element.48), channel_id=1, source_target_pairs={{0,2},{2,0},{4,6},{6,4},{8,10},{10,8},{12,14},{14,12},{16,18},{18,... | collective-permute-start | bytes 7077896 | tf_op jit(solution)/shard_map/ppermute | solution.py:75
  12.3 12.9 %collective-permute-start.1 = (bf16[512,512]{1,0:T(8,128)(2,1)}, bf16[512,512]{1,0:T(8,128)(2,1)}, u32[]{:S(2)}, u32[]{:S(2)}) collective-permute-start(bf16[512,512]{1,0:T(8,128)(2,1)} %refs_0_.3), channel_id=1, source_target_pairs={{0,8},{2,6},{8,16},{10,2},{16,24},{18,10},{24,28},{26,18},{28,20},... | collective-permute-start | bytes 1572872 | tf_op jit(solution)/shard_map/ppermute | solution.py:88
  14.3 9.4 %collective-permute-start.10 = (bf16[512,256]{1,0:T(8,128)(2,1)}, bf16[512,256]{1,0:T(8,128)(2,1)S(1)}, u32[]{:S(2)}, u32[]{:S(2)}) collective-permute-start(bf16[512,256]{1,0:T(8,128)(2,1)} %prep.1.refs_0_), channel_id=1, source_target_pairs={{0,8},{2,6},{8,16},{10,2},{16,24},{18,10},{24,28},{26,18},{28,20},... | collective-permute-start | bytes 786440 | tf_op jit(solution)/shard_map/ppermute | solution.py:88
  14.5 10.4 %collective-permute-start.11 = (bf16[512,256]{1,0:T(8,128)(2,1)}, bf16[512,256]{1,0:T(8,128)(2,1)S(1)}, u32[]{:S(2)}, u32[]{:S(2)}) collective-permute-start(bf16[512,256]{1,0:T(8,128)(2,1)} %prep.1.refs_0_), channel_id=1, source_target_pairs={{0,2},{2,0},{4,6},{6,4},{8,10},{10,8},{12,14},{14,12},{16,18},{18,... | collective-permute-start | bytes 786440 | tf_op jit(solution)/shard_map/ppermute | solution.py:75
  17.5 17.8 %collective-permute-start.5 = (bf16[512,512]{1,0:T(8,128)(2,1)}, bf16[512,512]{1,0:T(8,128)(2,1)S(1)}, u32[]{:S(2)}, u32[]{:S(2)}) collective-permute-start(bf16[512,512]{1,0:T(8,128)(2,1)} %collective-permute-done.4), channel_id=1, source_target_pairs={{0,8},{2,6},{8,16},{10,2},{16,24},{18,10},{24,28},{26,18},{28,20},... | collective-permute-start | bytes 1572872 | tf_op jit(solution)/shard_map/ppermute | solution.py:88
  23.7 13.3 %collective-permute-start.46 = (bf16[512,512]{1,0:T(8,128)(2,1)S(1)}, bf16[512,512]{1,0:T(8,128)(2,1)S(1)}, u32[]{:S(2)}, u32[]{:S(2)}) collective-permute-start(bf16[512,512]{1,0:T(8,128)(2,1)S(1)} %copy-done.1), channel_id=1, source_target_pairs={{0,1},{1,0},{2,3},{3,2},{4,5},{5,4},{6,7},{7,6},{8,9},{9,8},{10,11... | collective-permute-start | bytes 1572872 | tf_op jit(solution)/shard_map/ppermute | solution.py:79
  24.9 7.3 %collective-permute-start.13 = (bf16[512,256]{1,0:T(8,128)(2,1)S(1)}, bf16[512,256]{1,0:T(8,128)(2,1)}, u32[]{:S(2)}, u32[]{:S(2)}) collective-permute-start(bf16[512,256]{1,0:T(8,128)(2,1)S(1)} %collective-permute-done.10.refs_1_), channel_id=1, source_target_pairs={{0,8},{2,6},{8,16},{10,2},{16,24},{18,10},{24,28},{26,18},{28,20},... | collective-permute-start | bytes 786440 | tf_op jit(solution)/shard_map/ppermute | solution.py:88
  25.2 9.8 %collective-permute-start.12 = (bf16[512,256]{1,0:T(8,128)(2,1)S(1)}, bf16[512,256]{1,0:T(8,128)(2,1)}, u32[]{:S(2)}, u32[]{:S(2)}) collective-permute-start(bf16[512,256]{1,0:T(8,128)(2,1)S(1)} %collective-permute-done.11), channel_id=1, source_target_pairs={{0,8},{2,6},{8,16},{10,2},{16,24},{18,10},{24,28},{26,18},{28,20},... | collective-permute-start | bytes 786440 | tf_op jit(solution)/shard_map/ppermute | solution.py:88
  32.2 6.9 %collective-permute-start.34 = (bf16[512,256]{1,0:T(8,128)(2,1)}, bf16[512,256]{1,0:T(8,128)(2,1)}, u32[]{:S(2)}, u32[]{:S(2)}) collective-permute-start(bf16[512,256]{1,0:T(8,128)(2,1)} %get-tuple-element.61), channel_id=1, source_target_pairs={{0,8},{2,6},{8,16},{10,2},{16,24},{18,10},{24,28},{26,18},{28,20},... | collective-permute-start | bytes 786440 | tf_op jit(solution)/shard_map/ppermute | solution.py:88
  35.3 8.4 %collective-permute-start.14 = (bf16[512,256]{1,0:T(8,128)(2,1)}, bf16[512,256]{1,0:T(8,128)(2,1)}, u32[]{:S(2)}, u32[]{:S(2)}) collective-permute-start(bf16[512,256]{1,0:T(8,128)(2,1)} %collective-permute-done.12.refs_2_), channel_id=1, source_target_pairs={{0,8},{2,6},{8,16},{10,2},{16,24},{18,10},{24,28},{26,18},{28,20},... | collective-permute-start | bytes 786440 | tf_op jit(solution)/shard_map/ppermute | solution.py:88
  37.8 8.7 %collective-permute-start.36 = (bf16[512,256]{1,0:T(8,128)(2,1)}, bf16[512,256]{1,0:T(8,128)(2,1)}, u32[]{:S(2)}, u32[]{:S(2)}) collective-permute-start(bf16[512,256]{1,0:T(8,128)(2,1)} %get-tuple-element.62), channel_id=1, source_target_pairs={{0,8},{2,6},{8,16},{10,2},{16,24},{18,10},{24,28},{26,18},{28,20},... | collective-permute-start | bytes 786440 | tf_op jit(solution)/shard_map/ppermute | solution.py:88
  40.0 9.3 %collective-permute-start.2 = (bf16[512,256]{1,0:T(8,128)(2,1)S(1)}, bf16[512,256]{1,0:T(8,128)(2,1)S(1)}, u32[]{:S(2)}, u32[]{:S(2)}) collective-permute-start(bf16[512,256]{1,0:T(8,128)(2,1)S(1)} %copy-done.10), channel_id=1, source_target_pairs={{0,8},{2,6},{8,16},{10,2},{16,24},{18,10},{24,28},{26,18},{28,20},... | collective-permute-start | bytes 786440 | tf_op jit(solution)/shard_map/ppermute | solution.py:88
  40.9 32.2 %collective-permute-start.54 = (bf16[1024,256]{1,0:T(8,128)(2,1)S(1)}, bf16[1024,256]{1,0:T(8,128)(2,1)S(1)}, u32[]{:S(2)}, u32[]{:S(2)}) collective-permute-start(bf16[1024,256]{1,0:T(8,128)(2,1)S(1)} %get-tuple-element.67.refs_8_), channel_id=1, source_target_pairs={{0,2},{2,0},{4,6},{6,4},{8,10},{10,8},{12,14},{14,12},{16,18},{18,... | collective-permute-start | bytes 1572872 | tf_op jit(solution)/shard_map/ppermute | solution.py:75
  43.7 8.3 %collective-permute-start.35 = (bf16[512,256]{1,0:T(8,128)(2,1)}, bf16[512,256]{1,0:T(8,128)(2,1)S(1)}, u32[]{:S(2)}, u32[]{:S(2)}) collective-permute-start(bf16[512,256]{1,0:T(8,128)(2,1)} %collective-permute-done.34.refs_3_), channel_id=1, source_target_pairs={{0,8},{2,6},{8,16},{10,2},{16,24},{18,10},{24,28},{26,18},{28,20},... | collective-permute-start | bytes 786440 | tf_op jit(solution)/shard_map/ppermute | solution.py:88
  46.5 8.3 %collective-permute-start.17 = (bf16[512,256]{1,0:T(8,128)(2,1)}, bf16[512,256]{1,0:T(8,128)(2,1)S(1)}, u32[]{:S(2)}, u32[]{:S(2)}) collective-permute-start(bf16[512,256]{1,0:T(8,128)(2,1)} %collective-permute-done.15.refs_5_), channel_id=1, source_target_pairs={{0,8},{2,6},{8,16},{10,2},{16,24},{18,10},{24,28},{26,18},{28,20},... | collective-permute-start | bytes 786440 | tf_op jit(solution)/shard_map/ppermute | solution.py:88
  46.7 10.9 %collective-permute-start.16 = (bf16[512,256]{1,0:T(8,128)(2,1)}, bf16[512,256]{1,0:T(8,128)(2,1)S(1)}, u32[]{:S(2)}, u32[]{:S(2)}) collective-permute-start(bf16[512,256]{1,0:T(8,128)(2,1)} %collective-permute-done.14.refs_4_), channel_id=1, source_target_pairs={{0,8},{2,6},{8,16},{10,2},{16,24},{18,10},{24,28},{26,18},{28,20},... | collective-permute-start | bytes 786440 | tf_op jit(solution)/shard_map/ppermute | solution.py:88
  49.3 24.5 %collective-permute-start.47 = (bf16[1024,256]{1,0:T(8,128)(2,1)S(1)}, bf16[1024,256]{1,0:T(8,128)(2,1)S(1)}, u32[]{:S(2)}, u32[]{:S(2)}) collective-permute-start(bf16[1024,256]{1,0:T(8,128)(2,1)S(1)} %get-tuple-element.67.refs_8_), channel_id=1, source_target_pairs={{0,8},{2,6},{8,16},{10,2},{16,24},{18,10},{24,28},{26,18},{28,20},... | collective-permute-start | bytes 1572872 | tf_op jit(solution)/shard_map/ppermute | solution.py:88
  52.0 14.0 %collective-permute-start.3 = (bf16[512,256]{1,0:T(8,128)(2,1)S(1)}, bf16[512,256]{1,0:T(8,128)(2,1)S(1)}, u32[]{:S(2)}, u32[]{:S(2)}) collective-permute-start(bf16[512,256]{1,0:T(8,128)(2,1)S(1)} %collective-permute-done.2.refs_3_), channel_id=1, source_target_pairs={{0,8},{2,6},{8,16},{10,2},{16,24},{18,10},{24,28},{26,18},{28,20},... | collective-permute-start | bytes 786440 | tf_op jit(solution)/shard_map/ppermute | solution.py:88
  54.8 14.0 %collective-permute-start.6 = (bf16[512,256]{1,0:T(8,128)(2,1)S(1)}, bf16[512,256]{1,0:T(8,128)(2,1)S(1)}, u32[]{:S(2)}, u32[]{:S(2)}) collective-permute-start(bf16[512,256]{1,0:T(8,128)(2,1)S(1)} %copy-done.8), channel_id=1, source_target_pairs={{0,8},{2,6},{8,16},{10,2},{16,24},{18,10},{24,28},{26,18},{28,20},... | collective-permute-start | bytes 786440 | tf_op jit(solution)/shard_map/ppermute | solution.py:88
  57.6 16.7 %collective-permute-start.38 = (bf16[512,256]{1,0:T(8,128)(2,1)S(1)}, bf16[512,256]{1,0:T(8,128)(2,1)S(1)}, u32[]{:S(2)}, u32[]{:S(2)}) collective-permute-start(bf16[512,256]{1,0:T(8,128)(2,1)S(1)} %collective-permute-done.35.refs_0_), channel_id=1, source_target_pairs={{0,8},{2,6},{8,16},{10,2},{16,24},{18,10},{24,28},{26,18},{28,20},... | collective-permute-start | bytes 786440 | tf_op jit(solution)/shard_map/ppermute | solution.py:88
  66.0 8.7 %collective-permute-start.37 = (bf16[512,256]{1,0:T(8,128)(2,1)}, bf16[512,256]{1,0:T(8,128)(2,1)S(1)}, u32[]{:S(2)}, u32[]{:S(2)}) collective-permute-start(bf16[512,256]{1,0:T(8,128)(2,1)} %collective-permute-done.36.refs_4_), channel_id=1, source_target_pairs={{0,8},{2,6},{8,16},{10,2},{16,24},{18,10},{24,28},{26,18},{28,20},... | collective-permute-start | bytes 786440 | tf_op jit(solution)/shard_map/ppermute | solution.py:88
  73.4 17.1 %collective-permute-start.55 = (bf16[1024,256]{1,0:T(8,128)(2,1)S(1)}, bf16[1024,256]{1,0:T(8,128)(2,1)S(1)}, u32[]{:S(2)}, u32[]{:S(2)}) collective-permute-start(bf16[1024,256]{1,0:T(8,128)(2,1)S(1)} %collective-permute-done.54), channel_id=1, source_target_pairs={{0,8},{2,6},{8,16},{10,2},{16,24},{18,10},{24,28},{26,18},{28,20},... | collective-permute-start | bytes 1572872 | tf_op jit(solution)/shard_map/ppermute | solution.py:88
  73.8 14.9 %collective-permute-start.7 = (bf16[512,256]{1,0:T(8,128)(2,1)S(1)}, bf16[512,256]{1,0:T(8,128)(2,1)S(1)}, u32[]{:S(2)}, u32[]{:S(2)}) collective-permute-start(bf16[512,256]{1,0:T(8,128)(2,1)S(1)} %collective-permute-done.6.refs_4_), channel_id=1, source_target_pairs={{0,8},{2,6},{8,16},{10,2},{16,24},{18,10},{24,28},{26,18},{28,20},... | collective-permute-start | bytes 786440 | tf_op jit(solution)/shard_map/ppermute | solution.py:88
  74.4 15.2 %collective-permute-start.20 = (bf16[288,256]{1,0:T(8,128)(2,1)S(1)}, bf16[288,256]{1,0:T(8,128)(2,1)S(1)}, u32[]{:S(2)}, u32[]{:S(2)}) collective-permute-start(bf16[288,256]{1,0:T(8,128)(2,1)S(1)} %kv.1.refs_0_), channel_id=1, source_target_pairs={{0,2},{2,0},{4,6},{6,4},{8,10},{10,8},{12,14},{14,12},{16,18},{18,... | collective-permute-start | bytes 442376 | tf_op jit(solution)/shard_map/ppermute | solution.py:75
  74.8 15.0 %collective-permute-start.19 = (bf16[288,256]{1,0:T(8,128)(2,1)S(1)}, bf16[288,256]{1,0:T(8,128)(2,1)S(1)}, u32[]{:S(2)}, u32[]{:S(2)}) collective-permute-start(bf16[288,256]{1,0:T(8,128)(2,1)S(1)} %kv.1.refs_0_), channel_id=1, source_target_pairs={{0,4},{2,10},{8,0},{10,18},{16,8},{18,26},{24,16},{26,30},{28,24},... | collective-permute-start | bytes 442376 | tf_op jit(solution)/shard_map/ppermute | solution.py:88
  78.7 19.1 %collective-permute-start.48 = (bf16[1024,256]{1,0:T(8,128)(2,1)S(1)}, bf16[1024,256]{1,0:T(8,128)(2,1)S(1)}, u32[]{:S(2)}, u32[]{:S(2)}) collective-permute-start(bf16[1024,256]{1,0:T(8,128)(2,1)S(1)} %collective-permute-done.47.refs_8_), channel_id=1, source_target_pairs={{0,8},{2,6},{8,16},{10,2},{16,24},{18,10},{24,28},{26,18},{28,20},... | collective-permute-start | bytes 1572872 | tf_op jit(solution)/shard_map/ppermute | solution.py:88
  88.7 9.7 %collective-permute-start.39 = (f32[288,256]{1,0:T(8,128)S(1)}, f32[288,256]{1,0:T(8,128)S(1)}, u32[]{:S(2)}, u32[]{:S(2)}) collective-permute-start(f32[288,256]{1,0:T(8,128)S(1)} %get-tuple-element.66), channel_id=1, source_target_pairs={{0,2},{2,0},{4,6},{6,4},{8,10},{10,8},{12,14},{14,12},{16,18},{18,... | collective-permute-start | bytes 884744 | tf_op jit(solution)/shard_map/ppermute | solution.py:75
  89.7 7.9 %collective-permute-start.22 = (bf16[288,256]{1,0:T(8,128)(2,1)S(1)}, bf16[288,256]{1,0:T(8,128)(2,1)S(1)}, u32[]{:S(2)}, u32[]{:S(2)}) collective-permute-start(bf16[288,256]{1,0:T(8,128)(2,1)S(1)} %collective-permute-done.19.refs_1_), channel_id=1, source_target_pairs={{0,4},{2,10},{8,0},{10,18},{16,8},{18,26},{24,16},{26,30},{28,24},... | collective-permute-start | bytes 442376 | tf_op jit(solution)/shard_map/ppermute | solution.py:88
  90.5 11.8 %collective-permute-start.9 = (f32[288,256]{1,0:T(8,128)S(1)}, f32[288,256]{1,0:T(8,128)S(1)}, u32[]{:S(2)}, u32[]{:S(2)}) collective-permute-start(f32[288,256]{1,0:T(8,128)S(1)} %get-tuple-element.54), channel_id=1, source_target_pairs={{0,2},{2,0},{4,6},{6,4},{8,10},{10,8},{12,14},{14,12},{16,18},{18,... | collective-permute-start | bytes 884744 | tf_op jit(solution)/shard_map/ppermute | solution.py:75
  97.8 6.1 %collective-permute-start.27 = (bf16[288,256]{1,0:T(8,128)(2,1)S(1)}, bf16[288,256]{1,0:T(8,128)(2,1)S(1)}, u32[]{:S(2)}, u32[]{:S(2)}) collective-permute-start(bf16[288,256]{1,0:T(8,128)(2,1)S(1)} %collective-permute-done.19.refs_1_), channel_id=1, source_target_pairs={{0,2},{2,0},{4,6},{6,4},{8,10},{10,8},{12,14},{14,12},{16,18},{18,... | collective-permute-start | bytes 442376 | tf_op jit(solution)/shard_map/ppermute | solution.py:75
  102.4 6.0 %collective-permute-start.29 = (bf16[288,256]{1,0:T(8,128)(2,1)S(1)}, bf16[288,256]{1,0:T(8,128)(2,1)S(1)}, u32[]{:S(2)}, u32[]{:S(2)}) collective-permute-start(bf16[288,256]{1,0:T(8,128)(2,1)S(1)} %collective-permute-done.22.refs_3_), channel_id=1, source_target_pairs={{0,2},{2,0},{4,6},{6,4},{8,10},{10,8},{12,14},{14,12},{16,18},{18,... | collective-permute-start | bytes 442376 | tf_op jit(solution)/shard_map/ppermute | solution.py:75
  108.4 15.0 %collective-permute-start.56 = (bf16[1024,256]{1,0:T(8,128)(2,1)S(1)}, bf16[1024,256]{1,0:T(8,128)(2,1)S(1)}, u32[]{:S(2)}, u32[]{:S(2)}) collective-permute-start(bf16[1024,256]{1,0:T(8,128)(2,1)S(1)} %collective-permute-done.55.refs_9_), channel_id=1, source_target_pairs={{0,8},{2,6},{8,16},{10,2},{16,24},{18,10},{24,28},{26,18},{28,20},... | collective-permute-start | bytes 1572872 | tf_op jit(solution)/shard_map/ppermute | solution.py:88
  108.7 20.5 %collective-permute-start.49 = (bf16[1024,256]{1,0:T(8,128)(2,1)S(1)}, bf16[1024,256]{1,0:T(8,128)(2,1)S(1)}, u32[]{:S(2)}, u32[]{:S(2)}) collective-permute-start(bf16[1024,256]{1,0:T(8,128)(2,1)S(1)} %collective-permute-done.48.refs_8_), channel_id=1, source_target_pairs={{0,8},{2,6},{8,16},{10,2},{16,24},{18,10},{24,28},{26,18},{28,20},... | collective-permute-start | bytes 1572872 | tf_op jit(solution)/shard_map/ppermute | solution.py:88
  115.4 8.5 %collective-permute-start.41 = (bf16[288,256]{1,0:T(8,128)(2,1)S(1)}, bf16[288,256]{1,0:T(8,128)(2,1)S(1)}, u32[]{:S(2)}, u32[]{:S(2)}) collective-permute-start(bf16[288,256]{1,0:T(8,128)(2,1)S(1)} %shard_map.101.refs_1_), channel_id=1, source_target_pairs={{0,1},{1,0},{2,3},{3,2},{4,5},{5,4},{6,7},{7,6},{8,9},{9,8},{10,11... | collective-permute-start | bytes 442376 | tf_op jit(solution)/shard_map/ppermute | solution.py:79
  129.2 8.3 %collective-permute-start.57 = (bf16[1024,256]{1,0:T(8,128)(2,1)S(1)}, bf16[1024,256]{1,0:T(8,128)(2,1)S(1)}, u32[]{:S(2)}, u32[]{:S(2)}) collective-permute-start(bf16[1024,256]{1,0:T(8,128)(2,1)S(1)} %collective-permute-done.56.refs_9_), channel_id=1, source_target_pairs={{0,8},{2,6},{8,16},{10,2},{16,24},{18,10},{24,28},{26,18},{28,20},... | collective-permute-start | bytes 1572872 | tf_op jit(solution)/shard_map/ppermute | solution.py:88
  129.2 13.9 %collective-permute-start.50 = (bf16[1024,256]{1,0:T(8,128)(2,1)S(1)}, bf16[1024,256]{1,0:T(8,128)(2,1)S(1)}, u32[]{:S(2)}, u32[]{:S(2)}) collective-permute-start(bf16[1024,256]{1,0:T(8,128)(2,1)S(1)} %collective-permute-done.49.refs_8_), channel_id=1, source_target_pairs={{0,8},{2,6},{8,16},{10,2},{16,24},{18,10},{24,28},{26,18},{28,20},... | collective-permute-start | bytes 1572872 | tf_op jit(solution)/shard_map/ppermute | solution.py:88
  131.0 14.2 %collective-permute-start.65 = (bf16[2,144,256]{2,1,0:T(8,128)(2,1)S(1)}, bf16[2,144,256]{2,1,0:T(8,128)(2,1)S(1)}, u32[]{:S(2)}, u32[]{:S(2)}) collective-permute-start(bf16[2,144,256]{2,1,0:T(8,128)(2,1)S(1)} %get-tuple-element.84), channel_id=1, source_target_pairs={{0,1},{1,0},{2,3},{3,2},{4,5},{5,4},{6,7},{7,6},{8,9},{9,8},{10,11... | collective-permute-start | bytes 442376 | tf_op jit(solution)/shard_map/ppermute | solution.py:79
  131.3 15.2 %collective-permute-start.66 = (bf16[2,144,256]{2,1,0:T(8,128)(2,1)S(1)}, bf16[2,144,256]{2,1,0:T(8,128)(2,1)S(1)}, u32[]{:S(2)}, u32[]{:S(2)}) collective-permute-start(bf16[2,144,256]{2,1,0:T(8,128)(2,1)S(1)} %get-tuple-element.85), channel_id=1, source_target_pairs={{0,2},{2,0},{4,6},{6,4},{8,10},{10,8},{12,14},{14,12},{16,18},{18,... | collective-permute-start | bytes 442376 | tf_op jit(solution)/shard_map/ppermute | solution.py:75
  131.9 14.7 %collective-permute-start.67 = (bf16[2,144,256]{2,1,0:T(8,128)(2,1)S(1)}, bf16[2,144,256]{2,1,0:T(8,128)(2,1)S(1)}, u32[]{:S(2)}, u32[]{:S(2)}) collective-permute-start(bf16[2,144,256]{2,1,0:T(8,128)(2,1)S(1)} %get-tuple-element.86), channel_id=1, source_target_pairs={{0,3},{1,2},{2,1},{3,0},{4,7},{5,6},{6,5},{7,4},{8,11},{9,10},{10,... | collective-permute-start | bytes 442376 | tf_op jit(solution)/shard_map/ppermute | solution.py:84
  137.5 6.3 %collective-permute-start.64 = (bf16[2,144,256]{2,1,0:T(8,128)(2,1)S(1)}, bf16[2,144,256]{2,1,0:T(8,128)(2,1)S(1)}, u32[]{:S(2)}, u32[]{:S(2)}) collective-permute-start(bf16[2,144,256]{2,1,0:T(8,128)(2,1)S(1)} %get-tuple-element.82), channel_id=1, source_target_pairs={{0,2},{2,0},{4,6},{6,4},{8,10},{10,8},{12,14},{14,12},{16,18},{18,... | collective-permute-start | bytes 442376 | tf_op jit(solution)/shard_map/ppermute | solution.py:75
  143.9 7.5 %collective-permute-start.62 = (bf16[2,144,256]{2,1,0:T(8,128)(2,1)S(1)}, bf16[2,144,256]{2,1,0:T(8,128)(2,1)S(1)}, u32[]{:S(2)}, u32[]{:S(2)}) collective-permute-start(bf16[2,144,256]{2,1,0:T(8,128)(2,1)S(1)} %get-tuple-element.78), channel_id=1, source_target_pairs={{0,2},{2,0},{4,6},{6,4},{8,10},{10,8},{12,14},{14,12},{16,18},{18,... | collective-permute-start | bytes 442376 | tf_op jit(solution)/shard_map/ppermute | solution.py:75
  145.2 8.0 %collective-permute-start.63 = (bf16[2,144,256]{2,1,0:T(8,128)(2,1)S(1)}, bf16[2,144,256]{2,1,0:T(8,128)(2,1)S(1)}, u32[]{:S(2)}, u32[]{:S(2)}) collective-permute-start(bf16[2,144,256]{2,1,0:T(8,128)(2,1)S(1)} %get-tuple-element.79), channel_id=1, source_target_pairs={{0,3},{1,2},{2,1},{3,0},{4,7},{5,6},{6,5},{7,4},{8,11},{9,10},{10,... | collective-permute-start | bytes 442376 | tf_op jit(solution)/shard_map/ppermute | solution.py:84
  146.4 8.2 %collective-permute-start.58 = (bf16[2,144,256]{2,1,0:T(8,128)(2,1)S(1)}, bf16[2,144,256]{2,1,0:T(8,128)(2,1)S(1)}, u32[]{:S(2)}, u32[]{:S(2)}) collective-permute-start(bf16[2,144,256]{2,1,0:T(8,128)(2,1)S(1)} %get-tuple-element.73), channel_id=1, source_target_pairs={{0,1},{1,0},{2,3},{3,2},{4,5},{5,4},{6,7},{7,6},{8,9},{9,8},{10,11... | collective-permute-start | bytes 442376 | tf_op jit(solution)/shard_map/ppermute | solution.py:79
  146.7 9.8 %collective-permute-start.59 = (bf16[2,144,256]{2,1,0:T(8,128)(2,1)S(1)}, bf16[2,144,256]{2,1,0:T(8,128)(2,1)S(1)}, u32[]{:S(2)}, u32[]{:S(2)}) collective-permute-start(bf16[2,144,256]{2,1,0:T(8,128)(2,1)S(1)} %get-tuple-element.74), channel_id=1, source_target_pairs={{0,2},{2,0},{4,6},{6,4},{8,10},{10,8},{12,14},{14,12},{16,18},{18,... | collective-permute-start | bytes 442376 | tf_op jit(solution)/shard_map/ppermute | solution.py:75
  148.9 10.1 %collective-permute-start.60 = (bf16[2,144,256]{2,1,0:T(8,128)(2,1)S(1)}, bf16[2,144,256]{2,1,0:T(8,128)(2,1)S(1)}, u32[]{:S(2)}, u32[]{:S(2)}) collective-permute-start(bf16[2,144,256]{2,1,0:T(8,128)(2,1)S(1)} %get-tuple-element.75), channel_id=1, source_target_pairs={{0,3},{1,2},{2,1},{3,0},{4,7},{5,6},{6,5},{7,4},{8,11},{9,10},{10,... | collective-permute-start | bytes 442376 | tf_op jit(solution)/shard_map/ppermute | solution.py:84
  151.4 9.0 %collective-permute-start.51 = (bf16[1,144,256]{2,1,0:T(8,128)(2,1)S(1)}, bf16[1,144,256]{2,1,0:T(8,128)(2,1)S(1)}, u32[]{:S(2)}, u32[]{:S(2)}) collective-permute-start(bf16[1,144,256]{2,1,0:T(8,128)(2,1)S(1)} %get-tuple-element.69), channel_id=1, source_target_pairs={{0,1},{1,0},{2,3},{3,2},{4,5},{5,4},{6,7},{7,6},{8,9},{9,8},{10,11... | collective-permute-start | bytes 221192 | tf_op jit(solution)/shard_map/ppermute | solution.py:79
  153.3 7.2 %collective-permute-start.52 = (bf16[1,144,256]{2,1,0:T(8,128)(2,1)S(1)}, bf16[1,144,256]{2,1,0:T(8,128)(2,1)S(1)}, u32[]{:S(2)}, u32[]{:S(2)}) collective-permute-start(bf16[1,144,256]{2,1,0:T(8,128)(2,1)S(1)} %get-tuple-element.70), channel_id=1, source_target_pairs={{0,2},{2,0},{4,6},{6,4},{8,10},{10,8},{12,14},{14,12},{16,18},{18,... | collective-permute-start | bytes 221192 | tf_op jit(solution)/shard_map/ppermute | solution.py:75
  154.7 6.7 %collective-permute-start.53 = (bf16[1,144,256]{2,1,0:T(8,128)(2,1)S(1)}, bf16[1,144,256]{2,1,0:T(8,128)(2,1)S(1)}, u32[]{:S(2)}, u32[]{:S(2)}) collective-permute-start(bf16[1,144,256]{2,1,0:T(8,128)(2,1)S(1)} %get-tuple-element.71), channel_id=1, source_target_pairs={{0,3},{1,2},{2,1},{3,0},{4,7},{5,6},{6,5},{7,4},{8,11},{9,10},{10,... | collective-permute-start | bytes 221192 | tf_op jit(solution)/shard_map/ppermute | solution.py:84
  (33 other events, 164.9 us)
